TPU v7x, 8 devices: a whole 2x2x1 slice. The times are simulated.
8 devices in a mesh: fsdp: 8 (over z, y, x, core).
Axes of the slice: x: 2, y: 2, z: 1, core: 2. Of those that a mesh axis runs over, the one named last changes fastest.
Arguments:
- hidden: bfloat16 [24, 256, 2048], P('fsdp')
- grad_out: bfloat16 [24, 256, 2048], P('fsdp')
- positions: int32 [24, 256], P('fsdp')
- norm1_gain: bfloat16 [2048], P('fsdp')
- norm2_gain: bfloat16 [2048], P('fsdp')
- q_norm_gain: bfloat16 [128], replicated
- k_norm_gain: bfloat16 [128], replicated
- w_q: bfloat16 [2048, 2048], P('fsdp')
- w_k: bfloat16 [2048, 1024], P('fsdp')
- w_v: bfloat16 [2048, 1024], P('fsdp')
- w_o: bfloat16 [2048, 2048], P('fsdp')
- w_gate: bfloat16 [2048, 6144], P('fsdp')
- w_up: bfloat16 [2048, 6144], P('fsdp')
- w_down: bfloat16 [6144, 2048], P('fsdp')
Outputs:
- output 1: bfloat16 [24, 256, 2048], P('fsdp')
- output 2: bfloat16 [24, 256, 2048], P('fsdp')
- output 3: float32 [2048], P('fsdp')
- output 4: float32 [2048], P('fsdp')
- output 5: float32 [128], replicated
- output 6: float32 [128], replicated
- output 7: float32 [2048, 2048], P('fsdp')
- output 8: float32 [2048, 1024], P('fsdp')
- output 9: float32 [2048, 1024], P('fsdp')
- output 10: float32 [2048, 2048], P('fsdp')
- output 11: float32 [2048, 6144], P('fsdp')
- output 12: float32 [2048, 6144], P('fsdp')
- output 13: float32 [6144, 2048], P('fsdp')
All inputs are finite; a program needn't handle non-finite values.
Results may differ from a plain program's by a relative error of at most 0.02.
Values are sent between devices in bfloat16 or wider.
A program may use at most 1 GiB of HBM per device.

v0:
```python
import jax
import jax.numpy as jnp
from jax import lax
from jax.sharding import PartitionSpec as P

RMS_EPS = 1e-6
ROPE_THETA = 1000000.0


def rms_scale(tensor):
    return lax.rsqrt(jnp.mean(tensor * tensor, axis=-1, keepdims=True) + RMS_EPS)


def norm_backward(d_unit, unit_val, scale_val):
    return scale_val * (d_unit - unit_val * jnp.mean(d_unit * unit_val, axis=-1, keepdims=True))


def rotate_half(tensor):
    half_dim = tensor.shape[-1] // 2
    return jnp.concatenate([-tensor[..., half_dim:], tensor[..., :half_dim]], axis=-1)


def matmul(left_op, right_op):
    return jnp.dot(left_op, right_op, preferred_element_type=jnp.float32)


def matmul_tn(left_op, right_op):
    return lax.dot_general(left_op, right_op, (((0,), (0,)), ((), ())), preferred_element_type=jnp.float32)


def matmul_nt(left_op, right_op):
    return lax.dot_general(left_op, right_op, (((1,), (1,)), ((), ())), preferred_element_type=jnp.float32)


def rope_tables(positions, head_dim):
    inv_freq = ROPE_THETA ** (-2.0 * jnp.arange(head_dim // 2, dtype=jnp.float32) / head_dim)
    rope_angle = positions.reshape(-1, 1).astype(jnp.float32) * inv_freq
    cos_half = jnp.cos(rope_angle)
    sin_half = jnp.sin(rope_angle)
    cos_t = jnp.concatenate([cos_half, cos_half], axis=-1)[:, None, :]
    sin_t = jnp.concatenate([sin_half, sin_half], axis=-1)[:, None, :]
    return cos_t, sin_t


def head_norm_rope(projected, num_heads, head_dim, gain_vec, cos_t, sin_t):
    heads_float = projected.reshape(projected.shape[0], num_heads, head_dim).astype(jnp.float32)
    head_scale = rms_scale(heads_float)
    head_unit = heads_float * head_scale
    scaled = head_unit * gain_vec.astype(jnp.float32)
    rotated = (scaled * cos_t + rotate_half(scaled) * sin_t).astype(jnp.bfloat16)
    return rotated, head_unit, head_scale


def head_norm_rope_backward(d_rotated, head_unit, head_scale, gain_vec, cos_t, sin_t):
    d_scaled = d_rotated * cos_t - rotate_half(d_rotated * sin_t)
    d_gain = jnp.sum(d_scaled * head_unit, axis=(0, 1))
    d_projected = norm_backward(d_scaled * gain_vec.astype(jnp.float32), head_unit, head_scale)
    return d_projected.reshape(d_projected.shape[0], -1).astype(jnp.bfloat16), d_gain


def forward_local(hidden, positions, weights):
    norm1_gain, norm2_gain, q_norm_gain, k_norm_gain, w_q, w_k, w_v, w_o, w_gate, w_up, w_down = weights
    batch_local, seq_len, model_width = hidden.shape
    head_dim = q_norm_gain.shape[0]
    num_heads = w_q.shape[1] // head_dim
    kv_heads = w_k.shape[1] // head_dim
    tokens = batch_local * seq_len
    x_float = hidden.reshape(tokens, model_width).astype(jnp.float32)
    x_scale = rms_scale(x_float)
    x_unit = x_float * x_scale
    normed = (x_unit * norm1_gain.astype(jnp.float32)).astype(jnp.bfloat16)
    q_proj = matmul(normed, w_q).astype(jnp.bfloat16)
    k_proj = matmul(normed, w_k).astype(jnp.bfloat16)
    v_proj = matmul(normed, w_v).astype(jnp.bfloat16)
    cos_t, sin_t = rope_tables(positions, head_dim)
    q_rot, q_unit, q_scale = head_norm_rope(q_proj, num_heads, head_dim, q_norm_gain, cos_t, sin_t)
    k_rot, k_unit, k_scale = head_norm_rope(k_proj, kv_heads, head_dim, k_norm_gain, cos_t, sin_t)
    q_grouped = q_rot.reshape(batch_local, seq_len, kv_heads, num_heads // kv_heads, head_dim)
    k_seq = k_rot.reshape(batch_local, seq_len, kv_heads, head_dim)
    v_seq = v_proj.reshape(batch_local, seq_len, kv_heads, head_dim)
    scores = jnp.einsum("bskgd,btkd->bksgt", q_grouped, k_seq, preferred_element_type=jnp.float32) * (head_dim ** -0.5)
    causal = (jnp.arange(seq_len)[:, None] >= jnp.arange(seq_len)[None, :])[:, None, :]
    attn_probs = jax.nn.softmax(jnp.where(causal, scores, -1e30), axis=-1)
    attn_ctx = jnp.einsum("bksgt,btkd->bskgd", attn_probs.astype(jnp.bfloat16), v_seq, preferred_element_type=jnp.float32).astype(jnp.bfloat16).reshape(tokens, num_heads * head_dim)
    attn_out = matmul(attn_ctx, w_o).astype(jnp.bfloat16)
    resid_float = (x_float + attn_out.astype(jnp.float32)).astype(jnp.bfloat16).astype(jnp.float32)
    r_scale = rms_scale(resid_float)
    r_unit = resid_float * r_scale
    mlp_in = (r_unit * norm2_gain.astype(jnp.float32)).astype(jnp.bfloat16)
    gate_proj = matmul(mlp_in, w_gate).astype(jnp.bfloat16)
    up_proj = matmul(mlp_in, w_up).astype(jnp.bfloat16)
    mlp_act = (jax.nn.silu(gate_proj.astype(jnp.float32)) * up_proj.astype(jnp.float32)).astype(jnp.bfloat16)
    down_proj = matmul(mlp_act, w_down).astype(jnp.bfloat16)
    layer_out = (resid_float + down_proj.astype(jnp.float32)).astype(jnp.bfloat16).reshape(batch_local, seq_len, model_width)
    saved_acts = {"x_unit": x_unit, "x_scale": x_scale, "normed": normed, "cos_t": cos_t, "sin_t": sin_t, "q_unit": q_unit, "q_scale": q_scale, "k_unit": k_unit, "k_scale": k_scale, "q_grouped": q_grouped, "k_seq": k_seq, "v_seq": v_seq, "attn_probs": attn_probs, "attn_ctx": attn_ctx, "r_unit": r_unit, "r_scale": r_scale, "mlp_in": mlp_in, "gate_proj": gate_proj, "up_proj": up_proj, "mlp_act": mlp_act}
    return layer_out, saved_acts


def backward_local(grad_out, saved_acts, weights):
    norm1_gain, norm2_gain, q_norm_gain, k_norm_gain, w_q, w_k, w_v, w_o, w_gate, w_up, w_down = weights
    batch_local, seq_len, model_width = grad_out.shape
    tokens = batch_local * seq_len
    q_grouped = saved_acts["q_grouped"]
    kv_heads = q_grouped.shape[2]
    kv_group = q_grouped.shape[3]
    head_dim = q_grouped.shape[4]
    num_heads = kv_heads * kv_group
    dy_flat = grad_out.reshape(tokens, model_width)
    grad_down = matmul_tn(saved_acts["mlp_act"], dy_flat)
    d_mlp_act = matmul_nt(dy_flat, w_down)
    gate_float = saved_acts["gate_proj"].astype(jnp.float32)
    gate_sig = jax.nn.sigmoid(gate_float)
    d_up_proj = (d_mlp_act * gate_float * gate_sig).astype(jnp.bfloat16)
    d_gate_proj = (d_mlp_act * saved_acts["up_proj"].astype(jnp.float32) * gate_sig * (1.0 + gate_float * (1.0 - gate_sig))).astype(jnp.bfloat16)
    grad_gate = matmul_tn(saved_acts["mlp_in"], d_gate_proj)
    grad_up = matmul_tn(saved_acts["mlp_in"], d_up_proj)
    d_mlp_in = matmul_nt(d_gate_proj, w_gate) + matmul_nt(d_up_proj, w_up)
    grad_norm2 = jnp.sum(d_mlp_in * saved_acts["r_unit"], axis=0)
    d_resid = dy_flat.astype(jnp.float32) + norm_backward(d_mlp_in * norm2_gain.astype(jnp.float32), saved_acts["r_unit"], saved_acts["r_scale"])
    d_resid_bf = d_resid.astype(jnp.bfloat16)
    grad_wo = matmul_tn(saved_acts["attn_ctx"], d_resid_bf)
    d_attn_ctx = matmul_nt(d_resid_bf, w_o).astype(jnp.bfloat16).reshape(batch_local, seq_len, kv_heads, kv_group, head_dim)
    attn_probs = saved_acts["attn_probs"]
    d_value = jnp.einsum("bksgt,bskgd->btkd", attn_probs.astype(jnp.bfloat16), d_attn_ctx, preferred_element_type=jnp.float32).astype(jnp.bfloat16).reshape(tokens, kv_heads * head_dim)
    d_probs = jnp.einsum("bskgd,btkd->bksgt", d_attn_ctx, saved_acts["v_seq"], preferred_element_type=jnp.float32)
    d_scores = attn_probs * (d_probs - jnp.sum(attn_probs * d_probs, axis=-1, keepdims=True))
    d_scores = (d_scores * (head_dim ** -0.5)).astype(jnp.bfloat16)
    d_q_rot = jnp.einsum("bksgt,btkd->bskgd", d_scores, saved_acts["k_seq"], preferred_element_type=jnp.float32).reshape(tokens, num_heads, head_dim)
    d_k_rot = jnp.einsum("bksgt,bskgd->btkd", d_scores, q_grouped, preferred_element_type=jnp.float32).reshape(tokens, kv_heads, head_dim)
    d_query, grad_qgain = head_norm_rope_backward(d_q_rot, saved_acts["q_unit"], saved_acts["q_scale"], q_norm_gain, saved_acts["cos_t"], saved_acts["sin_t"])
    d_key, grad_kgain = head_norm_rope_backward(d_k_rot, saved_acts["k_unit"], saved_acts["k_scale"], k_norm_gain, saved_acts["cos_t"], saved_acts["sin_t"])
    normed = saved_acts["normed"]
    grad_wq = matmul_tn(normed, d_query)
    grad_wk = matmul_tn(normed, d_key)
    grad_wv = matmul_tn(normed, d_value)
    d_normed = matmul_nt(d_query, w_q) + matmul_nt(d_key, w_k) + matmul_nt(d_value, w_v)
    grad_norm1 = jnp.sum(d_normed * saved_acts["x_unit"], axis=0)
    d_hidden = (d_resid + norm_backward(d_normed * norm1_gain.astype(jnp.float32), saved_acts["x_unit"], saved_acts["x_scale"])).astype(jnp.bfloat16)
    local_grads = (grad_norm1, grad_norm2, grad_qgain, grad_kgain, grad_wq, grad_wk, grad_wv, grad_wo, grad_gate, grad_up, grad_down)
    return d_hidden.reshape(batch_local, seq_len, model_width), local_grads


def solution(mesh):
    axis_name = mesh.axis_names[0]
    group_size = mesh.shape[axis_name]
    sharded = P(axis_name)
    in_specs = (sharded, sharded, sharded, sharded, sharded, P(), P()) + (sharded,) * 7
    out_specs = (sharded, sharded, sharded, sharded, P(), P()) + (sharded,) * 7

    def gather_weights(row_shards, q_norm_gain, k_norm_gain):
        full_rows = tuple(lax.all_gather(row_shard, axis_name, axis=0, tiled=True) for row_shard in row_shards)
        return (full_rows[0], full_rows[1], q_norm_gain, k_norm_gain) + full_rows[2:]

    def device_step(hidden, grad_out, positions, norm1_gain, norm2_gain, q_norm_gain, k_norm_gain, w_q, w_k, w_v, w_o, w_gate, w_up, w_down):
        row_shards = (norm1_gain, norm2_gain, w_q, w_k, w_v, w_o, w_gate, w_up, w_down)
        weights_fwd = gather_weights(row_shards, q_norm_gain, k_norm_gain)
        layer_out, saved_acts = forward_local(hidden, positions, weights_fwd)
        layer_out, row_shards = lax.optimization_barrier((layer_out, row_shards))
        weights_bwd = gather_weights(row_shards, q_norm_gain, k_norm_gain)
        d_hidden, local_grads = backward_local(grad_out, saved_acts, weights_bwd)
        inv_tokens = 1.0 / (hidden.shape[0] * hidden.shape[1] * group_size)
        row_grads = local_grads[:2] + local_grads[4:]
        reduced = tuple(lax.psum_scatter(row_grad * inv_tokens, axis_name, scatter_dimension=0, tiled=True) for row_grad in row_grads)
        qgain_sum = lax.psum(local_grads[2] * inv_tokens, axis_name)
        kgain_sum = lax.psum(local_grads[3] * inv_tokens, axis_name)
        return (layer_out, d_hidden, reduced[0], reduced[1], qgain_sum, kgain_sum) + reduced[2:]

    return jax.shard_map(device_step, mesh=mesh, in_specs=in_specs, out_specs=out_specs, check_vma=False)
```

profile of v0, /device:TPU:0, one launch (start us, length us, event | category | flops | bytes accessed | tf_op | source)
XLA Modules:
  0.0 2295.4 jit_solution(2494556886441159060)
XLA Ops:
  52.1 24.2 %all-gather.23.cloned.1.call-done = bf16[2048,1024]{1,0:T(8,128)(2,1)} async-done(((bf16[256,1024]{1,0:T(8,128)(2,1)}), bf16[2048,1024]{1,0:T(8,128)(2,1)}) %all-gather.23.cloned.1.call-update) | async-done | bytes 4194320 | tf_op jit(solution)/shard_map/all_gather | solution.py:151
  101.2 25.4 %all-gather.21.cloned.1.call-done = bf16[2048,2048]{1,0:T(8,128)(2,1)} async-done(((bf16[256,2048]{1,0:T(8,128)(2,1)}), bf16[2048,2048]{1,0:T(8,128)(2,1)}) %all-gather.21.cloned.1.call-update) | async-done | bytes 8388624 | tf_op jit(solution)/shard_map/all_gather | solution.py:151
  251.5 46.4 %all-gather.29.cloned.1.call-done = bf16[2048,6144]{1,0:T(8,128)(2,1)} async-done(((bf16[256,6144]{1,0:T(8,128)(2,1)}), bf16[2048,6144]{1,0:T(8,128)(2,1)}) %all-gather.29.cloned.1.call-update) | async-done | bytes 25165840 | tf_op jit(solution)/shard_map/all_gather | solution.py:151
  297.9 28.8 %convolution_convert_fusion = bf16[768,6144]{1,0:T(8,128)(2,1)} fusion(bf16[2048,6144]{1,0:T(8,128)(2,1)} %all-gather.29.cloned.1.call-done, bf16[768,2048]{1,0:T(8,128)(2,1)} %get-tuple-element.60, f32[2048]{0:T(1024)S(1)} %bitcast.243, f32[768]{0:T(1024)S(1)} %add_rsqrt_fusion.2), kind=kOutput, calls=%fused_computation.26 | convolution fusion | flops 19338362880 | bytes 37760000 | tf_op jit(solution)/shard_map/dot_general | solution.py:24
  326.7 92.6 %all-gather.27.cloned.1.call-done = bf16[2048,6144]{1,0:T(8,128)(2,1)} async-done(((bf16[256,6144]{1,0:T(8,128)(2,1)}), bf16[2048,6144]{1,0:T(8,128)(2,1)}) %all-gather.27.cloned.1.call-update) | async-done | bytes 25165840 | tf_op jit(solution)/shard_map/all_gather | solution.py:151
  419.2 25.4 %convolution_convert_fusion.1 = bf16[768,6144]{1,0:T(8,128)(2,1)} fusion(bf16[2048,6144]{1,0:T(8,128)(2,1)} %all-gather.27.cloned.1.call-done, bf16[768,2048]{1,0:T(8,128)(2,1)S(1)} %copy-done.27, f32[2048]{0:T(1024)S(1)} %bitcast.244, f32[768]{0:T(1024)S(1)} %add_rsqrt_fusion.2), kind=kOutput, calls=%fused_computation.27 | convolution fusion | flops 19338362880 | bytes 37760000 | tf_op jit(solution)/shard_map/dot_general | solution.py:24
  444.6 96.1 %all-gather.31.cloned.1.call-done = bf16[6144,2048]{1,0:T(8,128)(2,1)} async-done(((bf16[768,2048]{1,0:T(8,128)(2,1)}), bf16[6144,2048]{1,0:T(8,128)(2,1)}) %all-gather.31.cloned.1.call-update) | async-done | bytes 25165840 | tf_op jit(solution)/shard_map/all_gather | solution.py:151
  540.7 28.3 %fusion.27 = bf16[768,2048]{1,0:T(8,128)(2,1)} fusion(bf16[768,2048]{1,0:T(8,128)(2,1)S(1)} %copy-done.27, bf16[6144,2048]{1,0:T(8,128)(2,1)} %all-gather.31.cloned.1.call-done, bf16[768,6144]{1,0:T(8,128)(2,1)} %convolution_convert_fusion, bf16[768,6144]{1,0:T(8,128)(2,1)} %convolution_convert_fusion.1), kind=kOutput, calls=%fused_computation.45 | convolution fusion | flops 19372965888 | bytes 50331648 | tf_op jit(solution)/shard_map/dot_general | solution.py:24
  589.4 99.7 %all-gather.33.cloned.1.call-done = bf16[6144,2048]{1,0:T(8,128)(2,1)} async-done(((bf16[768,2048]{1,0:T(8,128)(2,1)}), bf16[6144,2048]{1,0:T(8,128)(2,1)}) %all-gather.33.cloned.1.call-update) | async-done | bytes 25165840 | tf_op jit(solution)/shard_map/all_gather | solution.py:151
  689.0 38.7 %fusion.5 = (bf16[768,6144]{1,0:T(8,128)(2,1)}, f32[6144,768]{0,1:T(8,128)}) fusion(bf16[768,6144]{1,0:T(8,128)(2,1)} %convolution_convert_fusion, bf16[768,6144]{1,0:T(8,128)(2,1)} %convolution_convert_fusion.1, bf16[6144,2048]{1,0:T(8,128)(2,1)} %all-gather.33.cloned.1.call-done, bf16[768,2048]{1,0:T(8,128)(2,1)} %bitcast.227), kind=kOutput, calls=%fused_computation.14 | convolution fusion | flops 19383975936 | bytes 75497472 | tf_op jit(solution)/shard_map/dot_general | solution.py:32
  727.7 82.8 %all-gather.35.cloned.1.call-done = bf16[2048,6144]{1,0:T(8,128)(2,1)} async-done(((bf16[256,6144]{1,0:T(8,128)(2,1)}), bf16[2048,6144]{1,0:T(8,128)(2,1)}) %all-gather.35.cloned.1.call-update) | async-done | bytes 25165840 | tf_op jit(solution)/shard_map/all_gather | solution.py:151
  810.5 27.0 %fusion.113 = f32[768,2048]{1,0:T(8,128)} fusion(bf16[768,6144]{1,0:T(8,128)(2,1)} %get-tuple-element.61, bf16[2048,6144]{1,0:T(8,128)(2,1)} %all-gather.35.cloned.1.call-done), kind=kOutput, calls=%fused_computation.178 | convolution fusion | flops 19327352832 | bytes 40894464 | tf_op jit(solution)/shard_map/dot_general | solution.py:32
  837.5 94.3 %all-gather.37.cloned.1.call-done = bf16[2048,6144]{1,0:T(8,128)(2,1)} async-done(((bf16[256,6144]{1,0:T(8,128)(2,1)}), bf16[2048,6144]{1,0:T(8,128)(2,1)}) %all-gather.37.cloned.1.call-update) | async-done | bytes 25165840 | tf_op jit(solution)/shard_map/all_gather | solution.py:151
  931.8 35.3 %fusion.25 = (f32[2048]{0:T(1024)}, f32[768]{0:T(1024)S(1)}, f32[768,2048]{1,0:T(8,128)}) fusion(bf16[768,2048]{1,0:T(8,128)(2,1)} %get-tuple-element.60, f32[768]{0:T(1024)S(1)} %copy-done.47, f32[2048]{0:T(1024)S(1)} %bitcast.241, f32[768,2048]{1,0:T(8,128)} %fusion.113, bf16[2048,6144]{1,0:T(8,128)(2,1)} %all-gather.37.cloned.1.call-done, ...), kind=kOutput, calls=%fused_computation.43 | convolution fusion | flops 19372963840 | bytes 69228544 | tf_op jit(solution)/shard_map/dot_general | solution.py:32
  1014.2 19.3 fusion.76
  1102.5 20.0 fusion.71
  1230.4 32.0 %convolution_multiply_fusion.2 = f32[6144,2048]{1,0:T(8,128)} fusion(bf16[768,2048]{1,0:T(8,128)(2,1)S(1)} %bitcast.228, bf16[768,6144]{1,0:T(8,128)(2,1)} %convolution_convert_fusion, bf16[768,6144]{1,0:T(8,128)(2,1)} %convolution_convert_fusion.1), kind=kOutput, calls=%fused_computation.8 | convolution fusion | flops 19377684480 | bytes 72351744 | tf_op jit(solution)/shard_map/dot_general | solution.py:28
  1264.2 30.1 %convolution_multiply_fusion.1 = f32[2048,6144]{1,0:T(8,128)} fusion(bf16[768,6144]{1,0:T(8,128)(2,1)} %get-tuple-element.61, bf16[768,2048]{1,0:T(8,128)(2,1)S(1)} %copy-done.28, f32[2048]{0:T(1024)S(1)} %bitcast.245, f32[768]{0:T(1024)S(1)} %copy-done.48), kind=kOutput, calls=%fused_computation.7 | convolution fusion | flops 19346227200 | bytes 62925824 | tf_op jit(solution)/shard_map/dot_general | solution.py:28
  1294.4 40.0 %convolution_multiply_fusion = f32[2048,6144]{1,0:T(8,128)} fusion(bf16[768,2048]{1,0:T(8,128)(2,1)S(1)} %copy-done.28, f32[2048]{0:T(1024)S(1)} %bitcast.246, f32[768]{0:T(1024)S(1)} %copy-done.48, bf16[768,6144]{1,0:T(8,128)(2,1)} %convolution_convert_fusion.1, f32[6144,768]{0,1:T(8,128)} %get-tuple-element.62), kind=kOutput, calls=%fused_computation.6 | convolution fusion | flops 19379257344 | bytes 81800192 | tf_op jit(solution)/shard_map/dot_general | solution.py:28
  1378.2 23.3 %all-reduce.2 = (f32[2048]{0:T(1024)S(1)}, f32[2048]{0:T(1024)S(1)}, f32[128]{0:T(128)}, f32[128]{0:T(128)}) all-reduce(f32[2048]{0:T(1024)S(1)} %broadcast_multiply_fusion.5, f32[2048]{0:T(1024)S(1)} %broadcast_multiply_fusion.4, f32[128]{0:T(128)S(1)} %broadcast_multiply_fusion.9, ...), channel_id=2, replica_groups=mesh['fsdp'=8] {'fsdp'}, use_global_device_ids=true, to_apply=%region_12.13.clone | all-reduce | flops 4352 | bytes 34816
  1410.8 41.7 %reduce-scatter.14.cloned.1.call-done = f32[256,2048]{1,0:T(8,128)} async-done(((f32[2048,2048]{1,0:T(8,128)}), f32[256,2048]{1,0:T(8,128)}) %reduce-scatter.14.cloned.1.call-update) | async-done | bytes 2097168 | tf_op jit(solution)/shard_map/reduce_scatter | solution.py:163
  1452.5 278.7 %reduce-scatter.20.cloned.1.call-done = f32[768,2048]{1,0:T(8,128)} async-done(((f32[6144,2048]{1,0:T(8,128)}), f32[768,2048]{1,0:T(8,128)}) %reduce-scatter.20.cloned.1.call-update) | async-done | bytes 6291472 | tf_op jit(solution)/shard_map/reduce_scatter | solution.py:163
  1731.1 278.5 %reduce-scatter.16.cloned.1.call-done = f32[256,6144]{1,0:T(8,128)} async-done(((f32[2048,6144]{1,0:T(8,128)}), f32[256,6144]{1,0:T(8,128)}) %reduce-scatter.16.cloned.1.call-update) | async-done | bytes 6291472 | tf_op jit(solution)/shard_map/reduce_scatter | solution.py:163
  2009.7 278.7 %reduce-scatter.18.cloned.1.call-done = f32[256,6144]{1,0:T(8,128)} async-done(((f32[2048,6144]{1,0:T(8,128)}), f32[256,6144]{1,0:T(8,128)}) %reduce-scatter.18.cloned.1.call-update) | async-done | bytes 6291472 | tf_op jit(solution)/shard_map/reduce_scatter | solution.py:163
  (321 shorter events, 492.8 us)
Async XLA Ops:
  7.2 36.6 %all-gather.19.cloned.1.call-start = ((), (), s32[]{:S(2)}) async-start(), calls=%async_computation.7 | async-start | bytes 4718592 | tf_op jit(solution)/shard_map/all_gather | solution.py:151
  7.9 68.4 %all-gather.23.cloned.1.call-start = ((), (), s32[]{:S(2)}) async-start(), calls=%async_computation.9 | async-start | bytes 4718592 | tf_op jit(solution)/shard_map/all_gather | solution.py:151
  8.7 117.8 %all-gather.21.cloned.1.call-start = ((), (), s32[]{:S(2)}) async-start(), calls=%async_computation.8 | async-start | bytes 9437184 | tf_op jit(solution)/shard_map/all_gather | solution.py:151
  9.4 230.6 %all-gather.25.cloned.1.call-start = ((), (), s32[]{:S(2)}) async-start(), calls=%async_computation.10 | async-start | bytes 9437184 | tf_op jit(solution)/shard_map/all_gather | solution.py:151
  10.0 287.9 %all-gather.29.cloned.1.call-start = ((), (), s32[]{:S(2)}) async-start(), calls=%async_computation.12 | async-start | bytes 28311552 | tf_op jit(solution)/shard_map/all_gather | solution.py:151
  10.6 408.6 %all-gather.27.cloned.1.call-start = ((), (), s32[]{:S(2)}) async-start(), calls=%async_computation.11 | async-start | bytes 28311552 | tf_op jit(solution)/shard_map/all_gather | solution.py:151
  11.2 529.5 %all-gather.31.cloned.1.call-start = ((), (), s32[]{:S(2)}) async-start(), calls=%async_computation.13 | async-start | bytes 28311552 | tf_op jit(solution)/shard_map/all_gather | solution.py:151
  12.0 677.1 %all-gather.33.cloned.1.call-start = ((), (), s32[]{:S(2)}) async-start(), calls=%async_computation.14 | async-start | bytes 28311552 | tf_op jit(solution)/shard_map/all_gather | solution.py:151
  27.0 171.4 %copy-start.49 = (f32[128]{0:T(128)}, f32[128]{0:T(128)S(1)}, u32[]{:S(2)}) copy-start(f32[128]{0:T(128)S(1)} %convert_element_type.196) | copy-start | bytes 1540
  41.3 157.1 %copy-start.10 = (f32[3,256,128]{1,2,0:T(8,128)}, f32[3,256,128]{1,2,0:T(8,128)S(1)}, u32[]{:S(2)}) copy-start(f32[3,256,128]{1,2,0:T(8,128)S(1)} %get-tuple-element.65) | copy-start | bytes 1179652
  251.5 167.8 %copy-start.46 = (f32[768]{0:T(1024)}, f32[768]{0:T(1024)S(1)}, u32[]{:S(2)}) copy-start(f32[768]{0:T(1024)S(1)} %add_rsqrt_fusion.2) | copy-start | bytes 9220
  569.1 241.5 %all-gather.35.cloned.1.call-start = ((), (), s32[]{:S(2)}) async-start(), calls=%async_computation.15 | async-start | bytes 28311552 | tf_op jit(solution)/shard_map/all_gather | solution.py:151
  569.8 362.0 %all-gather.37.cloned.1.call-start = ((), (), s32[]{:S(2)}) async-start(), calls=%async_computation.16 | async-start | bytes 28311552 | tf_op jit(solution)/shard_map/all_gather | solution.py:151
  570.4 411.7 %all-gather.39.cloned.1.call-start = ((), (), s32[]{:S(2)}) async-start(), calls=%async_computation.17 | async-start | bytes 9437184 | tf_op jit(solution)/shard_map/all_gather | solution.py:151
  571.1 774.8 %all-gather.45.cloned.1.call-start = ((), (), s32[]{:S(2)}) async-start(), calls=%async_computation.20 | async-start | bytes 4718592 | tf_op jit(solution)/shard_map/all_gather | solution.py:151
  571.7 782.0 %all-gather.43.cloned.1.call-start = ((), (), s32[]{:S(2)}) async-start(), calls=%async_computation.19 | async-start | bytes 4718592 | tf_op jit(solution)/shard_map/all_gather | solution.py:151
  572.5 790.2 %all-gather.41.cloned.1.call-start = ((), (), s32[]{:S(2)}) async-start(), calls=%async_computation.18 | async-start | bytes 9437184 | tf_op jit(solution)/shard_map/all_gather | solution.py:151
  589.3 821.5 %reduce-scatter.10.cloned.1.call-start = ((), (), s32[]{:S(2)}) async-start(), calls=%async_computation.22 | async-start | bytes 9437184 | tf_op jit(solution)/shard_map/reduce_scatter | solution.py:163
  1069.0 341.8 %reduce-scatter.12.cloned.1.call-start = ((), (), s32[]{:S(2)}) async-start(), calls=%async_computation.23 | async-start | bytes 9437184 | tf_op jit(solution)/shard_map/reduce_scatter | solution.py:163
  1091.4 319.4 %reduce-scatter.8.cloned.1.call-start = ((), (), s32[]{:S(2)}) async-start(), calls=%async_computation.21 | async-start | bytes 18874368 | tf_op jit(solution)/shard_map/reduce_scatter | solution.py:163
  1213.6 238.9 %reduce-scatter.14.cloned.1.call-start = ((), (), s32[]{:S(2)}) async-start(), calls=%async_computation.24 | async-start | bytes 18874368 | tf_op jit(solution)/shard_map/reduce_scatter | solution.py:163
  1228.5 502.6 %reduce-scatter.20.cloned.1.call-start = ((), (), s32[]{:S(2)}) async-start(), calls=%async_computation.27 | async-start | bytes 56623104 | tf_op jit(solution)/shard_map/reduce_scatter | solution.py:163
  1262.4 747.3 %reduce-scatter.16.cloned.1.call-start = ((), (), s32[]{:S(2)}) async-start(), calls=%async_computation.25 | async-start | bytes 56623104 | tf_op jit(solution)/shard_map/reduce_scatter | solution.py:163
  1294.3 994.0 %reduce-scatter.18.cloned.1.call-start = ((), (), s32[]{:S(2)}) async-start(), calls=%async_computation.26 | async-start | bytes 56623104 | tf_op jit(solution)/shard_map/reduce_scatter | solution.py:163
  (71 other events, 844.1 us)
Sparse Core Ops, SparseCore 0:
  9.8 33.8 all-gather.18
  45.6 30.7 all-gather.22
  78.2 48.3 all-gather.20
  128.2 48.3 all-gather.24
  178.2 119.6 all-gather.28
  299.6 119.6 all-gather.26
  421.1 119.6 all-gather.30
  569.2 119.7 all-gather.32
  690.8 119.6 all-gather.34
  812.2 119.6 all-gather.36
  933.7 48.3 all-gather.38
  983.7 30.7 all-gather.44
  1016.3 30.7 all-gather.42
  1048.8 48.3 all-gather.40
  1100.9 62.2 reduce-scatter.9
  1167.0 62.2 reduce-scatter.11
  1233.2 106.9 reduce-scatter.7
  1344.1 108.3 reduce-scatter.13
  1456.6 274.4 reduce-scatter.19
  1735.1 274.5 reduce-scatter.15
  2013.8 274.5 reduce-scatter.17
where the time goes:
time: 2300 us
  waiting for transfers between devices  1460 us (63%)
  matrix products  479 us (21%)
  local copies, waits for them, and re-layouts  175 us (8%)
  other arithmetic  101 us (4%)
  blocking collectives  69.4 us (3%)
    reduce_scatter x7, waiting for transfers between devices, device_step(): lax.psum_scatter(row_grad * inv_tokens, axis_name, scatter_dimension=0, t...  878 us
    all_gather x14, waiting for transfers between devices, gather_weights(): lax.all_gather(row_shard, axis_name, axis=0, tiled=True)  570 us
    dot_general x7, matrix products, matmul_nt(): lax.dot_general(left_op, right_op, (((1,), (1,)), ((), ())), preferred_el...  146 us
    dot_general x7, matrix products, matmul_tn(): lax.dot_general(left_op, right_op, (((0,), (0,)), ((), ())), preferred_el...  141 us
    dot_general x7, matrix products, matmul(): return jnp.dot(left_op, right_op, preferred_element_type=jnp.float32)  117 us
    all_gather x4, blocking collectives, gather_weights(): lax.all_gather(row_shard, axis_name, axis=0, tiled=True)  46.1 us
  transfers between devices with their start and end apart: 21, of which 13 were waited for; matrix products, arithmetic and copies ran while one was open for 31% of the time, Pallas kernels for 0%

commit v1 on v0

v1 whole, which is shorter than its diff:
```python
import jax
import jax.numpy as jnp
from jax import lax
from jax.sharding import PartitionSpec as P


RMS_EPS = 1e-6
ROPE_THETA = 1000000.0


def rms_scale(tensor):
    return lax.rsqrt(jnp.mean(tensor * tensor, axis=-1, keepdims=True) + RMS_EPS)


def norm_backward(d_unit, unit_val, scale_val):
    return scale_val * (d_unit - unit_val * jnp.mean(d_unit * unit_val, axis=-1, keepdims=True))


def rotate_half(tensor):
    half_dim = tensor.shape[-1] // 2
    return jnp.concatenate([-tensor[..., half_dim:], tensor[..., :half_dim]], axis=-1)


def matmul(left_op, right_op):
    return jnp.dot(left_op, right_op, preferred_element_type=jnp.float32)


def matmul_tn(left_op, right_op):
    return lax.dot_general(left_op, right_op, (((0,), (0,)), ((), ())), preferred_element_type=jnp.float32)


def matmul_nt(left_op, right_op):
    return lax.dot_general(left_op, right_op, (((1,), (1,)), ((), ())), preferred_element_type=jnp.float32)


def rope_tables(positions, head_dim):
    inv_freq = ROPE_THETA ** (-2.0 * jnp.arange(head_dim // 2, dtype=jnp.float32) / head_dim)
    rope_angle = positions.reshape(-1, 1).astype(jnp.float32) * inv_freq
    cos_half = jnp.cos(rope_angle)
    sin_half = jnp.sin(rope_angle)
    cos_t = jnp.concatenate([cos_half, cos_half], axis=-1)[:, None, :]
    sin_t = jnp.concatenate([sin_half, sin_half], axis=-1)[:, None, :]
    return cos_t, sin_t


def head_norm_rope(projected, num_heads, head_dim, gain_vec, cos_t, sin_t):
    heads_float = projected.reshape(projected.shape[0], num_heads, head_dim).astype(jnp.float32)
    head_scale = rms_scale(heads_float)
    head_unit = heads_float * head_scale
    scaled = head_unit * gain_vec.astype(jnp.float32)
    rotated = (scaled * cos_t + rotate_half(scaled) * sin_t).astype(jnp.bfloat16)
    return rotated, head_unit, head_scale


def head_norm_rope_backward(d_rotated, head_unit, head_scale, gain_vec, cos_t, sin_t):
    d_scaled = d_rotated * cos_t - rotate_half(d_rotated * sin_t)
    d_gain = jnp.sum(d_scaled * head_unit, axis=(0, 1))
    d_projected = norm_backward(d_scaled * gain_vec.astype(jnp.float32), head_unit, head_scale)
    return d_projected.reshape(d_projected.shape[0], -1).astype(jnp.bfloat16), d_gain


NEG = -1e30


def attention_forward(x_float, positions, weights, batch_local, seq_len):
    norm1_gain, q_norm_gain, k_norm_gain, w_q, w_k, w_v = weights
    tokens = x_float.shape[0]
    head_dim = q_norm_gain.shape[0]
    num_heads = w_q.shape[1] // head_dim
    kv_heads = w_k.shape[1] // head_dim
    x_scale = rms_scale(x_float)
    x_unit = x_float * x_scale
    normed = (x_unit * norm1_gain.astype(jnp.float32)).astype(jnp.bfloat16)
    q_proj = matmul(normed, w_q).astype(jnp.bfloat16)
    k_proj = matmul(normed, w_k).astype(jnp.bfloat16)
    v_proj = matmul(normed, w_v).astype(jnp.bfloat16)
    cos_t, sin_t = rope_tables(positions, head_dim)
    q_rot, q_unit, q_scale = head_norm_rope(q_proj, num_heads, head_dim, q_norm_gain, cos_t, sin_t)
    k_rot, k_unit, k_scale = head_norm_rope(k_proj, kv_heads, head_dim, k_norm_gain, cos_t, sin_t)
    q_grouped = q_rot.reshape(batch_local, seq_len, kv_heads, num_heads // kv_heads, head_dim)
    k_seq = k_rot.reshape(batch_local, seq_len, kv_heads, head_dim)
    v_seq = v_proj.reshape(batch_local, seq_len, kv_heads, head_dim)
    scores = jnp.einsum("bskgd,btkd->bksgt", q_grouped, k_seq, preferred_element_type=jnp.float32) * (head_dim ** -0.5)
    causal = (jnp.arange(seq_len)[:, None] >= jnp.arange(seq_len)[None, :])[:, None, :]
    attn_probs = jax.nn.softmax(jnp.where(causal, scores, NEG), axis=-1)
    attn_ctx = jnp.einsum("bksgt,btkd->bskgd", attn_probs.astype(jnp.bfloat16), v_seq, preferred_element_type=jnp.float32).astype(jnp.bfloat16).reshape(tokens, num_heads * head_dim)
    saved = (x_unit, x_scale, normed, cos_t, sin_t, q_unit, q_scale, k_unit, k_scale, q_grouped, k_seq, v_seq, attn_probs)
    return attn_ctx, saved


def attention_backward(d_attn_ctx, saved, q_norm_gain, k_norm_gain):
    _, _, _, cos_t, sin_t, q_unit, q_scale, k_unit, k_scale, q_grouped, k_seq, v_seq, attn_probs = saved
    batch_local, seq_len, kv_heads, kv_group, head_dim = q_grouped.shape
    tokens = batch_local * seq_len
    num_heads = kv_heads * kv_group
    d_attn_ctx = d_attn_ctx.reshape(batch_local, seq_len, kv_heads, kv_group, head_dim)
    d_value = jnp.einsum("bksgt,bskgd->btkd", attn_probs.astype(jnp.bfloat16), d_attn_ctx, preferred_element_type=jnp.float32).astype(jnp.bfloat16).reshape(tokens, kv_heads * head_dim)
    d_probs = jnp.einsum("bskgd,btkd->bksgt", d_attn_ctx, v_seq, preferred_element_type=jnp.float32)
    d_scores = attn_probs * (d_probs - jnp.sum(attn_probs * d_probs, axis=-1, keepdims=True))
    d_scores = (d_scores * (head_dim ** -0.5)).astype(jnp.bfloat16)
    d_q_rot = jnp.einsum("bksgt,btkd->bskgd", d_scores, k_seq, preferred_element_type=jnp.float32).reshape(tokens, num_heads, head_dim)
    d_k_rot = jnp.einsum("bksgt,bskgd->btkd", d_scores, q_grouped, preferred_element_type=jnp.float32).reshape(tokens, kv_heads, head_dim)
    d_query, grad_qgain = head_norm_rope_backward(d_q_rot, q_unit, q_scale, q_norm_gain, cos_t, sin_t)
    d_key, grad_kgain = head_norm_rope_backward(d_k_rot, k_unit, k_scale, k_norm_gain, cos_t, sin_t)
    return d_query, d_key, d_value, grad_qgain, grad_kgain


def pick(bit, first, second):
    return jnp.where(bit == 0, first, second), jnp.where(bit == 0, second, first)


def solution(mesh):
    axis_name = mesh.axis_names[0]
    group_size = mesh.shape[axis_name]
    sharded = P(axis_name)
    in_specs = (sharded, sharded, sharded, sharded, sharded, P(), P()) + (sharded,) * 7
    out_specs = (sharded, sharded, sharded, sharded, P(), P()) + (sharded,) * 7
    CORE, XDIR, YDIR = 1, 2, 4

    def swap(value, mask):
        return lax.ppermute(value, axis_name, [(j, j ^ mask) for j in range(group_size)])

    def gather_rows(row_shard):
        return lax.all_gather(row_shard, axis_name, axis=0, tiled=True)

    def device_step(hidden, grad_out, positions, norm1_gain, norm2_gain, q_norm_gain, k_norm_gain, w_q, w_k, w_v, w_o, w_gate, w_up, w_down):
        batch_local, seq_len, width = hidden.shape
        tokens = batch_local * seq_len
        me = lax.axis_index(axis_name)
        c_bit, x_bit, y_bit = me % 2, (me // 2) % 2, me // 4
        ff_block = w_down.shape[0]
        rows = w_gate.shape[0]

        def row_tokens(own):
            pair = jnp.concatenate([own, swap(own, XDIR)], axis=0)
            return jnp.concatenate([pair, swap(pair, CORE)], axis=0)

        def quarter_columns(shard):
            blk = [shard[:, j * ff_block:(j + 1) * ff_block] for j in range(8)]
            first = jnp.concatenate([blk[0], blk[1], blk[4], blk[5]], axis=1)
            second = jnp.concatenate([blk[2], blk[3], blk[6], blk[7]], axis=1)
            keep, send = pick(x_bit, first, second)
            got = swap(send, XDIR)
            row0, row1 = pick(x_bit, keep, got)
            both = jnp.concatenate([row0, row1], axis=0)
            col = [both[:, j * ff_block:(j + 1) * ff_block] for j in range(4)]
            keep, send = pick(c_bit, jnp.concatenate([col[0], col[2]], axis=1), jnp.concatenate([col[1], col[3]], axis=1))
            got = swap(send, CORE)
            core0, core1 = pick(c_bit, keep, got)
            four = jnp.concatenate([core0[:rows], core1[:rows], core0[rows:], core1[rows:]], axis=0)
            got = swap(four, YDIR)
            return jnp.concatenate(pick(y_bit, four, got), axis=0)

        def row_sum(partial_rows):
            far = partial_rows(2 * tokens, 4 * tokens)
            from_core = swap(far, CORE)
            side = partial_rows(tokens, 2 * tokens) + from_core[tokens:]
            from_x = swap(side, XDIR)
            total = partial_rows(0, tokens) + from_core[:tokens]
            return total, from_x

        def scatter_columns(left_send, left_keep, right):
            part = matmul_tn(left_send, right)
            got = swap(part, YDIR)
            mine = matmul_tn(left_keep, right) + got
            blk = [mine[j * rows:(j + 1) * rows] for j in range(4)]
            keep, send = pick(c_bit, jnp.concatenate([blk[0], blk[2]], axis=0), jnp.concatenate([blk[1], blk[3]], axis=0))
            got = swap(send, CORE)
            core0, core1 = pick(c_bit, keep, got)
            both = jnp.concatenate([core0, core1], axis=1)
            keep, send = pick(x_bit, both[:rows], both[rows:])
            got = swap(send, XDIR)
            x0, x1 = pick(x_bit, keep, got)
            parts = [x0[:, :ff_block], x0[:, 2 * ff_block:3 * ff_block], x1[:, :ff_block], x1[:, 2 * ff_block:3 * ff_block]]
            parts += [x0[:, ff_block:2 * ff_block], x0[:, 3 * ff_block:], x1[:, ff_block:2 * ff_block], x1[:, 3 * ff_block:]]
            return jnp.concatenate(parts, axis=1)

        gains = lax.all_gather(jnp.stack([norm1_gain, norm2_gain]), axis_name, axis=1, tiled=True)
        gain1, gain2 = gains[0].astype(jnp.float32), gains[1].astype(jnp.float32)
        full_q, full_k, full_v, full_o = gather_rows(w_q), gather_rows(w_k), gather_rows(w_v), gather_rows(w_o)
        gate_q = quarter_columns(w_gate)
        up_q = quarter_columns(w_up)
        down_q = jnp.concatenate(pick(y_bit, w_down, swap(w_down, YDIR)), axis=0)
        dy_flat = grad_out.reshape(tokens, width)
        dy_row = row_tokens(dy_flat)

        x_float = hidden.reshape(tokens, width).astype(jnp.float32)
        attn_ctx, saved = attention_forward(x_float, positions, (gains[0], q_norm_gain, k_norm_gain, full_q, full_k, full_v), batch_local, seq_len)
        attn_out = matmul(attn_ctx, full_o).astype(jnp.bfloat16)
        resid_float = (x_float + attn_out.astype(jnp.float32)).astype(jnp.bfloat16).astype(jnp.float32)
        r_scale = rms_scale(resid_float)
        r_unit = resid_float * r_scale
        mlp_in = row_tokens((r_unit * gain2).astype(jnp.bfloat16))

        gate_proj = matmul(mlp_in, gate_q).astype(jnp.bfloat16)
        up_proj = matmul(mlp_in, up_q).astype(jnp.bfloat16)
        gate_float = gate_proj.astype(jnp.float32)
        up_float = up_proj.astype(jnp.float32)
        mlp_act = (jax.nn.silu(gate_float) * up_float).astype(jnp.bfloat16)

        d_mlp_act = matmul_nt(dy_row, down_q)
        gate_sig = jax.nn.sigmoid(gate_float)
        d_up = (d_mlp_act * gate_float * gate_sig).astype(jnp.bfloat16)
        d_gate = (d_mlp_act * up_float * gate_sig * (1.0 + gate_float * (1.0 - gate_sig))).astype(jnp.bfloat16)
        inv_tokens = 1.0 / (tokens * group_size)
        act_keep, act_send = pick(y_bit, mlp_act[:, :ff_block], mlp_act[:, ff_block:])
        down_part = matmul_tn(act_send, dy_row)
        down_got = swap(down_part, YDIR)
        grad_down = (matmul_tn(act_keep, dy_row) + down_got) * inv_tokens

        d_mlp_in, dm_from_x = row_sum(lambda lo, hi: matmul_nt(d_gate[lo:hi], gate_q) + matmul_nt(d_up[lo:hi], up_q))
        d_mlp_in = d_mlp_in + dm_from_x
        in_keep, in_send = pick(y_bit, mlp_in[:, :width // 2], mlp_in[:, width // 2:])
        grad_gate = scatter_columns(in_send, in_keep, d_gate) * inv_tokens
        grad_up = scatter_columns(in_send, in_keep, d_up) * inv_tokens

        down_total, down_from_x = row_sum(lambda lo, hi: matmul(mlp_act[lo:hi], down_q))

        grad_norm2 = jnp.sum(d_mlp_in * r_unit, axis=0)
        d_resid = dy_flat.astype(jnp.float32) + norm_backward(d_mlp_in * gain2, r_unit, r_scale)
        d_resid_bf = d_resid.astype(jnp.bfloat16)
        d_attn_ctx = matmul_nt(d_resid_bf, full_o).astype(jnp.bfloat16)
        down_from_x, d_attn_ctx = lax.optimization_barrier((down_from_x, d_attn_ctx))
        down_proj = (down_total + down_from_x).astype(jnp.bfloat16)
        layer_out = (resid_float + down_proj.astype(jnp.float32)).astype(jnp.bfloat16).reshape(hidden.shape)
        grad_wo = lax.psum_scatter(matmul_tn(attn_ctx, d_resid_bf) * inv_tokens, axis_name, scatter_dimension=0, tiled=True)
        d_query, d_key, d_value, grad_qgain, grad_kgain = attention_backward(d_attn_ctx, saved, q_norm_gain, k_norm_gain)
        x_unit, x_scale, normed = saved[:3]
        grad_wv = lax.psum_scatter(matmul_tn(normed, d_value) * inv_tokens, axis_name, scatter_dimension=0, tiled=True)
        grad_wk = lax.psum_scatter(matmul_tn(normed, d_key) * inv_tokens, axis_name, scatter_dimension=0, tiled=True)
        grad_wq = lax.psum_scatter(matmul_tn(normed, d_query) * inv_tokens, axis_name, scatter_dimension=0, tiled=True)
        d_normed = matmul_nt(d_query, full_q) + matmul_nt(d_key, full_k) + matmul_nt(d_value, full_v)
        grad_norm1 = jnp.sum(d_normed * x_unit, axis=0)
        d_hidden = (d_resid + norm_backward(d_normed * gain1, x_unit, x_scale)).astype(jnp.bfloat16).reshape(hidden.shape)

        small = lax.psum(jnp.concatenate([grad_norm1, grad_norm2, grad_qgain, grad_kgain]) * inv_tokens, axis_name)
        head_dim = q_norm_gain.shape[0]
        own1 = lax.dynamic_slice_in_dim(small, me * rows, rows)
        own2 = lax.dynamic_slice_in_dim(small, width + me * rows, rows)
        gq = small[2 * width:2 * width + head_dim]
        gk = small[2 * width + head_dim:]
        return (layer_out, d_hidden, own1, own2, gq, gk, grad_wq, grad_wk, grad_wv, grad_wo, grad_gate, grad_up, grad_down)

    return jax.shard_map(device_step, mesh=mesh, in_specs=in_specs, out_specs=out_specs, check_vma=False)
```

time: 2300 us -> 1870 us (0.81)
  waiting for transfers between devices: 1460 us -> 826 us
  other arithmetic: 101 us -> 198 us
  blocking collectives: 69.4 us -> 125 us
    reduce_scatter x7 -> x4, waiting for transfers between devices: 878 us -> 0.02 us  [the longest x1 0.01 us: device_step(): lax.psum_scatter(matmul_tn(attn_ctx, d_resid_bf) * inv_tokens, axis_name,...]
    ppermute x0 -> x22, waiting for transfers between devices: none -> 821 us  [swap(): lax.ppermute(value, axis_name, [(j, j ^ mask) for j in range(group_size)])]
    all_gather x14 -> x4, waiting for transfers between devices: 570 us -> 1.84 us  [gather_rows(): return lax.all_gather(row_shard, axis_name, axis=0, tiled=True)]
    all_gather x4 -> x1, blocking collectives: 46.1 us -> 101 us  [device_step(): lax.all_gather(jnp.stack([norm1_gain, norm2_gain]), axis_name, axis=1, ti...]
    select_n x0 -> x19, other arithmetic: none -> 52.2 us  [the longest x12 27.5 us: pick(): jnp.where(bit == 0, second, first)]
    psum x0 -> x1, blocking collectives: none -> 23.6 us  [device_step(): lax.psum(jnp.concatenate([grad_norm1, grad_norm2, grad_qgain, grad_kgain]...]
    unnamed x1 -> x0, blocking collectives: 23.3 us -> none
    dot_general x7 -> x9, matrix products: 117 us -> 126 us  [matmul(): return jnp.dot(left_op, right_op, preferred_element_type=jnp.float32)]
  transfers between devices with their start and end apart: 21 -> 30, of which waited for: 13 -> 10; matrix products, arithmetic and copies ran while one was open for 31% -> 38% of each run, Pallas kernels for 0% -> 0%
where the time goes in v1:
time: 1870 us
  waiting for transfers between devices  826 us (44%)
  matrix products  496 us (27%)
  other arithmetic  198 us (11%)
  local copies, waits for them, and re-layouts  187 us (10%)
  blocking collectives  125 us (7%)
    ppermute x22, waiting for transfers between devices, swap(): lax.ppermute(value, axis_name, [(j, j ^ mask) for j in range(group_size)])  821 us
    dot_general x11, matrix products, matmul_nt(): lax.dot_general(left_op, right_op, (((1,), (1,)), ((), ())), preferred_el...  151 us
    dot_general x10, matrix products, matmul_tn(): lax.dot_general(left_op, right_op, (((0,), (0,)), ((), ())), preferred_el...  140 us
    dot_general x9, matrix products, matmul(): return jnp.dot(left_op, right_op, preferred_element_type=jnp.float32)  126 us
    all_gather x1, blocking collectives, device_step(): lax.all_gather(jnp.stack([norm1_gain, norm2_gain]), axis_name, axis=1, ti...  101 us
  transfers between devices with their start and end apart: 30, of which 10 were waited for; matrix products, arithmetic and copies ran while one was open for 38% of the time, Pallas kernels for 0%

profile of v1, /device:TPU:0, one launch (start us, length us, event | category | flops | bytes accessed | tf_op | source)
XLA Modules:
  0.0 1866.4 jit_solution(2991978111220993656)
XLA Ops:
  22.0 101.2 %all_gather.15 = bf16[2,2048]{1,0:T(2,128)(2,1)S(1)} all-gather(bf16[2,256]{1,0:T(2,128)(2,1)S(1)} %pad_maximum_fusion.26), channel_id=1, replica_groups=mesh['fsdp'=8] {'fsdp'}, dimensions={1}, use_global_device_ids=true | all-gather | bytes 9216 | tf_op jit(solution)/shard_map/all_gather | solution.py:178
  298.7 57.3 %collective-permute-done = bf16[768,2048]{1,0:T(8,128)(2,1)S(1)} collective-permute-done((bf16[768,2048]{1,0:T(8,128)(2,1)S(1)}, bf16[768,2048]{1,0:T(8,128)(2,1)S(1)}, u32[]{:S(2)}, u32[]{:S(2)}) %collective-permute-start) | collective-permute-done | bytes 3145760 | tf_op jit(solution)/shard_map/ppermute | solution.py:121
  369.6 53.2 %collective-permute-done.11 = bf16[768,2048]{1,0:T(8,128)(2,1)} collective-permute-done((bf16[768,2048]{1,0:T(8,128)(2,1)}, bf16[768,2048]{1,0:T(8,128)(2,1)}, u32[]{:S(2)}, u32[]{:S(2)}) %collective-permute-start.11) | collective-permute-done | bytes 3145760 | tf_op jit(solution)/shard_map/ppermute | solution.py:121
  440.8 60.0 %collective-permute-done.7 = bf16[1024,1536]{1,0:T(8,128)(2,1)} collective-permute-done((bf16[1024,1536]{1,0:T(8,128)(2,1)}, bf16[1024,1536]{1,0:T(8,128)(2,1)}, u32[]{:S(2)}, u32[]{:S(2)}) %collective-permute-start.7) | collective-permute-done | bytes 3145760 | tf_op jit(solution)/shard_map/ppermute | solution.py:121
  505.6 28.0 %convolution_convert_fusion.1 = bf16[3072,1536]{1,0:T(8,128)(2,1)} fusion(bf16[1024,1536]{1,0:T(8,128)(2,1)} %get-tuple-element.54, bf16[1024,1536]{1,0:T(8,128)(2,1)} %get-tuple-element.53, bf16[1536,2048]{1,0:T(8,128)(2,1)} %collective-permute-done.1, bf16[768,2048]{1,0:T(8,128)(2,1)} %copy-done.36, bf16[768,2048]{1,0:T(8,128)(2,1)S(1)} %fusion.20), kind=kOutput, calls=%fused_computation.26 | convolution fusion | flops 19382403072 | bytes 28311552 | tf_op jit(solution)/shard_map/dot_general | solution.py:25
  533.6 27.6 %convolution_convert_fusion = bf16[3072,1536]{1,0:T(8,128)(2,1)} fusion(bf16[1024,1536]{1,0:T(8,128)(2,1)} %get-tuple-element.56, bf16[1024,1536]{1,0:T(8,128)(2,1)} %get-tuple-element.55, bf16[1536,2048]{1,0:T(8,128)(2,1)} %collective-permute-done.1, bf16[768,2048]{1,0:T(8,128)(2,1)} %copy-done.36, bf16[768,2048]{1,0:T(8,128)(2,1)S(1)} %fusion.20), kind=kOutput, calls=%fused_computation.25 | convolution fusion | flops 19382403072 | bytes 28311552 | tf_op jit(solution)/shard_map/dot_general | solution.py:25
  561.2 39.7 %fusion.5 = (bf16[3072,1536]{1,0:T(8,128)(2,1)}, bf16[3072,1536]{1,0:T(8,128)(2,1)}, bf16[3072,1536]{1,0:T(8,128)(2,1)}) fusion(bf16[3072,1536]{1,0:T(8,128)(2,1)} %convolution_convert_fusion, bf16[3072,1536]{1,0:T(8,128)(2,1)} %convolution_convert_fusion.1, bf16[768,2048]{1,0:T(8,128)(2,1)} %get-tuple-element.52, bf16[768,2048]{1,0:T(8,128)(2,1)} %get-tuple-element.51, ...), kind=kOutput, calls=%fused_computation.11 | convolution fusion | flops 19462619136 | bytes 66060288 | tf_op jit(solution)/shard_map/dot_general | solution.py:33
  616.3 18.2 convolution_add_fusion
  634.5 15.6 fusion.65
  709.3 102.7 %collective-permute-done.14 = f32[768,2048]{1,0:T(8,128)} collective-permute-done((f32[768,2048]{1,0:T(8,128)}, f32[768,2048]{1,0:T(8,128)}, u32[]{:S(2)}, u32[]{:S(2)}) %collective-permute-start.14) | collective-permute-done | bytes 6291488 | tf_op jit(solution)/shard_map/ppermute | solution.py:121
  837.4 108.4 %collective-permute-done.10 = f32[768,2048]{1,0:T(8,128)} collective-permute-done((f32[768,2048]{1,0:T(8,128)}, f32[768,2048]{1,0:T(8,128)}, u32[]{:S(2)}, u32[]{:S(2)}) %collective-permute-start.10) | collective-permute-done | bytes 6291488 | tf_op jit(solution)/shard_map/ppermute | solution.py:121
  965.3 19.6 %fusion.116 = f32[3,256,8,128]{1,3,2,0:T(8,128)} fusion(bf16[3,256,8,2,128]{1,4,3,2,0:T(8,128)(2,1)S(1)} %copy-done.80, f32[3,8,256,2,256]{2,4,3,1,0:T(8,128)} %fusion.138, f32[3,8,256,2,256]{2,4,3,1,0:T(8,128)} %get-tuple-element.104, f32[3,8,256,2]{2,3,1,0:T(2,128)} %copy-done.136), kind=kOutput, calls=%fused_computation.209 | convolution fusion | flops 827339008 | bytes 31506432 | tf_op jit(solution)/shard_map/bksgt,bskgd->btkd/dot_general | solution.py:102
  1056.1 21.1 %fusion.97 = f32[3,256,8,2,128]{1,4,3,2,0:T(8,128)} fusion(bf16[3,256,8,128,1]{1,3,4,2,0:T(8,128)(2,1)S(1)} %copy-done.98, f32[3,8,256,2,256]{2,4,3,1,0:T(8,128)} %fusion.138, f32[3,8,256,2,256]{2,4,3,1,0:T(8,128)} %get-tuple-element.104, f32[3,8,256,2]{2,3,1,0:T(2,128)S(1)} %copy-done.138), kind=kOutput, calls=%fused_computation.194 | convolution fusion | flops 827339008 | bytes 33079296 | tf_op jit(solution)/shard_map/bksgt,btkd->bskgd/dot_general | solution.py:101
  1141.1 17.6 fusion.30
  1180.7 16.8 fusion.142
  1213.5 17.8 fusion.67
  1232.4 171.3 %collective-permute-done.18 = f32[1024,1536]{1,0:T(8,128)} collective-permute-done((f32[1024,1536]{1,0:T(8,128)}, f32[1024,1536]{1,0:T(8,128)}, u32[]{:S(2)}, u32[]{:S(2)}) %collective-permute-start.18) | collective-permute-done | bytes 6291488 | tf_op jit(solution)/shard_map/ppermute | solution.py:121
  1403.6 18.5 convolution_add_fusion.1
  1437.2 162.7 %collective-permute-done.15 = f32[1024,1536]{1,0:T(8,128)} collective-permute-done((f32[1024,1536]{1,0:T(8,128)}, f32[1024,1536]{1,0:T(8,128)}, u32[]{:S(2)}, u32[]{:S(2)}) %collective-permute-start.15) | collective-permute-done | bytes 6291488 | tf_op jit(solution)/shard_map/ppermute | solution.py:121
  1599.9 18.8 %convolution_add_fusion.2 = f32[1024,1536]{1,0:T(8,128)S(1)} fusion(f32[1024,1536]{1,0:T(8,128)} %collective-permute-done.15, bf16[3072,1536]{1,0:T(8,128)(2,1)} %get-tuple-element.30, pred[]{:T(512)S(6)} %eq.9, bf16[3072,2048]{1,0:T(8,128)(2,1)} %copy-done.35), kind=kOutput, calls=%fused_computation.122 | convolution fusion | flops 9668395008 | bytes 34603008 | tf_op jit(solution)/shard_map/dot_general | solution.py:29
  1647.9 89.6 %collective-permute-done.21 = f32[768,2048]{1,0:T(8,128)} collective-permute-done((f32[768,2048]{1,0:T(8,128)}, f32[768,2048]{1,0:T(8,128)}, u32[]{:S(2)}, u32[]{:S(2)}) %collective-permute-start.21) | collective-permute-done | bytes 6291488 | tf_op jit(solution)/shard_map/ppermute | solution.py:121
  1737.5 18.6 add_multiply_fusion
  1762.2 16.2 collective-permute-done.17
  1815.0 23.6 %psum.7 = f32[4352]{0:T(1024)S(1)} all-reduce(f32[4352]{0:T(1024)S(1)} %maximum_multiply_fusion.2), channel_id=1, replica_groups=mesh['fsdp'=8] {'fsdp'}, use_global_device_ids=true, to_apply=%region_15.16 | all-reduce | flops 4352 | bytes 34816 | tf_op jit(solution)/shard_map/psum | solution.py:236
  (517 shorter events, 626.5 us)
Async XLA Ops:
  7.2 121.5 %all-gather.9.cloned.1.call-start = ((), (), s32[]{:S(2)}) async-start(), calls=%async_computation.6 | async-start | bytes 4718592 | tf_op jit(solution)/shard_map/all_gather | solution.py:124
  7.9 136.8 %all-gather.5.cloned.1.call-start = ((), (), s32[]{:S(2)}) async-start(), calls=%async_computation.4 | async-start | bytes 4718592 | tf_op jit(solution)/shard_map/all_gather | solution.py:124
  8.7 151.8 %all-gather.7.cloned.1.call-start = ((), (), s32[]{:S(2)}) async-start(), calls=%async_computation.5 | async-start | bytes 9437184 | tf_op jit(solution)/shard_map/all_gather | solution.py:124
  9.4 263.4 %all-gather.11.cloned.1.call-start = ((), (), s32[]{:S(2)}) async-start(), calls=%async_computation.7 | async-start | bytes 9437184 | tf_op jit(solution)/shard_map/all_gather | solution.py:124
  10.0 1849.3 %reduce-scatter.7.cloned.1.call-start = ((), (), s32[]{:S(2)}) async-start(), calls=%async_computation.9 | async-start | bytes 9437184 | tf_op jit(solution)/shard_map/reduce_scatter | solution.py:230
  12.7 273.9 %collective-permute-start.2 = (bf16[256,3072]{1,0:T(8,128)(2,1)}, bf16[256,3072]{1,0:T(8,128)(2,1)}, u32[]{:S(2)}, u32[]{:S(2)}) collective-permute-start(bf16[256,3072]{1,0:T(8,128)(2,1)} %broadcast_select_fusion.22), channel_id=1, source_target_pairs={{0,2},{1,3},{2,0},{3,1},{4,6},{5,7},{6,4},{7,5}} | collective-permute-start | bytes 4718600 | tf_op jit(solution)/shard_map/ppermute | solution.py:121
  18.9 274.4 %collective-permute-start.5 = (bf16[256,3072]{1,0:T(8,128)(2,1)}, bf16[256,3072]{1,0:T(8,128)(2,1)}, u32[]{:S(2)}, u32[]{:S(2)}) collective-permute-start(bf16[256,3072]{1,0:T(8,128)(2,1)} %broadcast_select_fusion.18), channel_id=1, source_target_pairs={{0,2},{1,3},{2,0},{3,1},{4,6},{5,7},{6,4},{7,5}} | collective-permute-start | bytes 4718600 | tf_op jit(solution)/shard_map/ppermute | solution.py:121
  290.6 139.0 %collective-permute-start.8 = (bf16[768,2048]{1,0:T(8,128)(2,1)}, bf16[768,2048]{1,0:T(8,128)(2,1)}, u32[]{:S(2)}, u32[]{:S(2)}) collective-permute-start(bf16[768,2048]{1,0:T(8,128)(2,1)} %param.27), channel_id=1, source_target_pairs={{0,4},{1,5},{2,6},{3,7},{4,0},{5,1},{6,2},{7,3}} | collective-permute-start | bytes 9437192 | tf_op jit(solution)/shard_map/ppermute | solution.py:121
  292.0 130.8 %collective-permute-start.11 = (bf16[768,2048]{1,0:T(8,128)(2,1)}, bf16[768,2048]{1,0:T(8,128)(2,1)}, u32[]{:S(2)}, u32[]{:S(2)}) collective-permute-start(bf16[768,2048]{1,0:T(8,128)(2,1)} %bitcast.7), channel_id=1, source_target_pairs={{0,2},{1,3},{2,0},{3,1},{4,6},{5,7},{6,4},{7,5}} | collective-permute-start | bytes 9437192 | tf_op jit(solution)/shard_map/ppermute | solution.py:121
  359.7 145.9 %collective-permute-start.1 = (bf16[1536,2048]{1,0:T(8,128)(2,1)}, bf16[1536,2048]{1,0:T(8,128)(2,1)}, u32[]{:S(2)}, u32[]{:S(2)}) collective-permute-start(bf16[1536,2048]{1,0:T(8,128)(2,1)} %pad_maximum_fusion.2), channel_id=1, source_target_pairs={{0,1},{1,0},{2,3},{3,2},{4,5},{5,4},{6,7},{7,6}} | collective-permute-start | bytes 18874376 | tf_op jit(solution)/shard_map/ppermute | solution.py:121
  362.6 73.1 %collective-permute-start.4 = (bf16[1024,1536]{1,0:T(8,128)(2,1)}, bf16[1024,1536]{1,0:T(8,128)(2,1)}, u32[]{:S(2)}, u32[]{:S(2)}) collective-permute-start(bf16[1024,1536]{1,0:T(8,128)(2,1)} %pad_maximum_fusion.9), channel_id=1, source_target_pairs={{0,4},{1,5},{2,6},{3,7},{4,0},{5,1},{6,2},{7,3}} | collective-permute-start | bytes 9437192 | tf_op jit(solution)/shard_map/ppermute | solution.py:121
  369.1 131.7 %collective-permute-start.7 = (bf16[1024,1536]{1,0:T(8,128)(2,1)}, bf16[1024,1536]{1,0:T(8,128)(2,1)}, u32[]{:S(2)}, u32[]{:S(2)}) collective-permute-start(bf16[1024,1536]{1,0:T(8,128)(2,1)} %pad_maximum_fusion.10), channel_id=1, source_target_pairs={{0,4},{1,5},{2,6},{3,7},{4,0},{5,1},{6,2},{7,3}} | collective-permute-start | bytes 9437192 | tf_op jit(solution)/shard_map/ppermute | solution.py:121
  429.6 131.7 %collective-permute-start.12 = (bf16[1536,2048]{1,0:T(8,128)(2,1)}, bf16[1536,2048]{1,0:T(8,128)(2,1)}, u32[]{:S(2)}, u32[]{:S(2)}) collective-permute-start(bf16[1536,2048]{1,0:T(8,128)(2,1)} %pad_maximum_fusion.6), channel_id=1, source_target_pairs={{0,1},{1,0},{2,3},{3,2},{4,5},{5,4},{6,7},{7,6}} | collective-permute-start | bytes 18874376 | tf_op jit(solution)/shard_map/ppermute | solution.py:121
  673.3 138.7 %collective-permute-start.14 = (f32[768,2048]{1,0:T(8,128)}, f32[768,2048]{1,0:T(8,128)}, u32[]{:S(2)}, u32[]{:S(2)}) collective-permute-start(f32[768,2048]{1,0:T(8,128)} %slice_add_fusion), channel_id=1, source_target_pairs={{0,2},{1,3},{2,0},{3,1},{4,6},{5,7},{6,4},{7,5}} | collective-permute-start | bytes 18874376 | tf_op jit(solution)/shard_map/ppermute | solution.py:121
  691.6 254.3 %collective-permute-start.10 = (f32[768,2048]{1,0:T(8,128)}, f32[768,2048]{1,0:T(8,128)}, u32[]{:S(2)}, u32[]{:S(2)}) collective-permute-start(f32[768,2048]{1,0:T(8,128)} %slice_add_fusion.2), channel_id=1, source_target_pairs={{0,2},{1,3},{2,0},{3,1},{4,6},{5,7},{6,4},{7,5}} | collective-permute-start | bytes 18874376 | tf_op jit(solution)/shard_map/ppermute | solution.py:121
  1020.4 838.9 %reduce-scatter.9.cloned.1.call-start = ((), (), s32[]{:S(2)}) async-start(), calls=%async_computation.10 | async-start | bytes 9437184 | tf_op jit(solution)/shard_map/reduce_scatter | solution.py:229
  1045.1 814.2 %reduce-scatter.5.cloned.1.call-start = ((), (), s32[]{:S(2)}) async-start(), calls=%async_computation.8 | async-start | bytes 18874368 | tf_op jit(solution)/shard_map/reduce_scatter | solution.py:231
  1171.4 688.0 %reduce-scatter.11.cloned.1.call-start = ((), (), s32[]{:S(2)}) async-start(), calls=%async_computation.11 | async-start | bytes 18874368 | tf_op jit(solution)/shard_map/reduce_scatter | solution.py:226
  1197.5 206.1 %collective-permute-start.18 = (f32[1024,1536]{1,0:T(8,128)}, f32[1024,1536]{1,0:T(8,128)}, u32[]{:S(2)}, u32[]{:S(2)}) collective-permute-start(f32[1024,1536]{1,0:T(8,128)} %fusion.142), channel_id=1, source_target_pairs={{0,4},{1,5},{2,6},{3,7},{4,0},{5,1},{6,2},{7,3}} | collective-permute-start | bytes 18874376 | tf_op jit(solution)/shard_map/ppermute | solution.py:121
  1212.6 387.3 %collective-permute-start.15 = (f32[1024,1536]{1,0:T(8,128)}, f32[1024,1536]{1,0:T(8,128)}, u32[]{:S(2)}, u32[]{:S(2)}) collective-permute-start(f32[1024,1536]{1,0:T(8,128)} %fusion.143), channel_id=1, source_target_pairs={{0,4},{1,5},{2,6},{3,7},{4,0},{5,1},{6,2},{7,3}} | collective-permute-start | bytes 18874376 | tf_op jit(solution)/shard_map/ppermute | solution.py:121
  1231.2 506.3 %collective-permute-start.21 = (f32[768,2048]{1,0:T(8,128)}, f32[768,2048]{1,0:T(8,128)}, u32[]{:S(2)}, u32[]{:S(2)}) collective-permute-start(f32[768,2048]{1,0:T(8,128)} %fusion.67), channel_id=1, source_target_pairs={{0,4},{1,5},{2,6},{3,7},{4,0},{5,1},{6,2},{7,3}} | collective-permute-start | bytes 18874376 | tf_op jit(solution)/shard_map/ppermute | solution.py:121
  1426.3 206.2 %collective-permute-start.19 = (f32[512,1536]{1,0:T(8,128)}, f32[512,1536]{1,0:T(8,128)}, u32[]{:S(2)}, u32[]{:S(2)}) collective-permute-start(f32[512,1536]{1,0:T(8,128)} %fusion.100), channel_id=1, source_target_pairs={{0,1},{1,0},{2,3},{3,2},{4,5},{5,4},{6,7},{7,6}} | collective-permute-start | bytes 9437192 | tf_op jit(solution)/shard_map/ppermute | solution.py:121
  1640.1 116.0 %collective-permute-start.20 = (f32[256,3072]{1,0:T(8,128)}, f32[256,3072]{1,0:T(8,128)}, u32[]{:S(2)}, u32[]{:S(2)}) collective-permute-start(f32[256,3072]{1,0:T(8,128)} %broadcast_select_fusion.10), channel_id=1, source_target_pairs={{0,2},{1,3},{2,0},{3,1},{4,6},{5,7},{6,4},{7,5}} | collective-permute-start | bytes 9437192 | tf_op jit(solution)/shard_map/ppermute | solution.py:121
  1647.2 131.1 %collective-permute-start.17 = (f32[256,3072]{1,0:T(8,128)}, f32[256,3072]{1,0:T(8,128)}, u32[]{:S(2)}, u32[]{:S(2)}) collective-permute-start(f32[256,3072]{1,0:T(8,128)} %broadcast_select_fusion.14), channel_id=1, source_target_pairs={{0,2},{1,3},{2,0},{3,1},{4,6},{5,7},{6,4},{7,5}} | collective-permute-start | bytes 9437192 | tf_op jit(solution)/shard_map/ppermute | solution.py:121
  (149 other events, 3211.8 us)
Sparse Core Ops, SparseCore 0:
  9.8 50.4 all-gather.8
  62.1 47.6 all-gather.4
  111.7 48.6 all-gather.6
  162.1 48.6 all-gather.10
  1020.6 63.9 reduce-scatter.6
  1088.4 63.1 reduce-scatter.8
  1171.5 176.0 reduce-scatter.4
  1437.3 175.9 reduce-scatter.10

commit v2 on v1

--- a/solution.py
+++ b/solution.py
@@ -176,13 +176,16 @@
             return jnp.concatenate(parts, axis=1)
 
         gains = lax.all_gather(jnp.stack([norm1_gain, norm2_gain]), axis_name, axis=1, tiled=True)
+        full_q, full_k, full_v, full_o = gather_rows(w_q), gather_rows(w_k), gather_rows(w_v), gather_rows(w_o)
+        gate_own, down_own, gains = lax.optimization_barrier((w_gate, w_down, gains))
         gain1, gain2 = gains[0].astype(jnp.float32), gains[1].astype(jnp.float32)
-        full_q, full_k, full_v, full_o = gather_rows(w_q), gather_rows(w_k), gather_rows(w_v), gather_rows(w_o)
-        gate_q = quarter_columns(w_gate)
-        up_q = quarter_columns(w_up)
-        down_q = jnp.concatenate(pick(y_bit, w_down, swap(w_down, YDIR)), axis=0)
+        up_own, full_k = lax.optimization_barrier((w_up, full_k))
         dy_flat = grad_out.reshape(tokens, width)
-        dy_row = row_tokens(dy_flat)
+        dy_own, full_q = lax.optimization_barrier((dy_flat, full_q))
+        gate_q = quarter_columns(gate_own)
+        up_q = quarter_columns(up_own)
+        down_q = jnp.concatenate(pick(y_bit, down_own, swap(down_own, YDIR)), axis=0)
+        dy_row = row_tokens(dy_own)
 
         x_float = hidden.reshape(tokens, width).astype(jnp.float32)
         attn_ctx, saved = attention_forward(x_float, positions, (gains[0], q_norm_gain, k_norm_gain, full_q, full_k, full_v), batch_local, seq_len)
@@ -220,20 +223,27 @@
         d_resid = dy_flat.astype(jnp.float32) + norm_backward(d_mlp_in * gain2, r_unit, r_scale)
         d_resid_bf = d_resid.astype(jnp.bfloat16)
         d_attn_ctx = matmul_nt(d_resid_bf, full_o).astype(jnp.bfloat16)
-        down_from_x, d_attn_ctx = lax.optimization_barrier((down_from_x, d_attn_ctx))
+        down_from_x, _ = lax.optimization_barrier((down_from_x, d_attn_ctx))
         down_proj = (down_total + down_from_x).astype(jnp.bfloat16)
         layer_out = (resid_float + down_proj.astype(jnp.float32)).astype(jnp.bfloat16).reshape(hidden.shape)
-        grad_wo = lax.psum_scatter(matmul_tn(attn_ctx, d_resid_bf) * inv_tokens, axis_name, scatter_dimension=0, tiled=True)
+        wo_part = matmul_tn(attn_ctx, d_resid_bf) * inv_tokens
+        wo_part, d_attn_ctx = lax.optimization_barrier((wo_part, d_attn_ctx))
+        grad_wo = lax.psum_scatter(wo_part, axis_name, scatter_dimension=0, tiled=True)
         d_query, d_key, d_value, grad_qgain, grad_kgain = attention_backward(d_attn_ctx, saved, q_norm_gain, k_norm_gain)
         x_unit, x_scale, normed = saved[:3]
-        grad_wv = lax.psum_scatter(matmul_tn(normed, d_value) * inv_tokens, axis_name, scatter_dimension=0, tiled=True)
-        grad_wk = lax.psum_scatter(matmul_tn(normed, d_key) * inv_tokens, axis_name, scatter_dimension=0, tiled=True)
-        grad_wq = lax.psum_scatter(matmul_tn(normed, d_query) * inv_tokens, axis_name, scatter_dimension=0, tiled=True)
+        wv_part = matmul_tn(normed, d_value) * inv_tokens
+        grad_wv = lax.psum_scatter(wv_part, axis_name, scatter_dimension=0, tiled=True)
+        wk_part = matmul_tn(normed, d_key) * inv_tokens
+        grad_wk = lax.psum_scatter(wk_part, axis_name, scatter_dimension=0, tiled=True)
+        wq_part = matmul_tn(normed, d_query) * inv_tokens
+        grad_wq = lax.psum_scatter(wq_part, axis_name, scatter_dimension=0, tiled=True)
         d_normed = matmul_nt(d_query, full_q) + matmul_nt(d_key, full_k) + matmul_nt(d_value, full_v)
         grad_norm1 = jnp.sum(d_normed * x_unit, axis=0)
         d_hidden = (d_resid + norm_backward(d_normed * gain1, x_unit, x_scale)).astype(jnp.bfloat16).reshape(hidden.shape)
 
-        small = lax.psum(jnp.concatenate([grad_norm1, grad_norm2, grad_qgain, grad_kgain]) * inv_tokens, axis_name)
+        small = jnp.concatenate([grad_norm1, grad_norm2, grad_qgain, grad_kgain]) * inv_tokens
+        for mask in (CORE, XDIR, YDIR):
+            small = small + swap(small, mask)
         head_dim = q_norm_gain.shape[0]
         own1 = lax.dynamic_slice_in_dim(small, me * rows, rows)
         own2 = lax.dynamic_slice_in_dim(small, width + me * rows, rows)

time: 1870 us -> 1920 us (1.027)
  waiting for transfers between devices: 826 us -> 962 us
  blocking collectives: 125 us -> 12.3 us
  local copies, waits for them, and re-layouts: 187 us -> 212 us
    ppermute x22 -> x25, waiting for transfers between devices: 821 us -> 915 us  [swap(): lax.ppermute(value, axis_name, [(j, j ^ mask) for j in range(group_size)])]
    all_gather x1, blocking collectives: 101 us -> 12.3 us  [device_step(): lax.all_gather(jnp.stack([norm1_gain, norm2_gain]), axis_name, axis=1, ti...]
    all_gather x4, waiting for transfers between devices: 1.84 us -> 44.1 us  [gather_rows(): return lax.all_gather(row_shard, axis_name, axis=0, tiled=True)]
    psum x1 -> x0, blocking collectives: 23.6 us -> none  [device_step(): lax.psum(jnp.concatenate([grad_norm1, grad_norm2, grad_qgain, grad_kgain]...]
    unnamed x304 -> x280, local copies, waits for them, and re-layouts: 34.6 us -> 44.9 us
  transfers between devices with their start and end apart: 30 -> 33, of which waited for: 10 -> 13; matrix products, arithmetic and copies ran while one was open for 38% -> 35% of each run, Pallas kernels for 0% -> 0%
where the time goes in v2:
time: 1920 us; the launch traced here: 1910 us
  waiting for transfers between devices  962 us (50%)
  matrix products  494 us (26%)
  local copies, waits for them, and re-layouts  212 us (11%)
  other arithmetic  197 us (10%)
  starting transfers between devices  19.2 us (1%)
    ppermute x25, waiting for transfers between devices, swap(): lax.ppermute(value, axis_name, [(j, j ^ mask) for j in range(group_size)])  915 us
    dot_general x11, matrix products, matmul_nt(): lax.dot_general(left_op, right_op, (((1,), (1,)), ((), ())), preferred_el...  156 us
    dot_general x10, matrix products, matmul_tn(): lax.dot_general(left_op, right_op, (((0,), (0,)), ((), ())), preferred_el...  138 us
    dot_general x9, matrix products, matmul(): return jnp.dot(left_op, right_op, preferred_element_type=jnp.float32)  122 us
    unnamed x280, local copies, waits for them, and re-layouts  44.9 us
    all_gather x4, waiting for transfers between devices, gather_rows(): return lax.all_gather(row_shard, axis_name, axis=0, tiled=True)  44.1 us
  transfers between devices with their start and end apart: 33, of which 13 were waited for; matrix products, arithmetic and copies ran while one was open for 35% of the time, Pallas kernels for 0%

profile of v2, /device:TPU:0, one launch (start us, length us, event | category | flops | bytes accessed | tf_op | source)
XLA Modules:
  0.0 1913.4 jit_solution(3585683189386309352)
XLA Ops:
  36.7 44.0 %collective-permute-done.2 = bf16[256,3072]{1,0:T(8,128)(2,1)} collective-permute-done((bf16[256,3072]{1,0:T(8,128)(2,1)}, bf16[256,3072]{1,0:T(8,128)(2,1)}, u32[]{:S(2)}, u32[]{:S(2)}) %collective-permute-start.2) | collective-permute-done | bytes 1572896 | tf_op jit(solution)/shard_map/ppermute | solution.py:121
  121.9 44.1 %all-gather.7.cloned.1.call-done = bf16[2048,2048]{1,0:T(8,128)(2,1)} async-done(((bf16[256,2048]{1,0:T(8,128)(2,1)}), bf16[2048,2048]{1,0:T(8,128)(2,1)}) %all-gather.7.cloned.1.call-update) | async-done | bytes 8388624 | tf_op jit(solution)/shard_map/all_gather | solution.py:124
  304.5 56.4 %collective-permute-done = bf16[768,2048]{1,0:T(8,128)(2,1)S(1)} collective-permute-done((bf16[768,2048]{1,0:T(8,128)(2,1)S(1)}, bf16[768,2048]{1,0:T(8,128)(2,1)S(1)}, u32[]{:S(2)}, u32[]{:S(2)}) %collective-permute-start) | collective-permute-done | bytes 3145760 | tf_op jit(solution)/shard_map/ppermute | solution.py:121
  378.1 52.3 %collective-permute-done.4 = bf16[1024,1536]{1,0:T(8,128)(2,1)} collective-permute-done((bf16[1024,1536]{1,0:T(8,128)(2,1)}, bf16[1024,1536]{1,0:T(8,128)(2,1)}, u32[]{:S(2)}, u32[]{:S(2)}) %collective-permute-start.4) | collective-permute-done | bytes 3145760 | tf_op jit(solution)/shard_map/ppermute | solution.py:121
  435.1 61.6 %collective-permute-done.7 = bf16[1024,1536]{1,0:T(8,128)(2,1)} collective-permute-done((bf16[1024,1536]{1,0:T(8,128)(2,1)}, bf16[1024,1536]{1,0:T(8,128)(2,1)}, u32[]{:S(2)}, u32[]{:S(2)}) %collective-permute-start.7) | collective-permute-done | bytes 3145760 | tf_op jit(solution)/shard_map/ppermute | solution.py:121
  516.2 28.1 %convolution_convert_fusion.1 = bf16[3072,1536]{1,0:T(8,128)(2,1)} fusion(bf16[1024,1536]{1,0:T(8,128)(2,1)} %get-tuple-element.70, bf16[1024,1536]{1,0:T(8,128)(2,1)} %get-tuple-element.69, bf16[1536,2048]{1,0:T(8,128)(2,1)} %collective-permute-done.1, bf16[768,2048]{1,0:T(8,128)(2,1)} %copy-done.24, bf16[768,2048]{1,0:T(8,128)(2,1)S(1)} %fusion.20), kind=kOutput, calls=%fused_computation.25 | convolution fusion | flops 19382403072 | bytes 28311552 | tf_op jit(solution)/shard_map/dot_general | solution.py:25
  544.2 27.7 %convolution_convert_fusion = bf16[3072,1536]{1,0:T(8,128)(2,1)} fusion(bf16[1024,1536]{1,0:T(8,128)(2,1)} %get-tuple-element.72, bf16[1024,1536]{1,0:T(8,128)(2,1)} %get-tuple-element.71, bf16[1536,2048]{1,0:T(8,128)(2,1)} %collective-permute-done.1, bf16[768,2048]{1,0:T(8,128)(2,1)} %copy-done.24, bf16[768,2048]{1,0:T(8,128)(2,1)S(1)} %fusion.20), kind=kOutput, calls=%fused_computation.24 | convolution fusion | flops 19382403072 | bytes 28311552 | tf_op jit(solution)/shard_map/dot_general | solution.py:25
  578.7 41.1 %fusion.5 = (bf16[3072,1536]{1,0:T(8,128)(2,1)}, bf16[3072,1536]{1,0:T(8,128)(2,1)}, bf16[3072,1536]{1,0:T(8,128)(2,1)}) fusion(bf16[3072,1536]{1,0:T(8,128)(2,1)} %convolution_convert_fusion, bf16[3072,1536]{1,0:T(8,128)(2,1)} %convolution_convert_fusion.1, bf16[3072,2048]{1,0:T(8,128)(2,1)} %constant_dynamic-update-slice_fusion, ...), kind=kOutput, calls=%fused_computation.11 | convolution fusion | flops 19424870400 | bytes 66060288 | tf_op jit(solution)/shard_map/dot_general | solution.py:33
  619.8 16.6 fusion.62
  636.4 17.5 convolution_add_fusion
  711.6 112.5 %collective-permute-done.14 = f32[768,2048]{1,0:T(8,128)} collective-permute-done((f32[768,2048]{1,0:T(8,128)}, f32[768,2048]{1,0:T(8,128)}, u32[]{:S(2)}, u32[]{:S(2)}) %collective-permute-start.14) | collective-permute-done | bytes 6291488 | tf_op jit(solution)/shard_map/ppermute | solution.py:121
  882.1 19.6 %fusion.116 = f32[3,256,8,128]{1,3,2,0:T(8,128)} fusion(bf16[3,256,8,2,128]{1,4,3,2,0:T(8,128)(2,1)S(1)} %copy-done.73, f32[3,8,256,2,256]{2,4,3,1,0:T(8,128)} %fusion.138, f32[3,8,256,2,256]{2,4,3,1,0:T(8,128)} %get-tuple-element.120, f32[3,8,256,2]{2,3,1,0:T(2,128)} %copy-done.125), kind=kOutput, calls=%fused_computation.208 | convolution fusion | flops 827339008 | bytes 31506432 | tf_op jit(solution)/shard_map/bksgt,bskgd->btkd/dot_general | solution.py:102
  973.6 20.8 %fusion.97 = f32[3,256,8,2,128]{1,4,3,2,0:T(8,128)} fusion(bf16[3,256,8,128,1]{1,3,4,2,0:T(8,128)(2,1)S(1)} %copy-done.90, f32[3,8,256,2,256]{2,4,3,1,0:T(8,128)} %fusion.138, f32[3,8,256,2,256]{2,4,3,1,0:T(8,128)} %get-tuple-element.120, f32[3,8,256,2]{2,3,1,0:T(2,128)S(1)} %copy-done.127), kind=kOutput, calls=%fused_computation.193 | convolution fusion | flops 827339008 | bytes 33079296 | tf_op jit(solution)/shard_map/bksgt,btkd->bskgd/dot_general | solution.py:101
  1058.0 17.4 fusion.30
  1097.6 16.8 fusion.142
  1130.1 17.8 fusion.67
  1172.8 147.7 %collective-permute-done.21 = f32[1024,1536]{1,0:T(8,128)} collective-permute-done((f32[1024,1536]{1,0:T(8,128)}, f32[1024,1536]{1,0:T(8,128)}, u32[]{:S(2)}, u32[]{:S(2)}) %collective-permute-start.21) | collective-permute-done | bytes 6291488 | tf_op jit(solution)/shard_map/ppermute | solution.py:121
  1320.5 16.7 convolution_add_fusion.1
  1348.7 174.0 %collective-permute-done.18 = f32[1024,1536]{1,0:T(8,128)} collective-permute-done((f32[1024,1536]{1,0:T(8,128)}, f32[1024,1536]{1,0:T(8,128)}, u32[]{:S(2)}, u32[]{:S(2)}) %collective-permute-start.18) | collective-permute-done | bytes 6291488 | tf_op jit(solution)/shard_map/ppermute | solution.py:121
  1522.7 18.5 convolution_add_fusion.2
  1550.8 104.5 %collective-permute-done.24 = f32[768,2048]{1,0:T(8,128)} collective-permute-done((f32[768,2048]{1,0:T(8,128)}, f32[768,2048]{1,0:T(8,128)}, u32[]{:S(2)}, u32[]{:S(2)}) %collective-permute-start.24) | collective-permute-done | bytes 6291488 | tf_op jit(solution)/shard_map/ppermute | solution.py:121
  1655.3 18.7 add_multiply_fusion
  1692.7 55.7 %collective-permute-done.20 = f32[256,3072]{1,0:T(8,128)S(1)} collective-permute-done((f32[256,3072]{1,0:T(8,128)S(1)}, f32[256,3072]{1,0:T(8,128)S(1)}, u32[]{:S(2)}, u32[]{:S(2)}) %collective-permute-start.20) | collective-permute-done | bytes 3145760 | tf_op jit(solution)/shard_map/ppermute | solution.py:121
  1783.6 96.6 %collective-permute-done.10 = f32[768,2048]{1,0:T(8,128)} collective-permute-done((f32[768,2048]{1,0:T(8,128)}, f32[768,2048]{1,0:T(8,128)}, u32[]{:S(2)}, u32[]{:S(2)}) %collective-permute-start.10) | collective-permute-done | bytes 6291488 | tf_op jit(solution)/shard_map/ppermute | solution.py:121
  (501 shorter events, 670.7 us)
Async XLA Ops:
  7.9 94.1 %all-gather.5.cloned.1.call-start = ((), (), s32[]{:S(2)}) async-start(), calls=%async_computation.4 | async-start | bytes 4718592 | tf_op jit(solution)/shard_map/all_gather | solution.py:124
  8.7 157.4 %all-gather.7.cloned.1.call-start = ((), (), s32[]{:S(2)}) async-start(), calls=%async_computation.5 | async-start | bytes 9437184 | tf_op jit(solution)/shard_map/all_gather | solution.py:124
  9.4 269.1 %all-gather.11.cloned.1.call-start = ((), (), s32[]{:S(2)}) async-start(), calls=%async_computation.7 | async-start | bytes 9437184 | tf_op jit(solution)/shard_map/all_gather | solution.py:124
  28.3 1878.0 %reduce-scatter.7.cloned.1.call-start = ((), (), s32[]{:S(2)}) async-start(), calls=%async_computation.9 | async-start | bytes 9437184 | tf_op jit(solution)/shard_map/reduce_scatter | solution.py:237
  85.6 207.7 %collective-permute-start.3 = (bf16[512,1536]{1,0:T(8,128)(2,1)}, bf16[512,1536]{1,0:T(8,128)(2,1)}, u32[]{:S(2)}, u32[]{:S(2)}) collective-permute-start(bf16[512,1536]{1,0:T(8,128)(2,1)} %get-tuple-element.42), channel_id=1, source_target_pairs={{0,1},{1,0},{2,3},{3,2},{4,5},{5,4},{6,7},{7,6}} | collective-permute-start | bytes 4718600 | tf_op jit(solution)/shard_map/ppermute | solution.py:121
  112.4 183.1 %collective-permute-start.5 = (bf16[256,3072]{1,0:T(8,128)(2,1)}, bf16[256,3072]{1,0:T(8,128)(2,1)}, u32[]{:S(2)}, u32[]{:S(2)}) collective-permute-start(bf16[256,3072]{1,0:T(8,128)(2,1)} %broadcast_select_fusion.18), channel_id=1, source_target_pairs={{0,2},{1,3},{2,0},{3,1},{4,6},{5,7},{6,4},{7,5}} | collective-permute-start | bytes 4718600 | tf_op jit(solution)/shard_map/ppermute | solution.py:121
  291.7 80.3 %collective-permute-start.8 = (bf16[768,2048]{1,0:T(8,128)(2,1)}, bf16[768,2048]{1,0:T(8,128)(2,1)}, u32[]{:S(2)}, u32[]{:S(2)}) collective-permute-start(bf16[768,2048]{1,0:T(8,128)(2,1)} %param.27), channel_id=1, source_target_pairs={{0,4},{1,5},{2,6},{3,7},{4,0},{5,1},{6,2},{7,3}} | collective-permute-start | bytes 9437192 | tf_op jit(solution)/shard_map/ppermute | solution.py:121
  303.2 127.2 %collective-permute-start.4 = (bf16[1024,1536]{1,0:T(8,128)(2,1)}, bf16[1024,1536]{1,0:T(8,128)(2,1)}, u32[]{:S(2)}, u32[]{:S(2)}) collective-permute-start(bf16[1024,1536]{1,0:T(8,128)(2,1)} %pad_maximum_fusion.8), channel_id=1, source_target_pairs={{0,4},{1,5},{2,6},{3,7},{4,0},{5,1},{6,2},{7,3}} | collective-permute-start | bytes 9437192 | tf_op jit(solution)/shard_map/ppermute | solution.py:121
  364.7 151.5 %collective-permute-start.1 = (bf16[1536,2048]{1,0:T(8,128)(2,1)}, bf16[1536,2048]{1,0:T(8,128)(2,1)}, u32[]{:S(2)}, u32[]{:S(2)}) collective-permute-start(bf16[1536,2048]{1,0:T(8,128)(2,1)} %pad_maximum_fusion.1), channel_id=1, source_target_pairs={{0,1},{1,0},{2,3},{3,2},{4,5},{5,4},{6,7},{7,6}} | collective-permute-start | bytes 18874376 | tf_op jit(solution)/shard_map/ppermute | solution.py:121
  369.7 127.1 %collective-permute-start.7 = (bf16[1024,1536]{1,0:T(8,128)(2,1)}, bf16[1024,1536]{1,0:T(8,128)(2,1)}, u32[]{:S(2)}, u32[]{:S(2)}) collective-permute-start(bf16[1024,1536]{1,0:T(8,128)(2,1)} %pad_maximum_fusion.9), channel_id=1, source_target_pairs={{0,4},{1,5},{2,6},{3,7},{4,0},{5,1},{6,2},{7,3}} | collective-permute-start | bytes 9437192 | tf_op jit(solution)/shard_map/ppermute | solution.py:121
  371.1 134.4 %collective-permute-start.11 = (bf16[768,2048]{1,0:T(8,128)(2,1)}, bf16[768,2048]{1,0:T(8,128)(2,1)}, u32[]{:S(2)}, u32[]{:S(2)}) collective-permute-start(bf16[768,2048]{1,0:T(8,128)(2,1)} %bitcast.3), channel_id=1, source_target_pairs={{0,2},{1,3},{2,0},{3,1},{4,6},{5,7},{6,4},{7,5}} | collective-permute-start | bytes 9437192 | tf_op jit(solution)/shard_map/ppermute | solution.py:121
  686.1 138.1 %collective-permute-start.14 = (f32[768,2048]{1,0:T(8,128)}, f32[768,2048]{1,0:T(8,128)}, u32[]{:S(2)}, u32[]{:S(2)}) collective-permute-start(f32[768,2048]{1,0:T(8,128)} %slice_add_fusion), channel_id=1, source_target_pairs={{0,2},{1,3},{2,0},{3,1},{4,6},{5,7},{6,4},{7,5}} | collective-permute-start | bytes 18874376 | tf_op jit(solution)/shard_map/ppermute | solution.py:121
  937.1 969.2 %reduce-scatter.9.cloned.1.call-start = ((), (), s32[]{:S(2)}) async-start(), calls=%async_computation.10 | async-start | bytes 9437184 | tf_op jit(solution)/shard_map/reduce_scatter | solution.py:235
  962.8 943.5 %reduce-scatter.5.cloned.1.call-start = ((), (), s32[]{:S(2)}) async-start(), calls=%async_computation.8 | async-start | bytes 18874368 | tf_op jit(solution)/shard_map/reduce_scatter | solution.py:239
  1087.9 818.4 %reduce-scatter.11.cloned.1.call-start = ((), (), s32[]{:S(2)}) async-start(), calls=%async_computation.11 | async-start | bytes 18874368 | tf_op jit(solution)/shard_map/reduce_scatter | solution.py:231
  1114.4 206.1 %collective-permute-start.21 = (f32[1024,1536]{1,0:T(8,128)}, f32[1024,1536]{1,0:T(8,128)}, u32[]{:S(2)}, u32[]{:S(2)}) collective-permute-start(f32[1024,1536]{1,0:T(8,128)} %fusion.142), channel_id=1, source_target_pairs={{0,4},{1,5},{2,6},{3,7},{4,0},{5,1},{6,2},{7,3}} | collective-permute-start | bytes 18874376 | tf_op jit(solution)/shard_map/ppermute | solution.py:121
  1129.5 393.2 %collective-permute-start.18 = (f32[1024,1536]{1,0:T(8,128)}, f32[1024,1536]{1,0:T(8,128)}, u32[]{:S(2)}, u32[]{:S(2)}) collective-permute-start(f32[1024,1536]{1,0:T(8,128)} %fusion.143), channel_id=1, source_target_pairs={{0,4},{1,5},{2,6},{3,7},{4,0},{5,1},{6,2},{7,3}} | collective-permute-start | bytes 18874376 | tf_op jit(solution)/shard_map/ppermute | solution.py:121
  1148.0 507.3 %collective-permute-start.24 = (f32[768,2048]{1,0:T(8,128)}, f32[768,2048]{1,0:T(8,128)}, u32[]{:S(2)}, u32[]{:S(2)}) collective-permute-start(f32[768,2048]{1,0:T(8,128)} %fusion.67), channel_id=1, source_target_pairs={{0,4},{1,5},{2,6},{3,7},{4,0},{5,1},{6,2},{7,3}} | collective-permute-start | bytes 18874376 | tf_op jit(solution)/shard_map/ppermute | solution.py:121
  1164.3 513.8 %collective-permute-start.9 = (f32[1536,2048]{1,0:T(8,128)}, f32[1536,2048]{1,0:T(8,128)}, u32[]{:S(2)}, u32[]{:S(2)}) collective-permute-start(f32[1536,2048]{1,0:T(8,128)} %fusion.65), channel_id=1, source_target_pairs={{0,1},{1,0},{2,3},{3,2},{4,5},{5,4},{6,7},{7,6}} | collective-permute-start | bytes 37748744 | tf_op jit(solution)/shard_map/ppermute | solution.py:121
  1348.7 195.4 %collective-permute-start.22 = (f32[512,1536]{1,0:T(8,128)}, f32[512,1536]{1,0:T(8,128)}, u32[]{:S(2)}, u32[]{:S(2)}) collective-permute-start(f32[512,1536]{1,0:T(8,128)} %fusion.100), channel_id=1, source_target_pairs={{0,1},{1,0},{2,3},{3,2},{4,5},{5,4},{6,7},{7,6}} | collective-permute-start | bytes 9437192 | tf_op jit(solution)/shard_map/ppermute | solution.py:121
  1544.1 130.0 %collective-permute-start.19 = (f32[512,1536]{1,0:T(8,128)}, f32[512,1536]{1,0:T(8,128)}, u32[]{:S(2)}, u32[]{:S(2)}) collective-permute-start(f32[512,1536]{1,0:T(8,128)} %fusion.102), channel_id=1, source_target_pairs={{0,1},{1,0},{2,3},{3,2},{4,5},{5,4},{6,7},{7,6}} | collective-permute-start | bytes 9437192 | tf_op jit(solution)/shard_map/ppermute | solution.py:121
  1550.7 139.2 %collective-permute-start.23 = (f32[256,3072]{1,0:T(8,128)}, f32[256,3072]{1,0:T(8,128)}, u32[]{:S(2)}, u32[]{:S(2)}) collective-permute-start(f32[256,3072]{1,0:T(8,128)} %broadcast_select_fusion.10), channel_id=1, source_target_pairs={{0,2},{1,3},{2,0},{3,1},{4,6},{5,7},{6,4},{7,5}} | collective-permute-start | bytes 9437192 | tf_op jit(solution)/shard_map/ppermute | solution.py:121
  1689.3 190.9 %collective-permute-start.10 = (f32[768,2048]{1,0:T(8,128)}, f32[768,2048]{1,0:T(8,128)}, u32[]{:S(2)}, u32[]{:S(2)}) collective-permute-start(f32[768,2048]{1,0:T(8,128)} %slice_add_fusion.2), channel_id=1, source_target_pairs={{0,2},{1,3},{2,0},{3,1},{4,6},{5,7},{6,4},{7,5}} | collective-permute-start | bytes 18874376 | tf_op jit(solution)/shard_map/ppermute | solution.py:121
  1783.5 107.3 %collective-permute-start.15 = (f32[4352]{0:T(1024)S(1)}, f32[4352]{0:T(1024)S(1)}, u32[]{:S(2)}, u32[]{:S(2)}) collective-permute-start(f32[4352]{0:T(1024)S(1)} %maximum_multiply_fusion.2), channel_id=1, source_target_pairs={{0,1},{1,0},{2,3},{3,2},{4,5},{5,4},{6,7},{7,6}} | collective-permute-start | bytes 52232 | tf_op jit(solution)/shard_map/ppermute | solution.py:121
  (139 other events, 3604.0 us)
Sparse Core Ops, SparseCore 0:
  9.8 44.9 all-gather.8
  56.7 36.5 all-gather.4
  95.1 70.9 all-gather.6
  167.7 48.6 all-gather.10
  937.2 63.5 reduce-scatter.6
  1004.7 63.1 reduce-scatter.8
  1088.1 175.2 reduce-scatter.4
  1342.2 175.8 reduce-scatter.10

commit v3 on v2

v3 whole, which is shorter than its diff:
```python
import jax
import jax.numpy as jnp
from jax import lax
from jax.experimental import pallas as pl
from jax.experimental.pallas import tpu as pltpu
from jax.sharding import PartitionSpec as P


RMS_EPS = 1e-6
ROPE_THETA = 1000000.0
NEG = -1e30


def rms_scale(tensor):
    return lax.rsqrt(jnp.mean(tensor * tensor, axis=-1, keepdims=True) + RMS_EPS)


def norm_backward(d_unit, unit_val, scale_val):
    return scale_val * (d_unit - unit_val * jnp.mean(d_unit * unit_val, axis=-1, keepdims=True))


def matmul(left_op, right_op):
    return jnp.dot(left_op, right_op, preferred_element_type=jnp.float32)


def matmul_tn(left_op, right_op):
    return lax.dot_general(left_op, right_op, (((0,), (0,)), ((), ())), preferred_element_type=jnp.float32)


def matmul_nt(left_op, right_op):
    return lax.dot_general(left_op, right_op, (((1,), (1,)), ((), ())), preferred_element_type=jnp.float32)


def rope_tables(positions, head_dim):
    inv_freq = ROPE_THETA ** (-2.0 * jnp.arange(head_dim // 2, dtype=jnp.float32) / head_dim)
    rope_angle = positions.reshape(-1, 1).astype(jnp.float32) * inv_freq
    cos_half = jnp.cos(rope_angle)
    sin_half = jnp.sin(rope_angle)
    return jnp.concatenate([cos_half, cos_half], axis=-1), jnp.concatenate([-sin_half, sin_half], axis=-1)


def half_turn(tensor):
    return pltpu.roll(tensor, tensor.shape[-1] // 2, 1)


def head_unit(projected):
    heads = projected.astype(jnp.float32)
    scale = rms_scale(heads)
    return heads * scale, scale


def head_rope(unit, gain, cos_t, sin_t):
    scaled = unit * gain
    return (scaled * cos_t + half_turn(scaled) * sin_t).astype(jnp.bfloat16)


def head_backward(d_rot, unit, scale, gain, cos_t, sin_t):
    d_scaled = d_rot * cos_t + half_turn(d_rot * sin_t)
    d_gain = jnp.sum((d_scaled * unit).reshape(-1, 8, d_rot.shape[-1]), axis=0)
    return norm_backward(d_scaled * gain, unit, scale).astype(jnp.bfloat16), d_gain


def head_probs(q_rot, k_rot):
    seq_len, head_dim = q_rot.shape
    scores = matmul_nt(q_rot, k_rot) * (head_dim ** -0.5)
    query = lax.broadcasted_iota(jnp.int32, (seq_len, seq_len), 0)
    key = lax.broadcasted_iota(jnp.int32, (seq_len, seq_len), 1)
    scores = jnp.where(query >= key, scores, NEG)
    weight = jnp.exp(scores - jnp.max(scores, axis=-1, keepdims=True))
    return weight / jnp.sum(weight, axis=-1, keepdims=True)


def attention_forward_kernel(q_ref, k_ref, v_ref, cos_ref, sin_ref, qg_ref, kg_ref, ctx_ref):
    head_dim = k_ref.shape[1]
    cos_t, sin_t = cos_ref[...], sin_ref[...]
    q_gain, k_gain = qg_ref[...].astype(jnp.float32), kg_ref[...].astype(jnp.float32)
    k_rot = head_rope(head_unit(k_ref[...])[0], k_gain, cos_t, sin_t)
    for g in range(q_ref.shape[1] // head_dim):
        cols = slice(g * head_dim, (g + 1) * head_dim)
        q_rot = head_rope(head_unit(q_ref[:, cols])[0], q_gain, cos_t, sin_t)
        probs = head_probs(q_rot, k_rot).astype(jnp.bfloat16)
        ctx_ref[:, cols] = matmul(probs, v_ref[...]).astype(jnp.bfloat16)


def attention_backward_kernel(d_ref, q_ref, k_ref, v_ref, cos_ref, sin_ref, qg_ref, kg_ref, dq_ref, dk_ref, dv_ref, dqg_ref, dkg_ref):
    head_dim = k_ref.shape[1]
    cos_t, sin_t = cos_ref[...], sin_ref[...]
    q_gain, k_gain = qg_ref[...].astype(jnp.float32), kg_ref[...].astype(jnp.float32)
    k_unit, k_scale = head_unit(k_ref[...])
    k_rot = head_rope(k_unit, k_gain, cos_t, sin_t)
    d_k_rot = d_value = d_q_gain = 0.0
    for g in range(q_ref.shape[1] // head_dim):
        cols = slice(g * head_dim, (g + 1) * head_dim)
        q_unit, q_scale = head_unit(q_ref[:, cols])
        q_rot = head_rope(q_unit, q_gain, cos_t, sin_t)
        probs = head_probs(q_rot, k_rot)
        d_ctx = d_ref[:, cols]
        d_value = d_value + matmul_tn(probs.astype(jnp.bfloat16), d_ctx)
        d_probs = matmul_nt(d_ctx, v_ref[...])
        d_scores = probs * (d_probs - jnp.sum(probs * d_probs, axis=-1, keepdims=True))
        d_scores = (d_scores * (head_dim ** -0.5)).astype(jnp.bfloat16)
        d_k_rot = d_k_rot + matmul_tn(d_scores, q_rot)
        dq_ref[:, cols], part = head_backward(matmul(d_scores, k_rot), q_unit, q_scale, q_gain, cos_t, sin_t)
        d_q_gain = d_q_gain + part
    dqg_ref[...] = d_q_gain
    dk_ref[...], dkg_ref[...] = head_backward(d_k_rot, k_unit, k_scale, k_gain, cos_t, sin_t)
    dv_ref[...] = d_value.astype(jnp.bfloat16)


def attention_specs(q_proj, k_proj, seq_len, head_dim):
    tokens = q_proj.shape[0]
    kv_heads = k_proj.shape[1] // head_dim
    q_spec = pl.BlockSpec((seq_len, q_proj.shape[1] // kv_heads), lambda b, h: (b, h))
    k_spec = pl.BlockSpec((seq_len, head_dim), lambda b, h: (b, h))
    t_spec = pl.BlockSpec((seq_len, head_dim), lambda b, h: (b, 0))
    g_spec = pl.BlockSpec((1, head_dim), lambda b, h: (0, 0))
    return (tokens // seq_len, kv_heads), q_spec, k_spec, [q_spec, k_spec, k_spec, t_spec, t_spec, g_spec, g_spec]


def attention_forward(operands, seq_len):
    q_proj, k_proj, head_dim = operands[0], operands[1], operands[3].shape[1]
    grid, q_spec, _, in_specs = attention_specs(q_proj, k_proj, seq_len, head_dim)
    return pl.pallas_call(
        attention_forward_kernel, grid=grid, in_specs=in_specs, out_specs=q_spec,
        out_shape=jax.ShapeDtypeStruct(q_proj.shape, jnp.bfloat16),
        cost_estimate=pl.CostEstimate(flops=4 * q_proj.size * seq_len, bytes_accessed=8 * q_proj.size, transcendentals=0),
        name="attn_fwd",
    )(*operands)


def attention_backward(d_ctx, operands, seq_len):
    q_proj, k_proj, head_dim = operands[0], operands[1], operands[3].shape[1]
    grid, q_spec, k_spec, in_specs = attention_specs(q_proj, k_proj, seq_len, head_dim)
    gain_spec = pl.BlockSpec((8, head_dim), lambda b, h: (b * grid[1] + h, 0))
    gain_shape = jax.ShapeDtypeStruct((8 * grid[0] * grid[1], head_dim), jnp.float32)
    dq, dk, dv, dqg, dkg = pl.pallas_call(
        attention_backward_kernel, grid=grid, in_specs=[q_spec] + in_specs,
        out_specs=[q_spec, k_spec, k_spec, gain_spec, gain_spec],
        out_shape=[jax.ShapeDtypeStruct(q_proj.shape, jnp.bfloat16)] + [jax.ShapeDtypeStruct(k_proj.shape, jnp.bfloat16)] * 2 + [gain_shape] * 2,
        cost_estimate=pl.CostEstimate(flops=10 * q_proj.size * seq_len, bytes_accessed=12 * q_proj.size, transcendentals=0),
        name="attn_bwd",
    )(d_ctx, *operands)
    return dq, dk, dv, jnp.sum(dqg, axis=0), jnp.sum(dkg, axis=0)


def pick(bit, first, second):
    return jnp.where(bit == 0, first, second), jnp.where(bit == 0, second, first)


def solution(mesh):
    axis_name = mesh.axis_names[0]
    group_size = mesh.shape[axis_name]
    sharded = P(axis_name)
    in_specs = (sharded, sharded, sharded, sharded, sharded, P(), P()) + (sharded,) * 7
    out_specs = (sharded, sharded, sharded, sharded, P(), P()) + (sharded,) * 7
    CORE, XDIR, YDIR = 1, 2, 4

    def swap(value, mask):
        return lax.ppermute(value, axis_name, [(j, j ^ mask) for j in range(group_size)])

    def gather_rows(row_shard):
        return lax.all_gather(row_shard, axis_name, axis=0, tiled=True)

    def device_step(hidden, grad_out, positions, norm1_gain, norm2_gain, q_norm_gain, k_norm_gain, w_q, w_k, w_v, w_o, w_gate, w_up, w_down):
        batch_local, seq_len, width = hidden.shape
        tokens = batch_local * seq_len
        me = lax.axis_index(axis_name)
        c_bit, x_bit, y_bit = me % 2, (me // 2) % 2, me // 4
        ff_block = w_down.shape[0]
        rows = w_gate.shape[0]

        def row_tokens(own):
            far = swap(own, XDIR)
            near = jnp.concatenate([own, swap(own, CORE)], axis=0)
            return near, jnp.concatenate([far, swap(far, CORE)], axis=0)

        def quarter_columns(shard):
            blk = [shard[:, j * ff_block:(j + 1) * ff_block] for j in range(8)]
            first = jnp.concatenate([blk[0], blk[1], blk[4], blk[5]], axis=1)
            second = jnp.concatenate([blk[2], blk[3], blk[6], blk[7]], axis=1)
            keep, send = pick(x_bit, first, second)
            got = swap(send, XDIR)
            row0, row1 = pick(x_bit, keep, got)
            both = jnp.concatenate([row0, row1], axis=0)
            col = [both[:, j * ff_block:(j + 1) * ff_block] for j in range(4)]
            keep, send = pick(c_bit, jnp.concatenate([col[0], col[2]], axis=1), jnp.concatenate([col[1], col[3]], axis=1))
            got = swap(send, CORE)
            core0, core1 = pick(c_bit, keep, got)
            four = jnp.concatenate([core0[:rows], core1[:rows], core0[rows:], core1[rows:]], axis=0)
            got = swap(four, YDIR)
            return jnp.concatenate(pick(y_bit, four, got), axis=0)

        def far_sum(partial_rows):
            part = partial_rows(1, tokens, 2 * tokens)
            part = swap(part, CORE)
            return partial_rows(1, 0, tokens) + part

        def near_sum(partial_rows):
            part = partial_rows(0, tokens, 2 * tokens)
            part = swap(part, CORE)
            return partial_rows(0, 0, tokens) + part

        def token_product(left, right):
            return matmul_tn(left[0], right[0]) + matmul_tn(left[1], right[1])

        def scatter_columns(left_send, left_keep, right):
            part = token_product(left_send, right)
            got = swap(part, YDIR)
            mine = token_product(left_keep, right) + got
            blk = [mine[j * rows:(j + 1) * rows] for j in range(4)]
            keep, send = pick(c_bit, jnp.concatenate([blk[0], blk[2]], axis=0), jnp.concatenate([blk[1], blk[3]], axis=0))
            got = swap(send, CORE)
            core0, core1 = pick(c_bit, keep, got)
            both = jnp.concatenate([core0, core1], axis=1)
            keep, send = pick(x_bit, both[:rows], both[rows:])
            got = swap(send, XDIR)
            x0, x1 = pick(x_bit, keep, got)
            parts = [x0[:, :ff_block], x0[:, 2 * ff_block:3 * ff_block], x1[:, :ff_block], x1[:, 2 * ff_block:3 * ff_block]]
            parts += [x0[:, ff_block:2 * ff_block], x0[:, 3 * ff_block:], x1[:, ff_block:2 * ff_block], x1[:, 3 * ff_block:]]
            return jnp.concatenate(parts, axis=1)

        gains = lax.all_gather(jnp.stack([norm1_gain, norm2_gain]), axis_name, axis=1, tiled=True)
        full_q, full_k, full_v, full_o = gather_rows(w_q), gather_rows(w_k), gather_rows(w_v), gather_rows(w_o)
        gate_own, gains = lax.optimization_barrier((w_gate, gains))
        gain1, gain2 = gains[0].astype(jnp.float32), gains[1].astype(jnp.float32)
        up_own, full_k = lax.optimization_barrier((w_up, full_k))
        dy_flat = grad_out.reshape(tokens, width)
        dy_own, down_own, full_q = lax.optimization_barrier((dy_flat, w_down, full_q))
        gate_q = quarter_columns(gate_own)
        up_q = quarter_columns(up_own)
        down_q = jnp.concatenate(pick(y_bit, down_own, swap(down_own, YDIR)), axis=0)
        dy_row = row_tokens(dy_own)

        x_float = hidden.reshape(tokens, width).astype(jnp.float32)
        x_scale = rms_scale(x_float)
        x_unit = x_float * x_scale
        normed = (x_unit * gain1).astype(jnp.bfloat16)
        k_proj = matmul(normed, full_k).astype(jnp.bfloat16)
        v_proj = matmul(normed, full_v).astype(jnp.bfloat16)
        q_proj = matmul(normed, full_q).astype(jnp.bfloat16)
        head_dim = q_norm_gain.shape[0]
        cos_t, sin_t = rope_tables(positions, head_dim)
        attn_in = (q_proj, k_proj, v_proj, cos_t, sin_t, q_norm_gain.reshape(1, head_dim), k_norm_gain.reshape(1, head_dim))
        attn_ctx = attention_forward(attn_in, seq_len)
        attn_out = matmul(attn_ctx, full_o).astype(jnp.bfloat16)
        resid_float = (x_float + attn_out.astype(jnp.float32)).astype(jnp.bfloat16).astype(jnp.float32)
        r_scale = rms_scale(resid_float)
        r_unit = resid_float * r_scale
        mlp_in = row_tokens((r_unit * gain2).astype(jnp.bfloat16))

        acts, d_gates, d_ups = [], [], []
        inv_tokens = 1.0 / (tokens * group_size)
        for part in range(2):
            gate_float = matmul(mlp_in[part], gate_q).astype(jnp.bfloat16).astype(jnp.float32)
            up_float = matmul(mlp_in[part], up_q).astype(jnp.bfloat16).astype(jnp.float32)
            acts.append((jax.nn.silu(gate_float) * up_float).astype(jnp.bfloat16))
            dy_part = dy_row[part]
            if part:
                act_keep, act_send = zip(*(pick(y_bit, act[:, :ff_block], act[:, ff_block:]) for act in acts))
                down_part = token_product(act_send, dy_row)
                down_part, dy_part = lax.optimization_barrier((down_part, dy_part))
                down_got = swap(down_part, YDIR)
            d_mlp_act = matmul_nt(dy_part, down_q)
            gate_sig = jax.nn.sigmoid(gate_float)
            d_ups.append((d_mlp_act * gate_float * gate_sig).astype(jnp.bfloat16))
            d_gates.append((d_mlp_act * up_float * gate_sig * (1.0 + gate_float * (1.0 - gate_sig))).astype(jnp.bfloat16))

        def out_rows(far, lo, hi):
            return matmul(acts[far][lo:hi], down_q)

        def in_rows(far, lo, hi):
            return matmul_nt(d_gates[far][lo:hi], gate_q) + matmul_nt(d_ups[far][lo:hi], up_q)

        half = tokens // 2
        out_side = far_sum(out_rows)
        out_xa = swap(out_side[:half], XDIR)
        in_side = far_sum(in_rows)
        in_x = swap(in_side, XDIR)
        out_xb = swap(out_side[half:], XDIR)
        d_mlp_in = near_sum(in_rows) + in_x

        in_keep, in_send = zip(*(pick(y_bit, part[:, :width // 2], part[:, width // 2:]) for part in mlp_in))
        grad_gate = scatter_columns(in_send, in_keep, d_gates) * inv_tokens
        grad_up = scatter_columns(in_send, in_keep, d_ups) * inv_tokens
        grad_down = (token_product(act_keep, dy_row) + down_got) * inv_tokens
        down_total = near_sum(out_rows)

        grad_norm2 = jnp.sum(d_mlp_in * r_unit, axis=0)
        d_resid = dy_flat.astype(jnp.float32) + norm_backward(d_mlp_in * gain2, r_unit, r_scale)
        d_resid_bf = d_resid.astype(jnp.bfloat16)
        d_attn_ctx = matmul_nt(d_resid_bf, full_o).astype(jnp.bfloat16)
        out_xa, out_xb, _ = lax.optimization_barrier((out_xa, out_xb, d_attn_ctx))
        down_proj = (down_total + jnp.concatenate([out_xa, out_xb], axis=0)).astype(jnp.bfloat16)
        layer_out = (resid_float + down_proj.astype(jnp.float32)).astype(jnp.bfloat16).reshape(hidden.shape)
        wo_part = matmul_tn(attn_ctx, d_resid_bf) * inv_tokens
        wo_part, d_attn_ctx = lax.optimization_barrier((wo_part, d_attn_ctx))
        grad_wo = lax.psum_scatter(wo_part, axis_name, scatter_dimension=0, tiled=True)
        d_query, d_key, d_value, grad_qgain, grad_kgain = attention_backward(d_attn_ctx, attn_in, seq_len)
        wv_part = matmul_tn(normed, d_value) * inv_tokens
        grad_wv = lax.psum_scatter(wv_part, axis_name, scatter_dimension=0, tiled=True)
        wk_part = matmul_tn(normed, d_key) * inv_tokens
        grad_wk = lax.psum_scatter(wk_part, axis_name, scatter_dimension=0, tiled=True)
        wq_part = matmul_tn(normed, d_query) * inv_tokens
        grad_wq = lax.psum_scatter(wq_part, axis_name, scatter_dimension=0, tiled=True)
        d_normed = matmul_nt(d_query, full_q) + matmul_nt(d_key, full_k) + matmul_nt(d_value, full_v)
        grad_norm1 = jnp.sum(d_normed * x_unit, axis=0)
        d_hidden = (d_resid + norm_backward(d_normed * gain1, x_unit, x_scale)).astype(jnp.bfloat16).reshape(hidden.shape)

        small = jnp.concatenate([grad_norm1, grad_norm2, grad_qgain, grad_kgain]) * inv_tokens
        for mask in (CORE, XDIR, YDIR):
            small = small + swap(small, mask)
        own1 = lax.dynamic_slice_in_dim(small, me * rows, rows)
        own2 = lax.dynamic_slice_in_dim(small, width + me * rows, rows)
        gq = small[2 * width:2 * width + head_dim]
        gk = small[2 * width + head_dim:]
        return (layer_out, d_hidden, own1, own2, gq, gk, grad_wq, grad_wk, grad_wv, grad_wo, grad_gate, grad_up, grad_down)

    return jax.shard_map(device_step, mesh=mesh, in_specs=in_specs, out_specs=out_specs, check_vma=False)
```

time: 1920 us -> 1810 us (0.943)
  local copies, waits for them, and re-layouts: 212 us -> 51 us
  Pallas kernels: 0 us -> 92.1 us
  waiting for transfers between devices: 962 us -> 1050 us
  other arithmetic: 197 us -> 128 us
  matrix products: 494 us -> 431 us
    pallas_call x0 -> x2, Pallas kernels: none -> 92.1 us  [the longest x1 54.5 us: attention_backward(): pl.pallas_call(attention_backward_kernel, grid=grid, in_specs=[q_spec] +...]
    ppermute x25 -> x30, waiting for transfers between devices: 915 us -> 1000 us  [swap(): lax.ppermute(value, axis_name, [(j, j ^ mask) for j in range(group_size)])]
    dot_general x5 -> x0, matrix products: 67.3 us -> none  [the longest x1 20.8 us: attention_backward(): jnp.einsum('bksgt,btkd->bskgd', d_scores, k_seq, preferred_element_type=j...]
    convert_element_type x9 -> x1, other arithmetic: 48.2 us -> 2.45 us  [device_step(): normed = (x_unit * gain1).astype(jnp.bfloat16)]
    convert_element_type x7 -> x0, local copies, waits for them, and re-layouts: 43.1 us -> none  [the longest x5 31.5 us: head_norm_rope(): projected.reshape(projected.shape[0], num_heads, head_dim)]
    concatenate x10 -> x3, local copies, waits for them, and re-layouts: 41 us -> 6.41 us  [the longest x2 4.52 us: row_tokens(): return (near, jnp.concatenate([far, swap(far, CORE)], axis=0))]
    reshape x5 -> x0, local copies, waits for them, and re-layouts: 27.3 us -> none  [the longest x2 10.6 us: attention_backward(): d_attn_ctx.reshape(batch_local, seq_len, kv_heads, kv_group, head_dim)]
    add x0 -> x3, other arithmetic: none -> 26.3 us  [the longest x2 17.8 us: scatter_columns(): mine = token_product(left_keep, right) + got]
  transfers between devices with their start and end apart: 33 -> 38, of which waited for: 13 -> 16; matrix products, arithmetic and copies ran while one was open for 35% -> 27% of each run, Pallas kernels for 0% -> 2%
where the time goes in v3:
time: 1810 us; the launch traced here: 1800 us
  waiting for transfers between devices  1050 us (58%)
  matrix products  431 us (24%)
  other arithmetic  128 us (7%)
  Pallas kernels  92.1 us (5%)
  local copies, waits for them, and re-layouts  51 us (3%)
  starting transfers between devices  22.7 us (1%)
    ppermute x30, waiting for transfers between devices, swap(): lax.ppermute(value, axis_name, [(j, j ^ mask) for j in range(group_size)])  1000 us
    dot_general x14, matrix products, matmul_nt(): lax.dot_general(left_op, right_op, (((1,), (1,)), ((), ())), preferred_el...  168 us
    dot_general x16, matrix products, matmul_tn(): lax.dot_general(left_op, right_op, (((0,), (0,)), ((), ())), preferred_el...  139 us
    dot_general x12, matrix products, matmul(): return jnp.dot(left_op, right_op, preferred_element_type=jnp.float32)  124 us
    pallas_call x1, Pallas kernels, attention_backward(): pl.pallas_call(attention_backward_kernel, grid=grid, in_specs=[q_spec] +...  54.5 us
    all_gather x4, waiting for transfers between devices, gather_rows(): return lax.all_gather(row_shard, axis_name, axis=0, tiled=True)  43.3 us
    pallas_call x1, Pallas kernels, attention_forward(): pl.pallas_call(attention_forward_kernel, grid=grid, in_specs=in_specs, ou...  37.6 us
  transfers between devices with their start and end apart: 38, of which 16 were waited for; matrix products, arithmetic and copies ran while one was open for 27% of the time, Pallas kernels for 2%

profile of v3, /device:TPU:0, one launch (start us, length us, event | category | flops | bytes accessed | tf_op | source)
XLA Modules:
  0.0 1801.8 jit_solution(6416554883711699550)
XLA Ops:
  10.1 12.4 all_gather.15
  28.6 49.4 %collective-permute-done.1 = bf16[256,3072]{1,0:T(8,128)(2,1)} collective-permute-done((bf16[256,3072]{1,0:T(8,128)(2,1)}, bf16[256,3072]{1,0:T(8,128)(2,1)}, u32[]{:S(2)}, u32[]{:S(2)}) %collective-permute-start.1) | collective-permute-done | bytes 1572896 | tf_op jit(solution)/shard_map/ppermute | solution.py:159
  97.4 47.3 %collective-permute-done.4 = bf16[256,3072]{1,0:T(8,128)(2,1)S(1)} collective-permute-done((bf16[256,3072]{1,0:T(8,128)(2,1)S(1)}, bf16[256,3072]{1,0:T(8,128)(2,1)S(1)}, u32[]{:S(2)}, u32[]{:S(2)}) %collective-permute-start.4) | collective-permute-done | bytes 1572896 | tf_op jit(solution)/shard_map/ppermute | solution.py:159
  189.5 37.6 %attn_fwd.1 = bf16[768,2048]{1,0:T(8,128)(2,1)} custom-call(bf16[768,2048]{1,0:T(8,128)(2,1)} %convolution_convert_fusion.6.q_ref, bf16[768,1024]{1,0:T(8,128)(2,1)} %convolution_convert_fusion.8.k_ref, bf16[768,1024]{1,0:T(8,128)(2,1)} %convolution_convert_fusion.7.v_ref, f32[768,128]{1,0:T(8,128)} %get-tuple-element.133.cos_ref, ...), custom_call_target="tpu_custom_call" | custom-call | flops 1610612736 | bytes 12582912 | tf_op jit(solution)/shard_map/attn_fwd/pallas_call | solution.py:123
  227.2 34.8 %all-gather.11.cloned.1.call-done = bf16[2048,2048]{1,0:T(8,128)(2,1)} async-done(((bf16[256,2048]{1,0:T(8,128)(2,1)}), bf16[2048,2048]{1,0:T(8,128)(2,1)}) %all-gather.11.cloned.1.call-update) | async-done | bytes 8388624 | tf_op jit(solution)/shard_map/all_gather | solution.py:162
  280.0 22.0 %collective-permute-done.6 = bf16[1024,1536]{1,0:T(8,128)(2,1)} collective-permute-done((bf16[1024,1536]{1,0:T(8,128)(2,1)}, bf16[1024,1536]{1,0:T(8,128)(2,1)}, u32[]{:S(2)}, u32[]{:S(2)}) %collective-permute-start.6) | collective-permute-done | bytes 3145760 | tf_op jit(solution)/shard_map/ppermute | solution.py:159
  310.8 34.6 %collective-permute-done.9 = bf16[768,2048]{1,0:T(8,128)(2,1)} collective-permute-done((bf16[768,2048]{1,0:T(8,128)(2,1)S(1)}, bf16[768,2048]{1,0:T(8,128)(2,1)}, u32[]{:S(2)}, u32[]{:S(2)}) %collective-permute-start.9) | collective-permute-done | bytes 3145760 | tf_op jit(solution)/shard_map/ppermute | solution.py:159
  345.4 23.2 %collective-permute-done.7 = bf16[768,2048]{1,0:T(8,128)(2,1)} collective-permute-done((bf16[768,2048]{1,0:T(8,128)(2,1)}, bf16[768,2048]{1,0:T(8,128)(2,1)}, u32[]{:S(2)}, u32[]{:S(2)}) %collective-permute-start.7) | collective-permute-done | bytes 3145760 | tf_op jit(solution)/shard_map/ppermute | solution.py:159
  386.6 12.1 convolution_convert_fusion.2
  401.7 22.9 %fusion.7 = (bf16[1536,1536]{1,0:T(8,128)(2,1)}, bf16[1536,1536]{1,0:T(8,128)(2,1)}, bf16[1536,1536]{1,0:T(8,128)(2,1)}) fusion(bf16[1536,1536]{1,0:T(8,128)(2,1)} %convolution_convert_fusion.2, bf16[1536,1536]{1,0:T(8,128)(2,1)} %convolution_convert_fusion.3, bf16[1536,2048]{1,0:T(8,128)(2,1)} %constant_dynamic-update-slice_fusion.2, ...), kind=kOutput, calls=%fused_computation.22 | convolution fusion | flops 9718726656 | bytes 36175872 | tf_op jit(solution)/shard_map/dot_general | solution.py:31
  453.7 16.4 fusion.8
  483.9 20.4 %fusion.11 = (bf16[1536,1536]{1,0:T(8,128)(2,1)}, bf16[1536,1536]{1,0:T(8,128)(2,1)}) fusion(bf16[1536,1536]{1,0:T(8,128)(2,1)} %get-tuple-element.131, bf16[1536,1536]{1,0:T(8,128)(2,1)} %convolution_convert_fusion.1, bf16[1536,2048]{1,0:T(8,128)(2,1)S(1)} %constant_dynamic-update-slice_fusion.4, bf16[768,2048]{1,0:T(8,128)(2,1)} %get-tuple-element.84, ...), kind=kOutput, calls=%fused_computation.26 | convolution fusion | flops 9711648768 | bytes 31457280 | tf_op jit(solution)/shard_map/dot_general | solution.py:31
  601.7 114.1 %collective-permute-done.19 = f32[768,2048]{1,0:T(8,128)} collective-permute-done((f32[768,2048]{1,0:T(8,128)S(1)}, f32[768,2048]{1,0:T(8,128)}, u32[]{:S(2)}, u32[]{:S(2)}) %collective-permute-start.19) | collective-permute-done | bytes 6291488 | tf_op jit(solution)/shard_map/ppermute | solution.py:159
  743.4 12.5 convolution_convert_fusion.4.d_ref
  756.0 54.5 %attn_bwd.1 = (bf16[768,2048]{1,0:T(8,128)(2,1)}, bf16[768,1024]{1,0:T(8,128)(2,1)}, bf16[768,1024]{1,0:T(8,128)(2,1)}, f32[192,128]{1,0:T(8,128)}, f32[192,128]{1,0:T(8,128)}) custom-call(bf16[768,2048]{1,0:T(8,128)(2,1)} %convolution_convert_fusion.4.d_ref, bf16[768,2048]{1,0:T(8,128)(2,1)} %convolution_convert_fusion.6.q_ref, ...), custom_call_target="tpu_custom_call" | custom-call | flops 4026531840 | bytes 18874368 | tf_op jit(solution)/shard_map/attn_bwd/pallas_call | solution.py:136
  825.0 12.7 broadcast_multiply_fusion
  948.2 179.0 %collective-permute-done.26 = f32[1024,1536]{1,0:T(8,128)} collective-permute-done((f32[1024,1536]{1,0:T(8,128)}, f32[1024,1536]{1,0:T(8,128)}, u32[]{:S(2)}, u32[]{:S(2)}) %collective-permute-start.26) | collective-permute-done | bytes 6291488 | tf_op jit(solution)/shard_map/ppermute | solution.py:159
  1140.3 339.7 %collective-permute-done.23 = f32[1024,1536]{1,0:T(8,128)} collective-permute-done((f32[1024,1536]{1,0:T(8,128)}, f32[1024,1536]{1,0:T(8,128)}, u32[]{:S(2)}, u32[]{:S(2)}) %collective-permute-start.23) | collective-permute-done | bytes 6291488 | tf_op jit(solution)/shard_map/ppermute | solution.py:159
  1509.2 12.2 add_multiply_fusion
  1550.8 14.8 fusion.43
  1565.7 12.7 collective-permute-done.12
  1578.4 67.4 %collective-permute-done.13 = f32[384,2048]{1,0:T(8,128)} collective-permute-done((f32[384,2048]{1,0:T(8,128)}, f32[384,2048]{1,0:T(8,128)}, u32[]{:S(2)}, u32[]{:S(2)}) %collective-permute-start.13) | collective-permute-done | bytes 3145760 | tf_op jit(solution)/shard_map/ppermute | solution.py:159
  1666.1 47.2 %collective-permute-done.28 = f32[256,3072]{1,0:T(8,128)} collective-permute-done((f32[256,3072]{1,0:T(8,128)}, f32[256,3072]{1,0:T(8,128)}, u32[]{:S(2)}, u32[]{:S(2)}) %collective-permute-start.28) | collective-permute-done | bytes 3145760 | tf_op jit(solution)/shard_map/ppermute | solution.py:159
  1716.0 63.6 %collective-permute-done.25 = f32[256,3072]{1,0:T(8,128)} collective-permute-done((f32[256,3072]{1,0:T(8,128)}, f32[256,3072]{1,0:T(8,128)}, u32[]{:S(2)}, u32[]{:S(2)}) %collective-permute-start.25) | collective-permute-done | bytes 3145760 | tf_op jit(solution)/shard_map/ppermute | solution.py:159
  (445 shorter events, 521.8 us)
Async XLA Ops:
  7.9 147.1 %all-gather.9.cloned.1.call-start = ((), (), s32[]{:S(2)}) async-start(), calls=%async_computation.6 | async-start | bytes 4718592 | tf_op jit(solution)/shard_map/all_gather | solution.py:162
  8.7 169.0 %all-gather.5.cloned.1.call-start = ((), (), s32[]{:S(2)}) async-start(), calls=%async_computation.4 | async-start | bytes 9437184 | tf_op jit(solution)/shard_map/all_gather | solution.py:162
  9.4 252.6 %all-gather.11.cloned.1.call-start = ((), (), s32[]{:S(2)}) async-start(), calls=%async_computation.7 | async-start | bytes 9437184 | tf_op jit(solution)/shard_map/all_gather | solution.py:162
  10.0 1784.4 %reduce-scatter.7.cloned.1.call-start = ((), (), s32[]{:S(2)}) async-start(), calls=%async_computation.9 | async-start | bytes 9437184 | tf_op jit(solution)/shard_map/reduce_scatter | solution.py:302
  95.9 180.5 %collective-permute-start.3 = (bf16[1024,1536]{1,0:T(8,128)(2,1)}, bf16[1024,1536]{1,0:T(8,128)(2,1)}, u32[]{:S(2)}, u32[]{:S(2)}) collective-permute-start(bf16[1024,1536]{1,0:T(8,128)(2,1)} %pad_maximum_fusion.8), channel_id=1, source_target_pairs={{0,4},{1,5},{2,6},{3,7},{4,0},{5,1},{6,2},{7,3}} | collective-permute-start | bytes 9437192 | tf_op jit(solution)/shard_map/ppermute | solution.py:159
  167.9 134.1 %collective-permute-start.6 = (bf16[1024,1536]{1,0:T(8,128)(2,1)}, bf16[1024,1536]{1,0:T(8,128)(2,1)}, u32[]{:S(2)}, u32[]{:S(2)}) collective-permute-start(bf16[1024,1536]{1,0:T(8,128)(2,1)} %pad_maximum_fusion.9), channel_id=1, source_target_pairs={{0,4},{1,5},{2,6},{3,7},{4,0},{5,1},{6,2},{7,3}} | collective-permute-start | bytes 9437192 | tf_op jit(solution)/shard_map/ppermute | solution.py:159
  276.4 98.2 %collective-permute-start = (bf16[768,2048]{1,0:T(8,128)(2,1)S(1)}, bf16[768,2048]{1,0:T(8,128)(2,1)}, u32[]{:S(2)}, u32[]{:S(2)}) collective-permute-start(bf16[768,2048]{1,0:T(8,128)(2,1)S(1)} %fusion.24), channel_id=1, source_target_pairs={{0,1},{1,0},{2,3},{3,2},{4,5},{5,4},{6,7},{7,6}} | collective-permute-start | bytes 9437192 | tf_op jit(solution)/shard_map/ppermute | solution.py:159
  304.7 93.9 %collective-permute-start.14 = (bf16[768,2048]{1,0:T(8,128)(2,1)}, bf16[768,2048]{1,0:T(8,128)(2,1)S(1)}, u32[]{:S(2)}, u32[]{:S(2)}) collective-permute-start(bf16[768,2048]{1,0:T(8,128)(2,1)} %bitcast.2), channel_id=1, source_target_pairs={{0,1},{1,0},{2,3},{3,2},{4,5},{5,4},{6,7},{7,6}} | collective-permute-start | bytes 9437192 | tf_op jit(solution)/shard_map/ppermute | solution.py:159
  304.8 119.8 %collective-permute-start.16 = (bf16[768,2048]{1,0:T(8,128)(2,1)}, bf16[768,2048]{1,0:T(8,128)(2,1)}, u32[]{:S(2)}, u32[]{:S(2)}) collective-permute-start(bf16[768,2048]{1,0:T(8,128)(2,1)} %bitcast.2), channel_id=1, source_target_pairs={{0,2},{1,3},{2,0},{3,1},{4,6},{5,7},{6,4},{7,5}} | collective-permute-start | bytes 9437192 | tf_op jit(solution)/shard_map/ppermute | solution.py:159
  345.4 93.0 %collective-permute-start.10 = (bf16[768,2048]{1,0:T(8,128)(2,1)}, bf16[768,2048]{1,0:T(8,128)(2,1)}, u32[]{:S(2)}, u32[]{:S(2)}) collective-permute-start(bf16[768,2048]{1,0:T(8,128)(2,1)} %collective-permute-done.9), channel_id=1, source_target_pairs={{0,1},{1,0},{2,3},{3,2},{4,5},{5,4},{6,7},{7,6}} | collective-permute-start | bytes 9437192 | tf_op jit(solution)/shard_map/ppermute | solution.py:159
  577.7 138.1 %collective-permute-start.19 = (f32[768,2048]{1,0:T(8,128)S(1)}, f32[768,2048]{1,0:T(8,128)}, u32[]{:S(2)}, u32[]{:S(2)}) collective-permute-start(f32[768,2048]{1,0:T(8,128)S(1)} %add_add_fusion.3), channel_id=1, source_target_pairs={{0,2},{1,3},{2,0},{3,1},{4,6},{5,7},{6,4},{7,5}} | collective-permute-start | bytes 18874376 | tf_op jit(solution)/shard_map/ppermute | solution.py:159
  817.5 976.9 %reduce-scatter.9.cloned.1.call-start = ((), (), s32[]{:S(2)}) async-start(), calls=%async_computation.10 | async-start | bytes 9437184 | tf_op jit(solution)/shard_map/reduce_scatter | solution.py:300
  825.0 969.4 %reduce-scatter.5.cloned.1.call-start = ((), (), s32[]{:S(2)}) async-start(), calls=%async_computation.8 | async-start | bytes 18874368 | tf_op jit(solution)/shard_map/reduce_scatter | solution.py:304
  837.8 956.6 %reduce-scatter.11.cloned.1.call-start = ((), (), s32[]{:S(2)}) async-start(), calls=%async_computation.11 | async-start | bytes 18874368 | tf_op jit(solution)/shard_map/reduce_scatter | solution.py:297
  849.2 796.6 %collective-permute-start.8 = (f32[768,2048]{1,0:T(8,128)}, f32[768,2048]{1,0:T(8,128)}, u32[]{:S(2)}, u32[]{:S(2)}) collective-permute-start(f32[768,2048]{1,0:T(8,128)} %fusion.75), channel_id=1, source_target_pairs={{0,1},{1,0},{2,3},{3,2},{4,5},{5,4},{6,7},{7,6}} | collective-permute-start | bytes 18874376 | tf_op jit(solution)/shard_map/ppermute | solution.py:159
  905.0 222.3 %collective-permute-start.26 = (f32[1024,1536]{1,0:T(8,128)}, f32[1024,1536]{1,0:T(8,128)}, u32[]{:S(2)}, u32[]{:S(2)}) collective-permute-start(f32[1024,1536]{1,0:T(8,128)} %convolution_add_fusion), channel_id=1, source_target_pairs={{0,4},{1,5},{2,6},{3,7},{4,0},{5,1},{6,2},{7,3}} | collective-permute-start | bytes 18874376 | tf_op jit(solution)/shard_map/ppermute | solution.py:159
  907.4 601.2 %collective-permute-start.29 = (f32[768,2048]{1,0:T(8,128)}, f32[768,2048]{1,0:T(8,128)}, u32[]{:S(2)}, u32[]{:S(2)}) collective-permute-start(f32[768,2048]{1,0:T(8,128)} %convolution_add_fusion.3), channel_id=1, source_target_pairs={{0,4},{1,5},{2,6},{3,7},{4,0},{5,1},{6,2},{7,3}} | collective-permute-start | bytes 18874376 | tf_op jit(solution)/shard_map/ppermute | solution.py:159
  914.9 565.1 %collective-permute-start.23 = (f32[1024,1536]{1,0:T(8,128)}, f32[1024,1536]{1,0:T(8,128)}, u32[]{:S(2)}, u32[]{:S(2)}) collective-permute-start(f32[1024,1536]{1,0:T(8,128)} %convolution_add_fusion.1), channel_id=1, source_target_pairs={{0,4},{1,5},{2,6},{3,7},{4,0},{5,1},{6,2},{7,3}} | collective-permute-start | bytes 18874376 | tf_op jit(solution)/shard_map/ppermute | solution.py:159
  925.6 568.4 %collective-permute-start.11 = (f32[768,2048]{1,0:T(8,128)}, f32[768,2048]{1,0:T(8,128)}, u32[]{:S(2)}, u32[]{:S(2)}) collective-permute-start(f32[768,2048]{1,0:T(8,128)} %fusion.72), channel_id=1, source_target_pairs={{0,1},{1,0},{2,3},{3,2},{4,5},{5,4},{6,7},{7,6}} | collective-permute-start | bytes 18874376 | tf_op jit(solution)/shard_map/ppermute | solution.py:159
  1140.3 381.1 %collective-permute-start.27 = (f32[512,1536]{1,0:T(8,128)}, f32[512,1536]{1,0:T(8,128)}, u32[]{:S(2)}, u32[]{:S(2)}) collective-permute-start(f32[512,1536]{1,0:T(8,128)} %fusion.54), channel_id=1, source_target_pairs={{0,1},{1,0},{2,3},{3,2},{4,5},{5,4},{6,7},{7,6}} | collective-permute-start | bytes 9437192 | tf_op jit(solution)/shard_map/ppermute | solution.py:159
  1508.6 137.2 %collective-permute-start.13 = (f32[384,2048]{1,0:T(8,128)}, f32[384,2048]{1,0:T(8,128)}, u32[]{:S(2)}, u32[]{:S(2)}) collective-permute-start(f32[384,2048]{1,0:T(8,128)} %get-tuple-element.81), channel_id=1, source_target_pairs={{0,2},{1,3},{2,0},{3,1},{4,6},{5,7},{6,4},{7,5}} | collective-permute-start | bytes 9437192 | tf_op jit(solution)/shard_map/ppermute | solution.py:159
  1529.1 184.1 %collective-permute-start.28 = (f32[256,3072]{1,0:T(8,128)}, f32[256,3072]{1,0:T(8,128)}, u32[]{:S(2)}, u32[]{:S(2)}) collective-permute-start(f32[256,3072]{1,0:T(8,128)} %broadcast_select_fusion.12), channel_id=1, source_target_pairs={{0,2},{1,3},{2,0},{3,1},{4,6},{5,7},{6,4},{7,5}} | collective-permute-start | bytes 9437192 | tf_op jit(solution)/shard_map/ppermute | solution.py:159
  1538.3 241.4 %collective-permute-start.25 = (f32[256,3072]{1,0:T(8,128)}, f32[256,3072]{1,0:T(8,128)}, u32[]{:S(2)}, u32[]{:S(2)}) collective-permute-start(f32[256,3072]{1,0:T(8,128)} %broadcast_select_fusion.16), channel_id=1, source_target_pairs={{0,2},{1,3},{2,0},{3,1},{4,6},{5,7},{6,4},{7,5}} | collective-permute-start | bytes 9437192 | tf_op jit(solution)/shard_map/ppermute | solution.py:159
  1578.4 207.2 %collective-permute-start.20 = (f32[4352]{0:T(1024)S(1)}, f32[4352]{0:T(1024)S(1)}, u32[]{:S(2)}, u32[]{:S(2)}) collective-permute-start(f32[4352]{0:T(1024)S(1)} %maximum_multiply_fusion), channel_id=1, source_target_pairs={{0,1},{1,0},{2,3},{3,2},{4,5},{5,4},{6,7},{7,6}} | collective-permute-start | bytes 52232 | tf_op jit(solution)/shard_map/ppermute | solution.py:159
  (137 other events, 3242.2 us)
Sparse Core Ops, SparseCore 0:
  9.8 45.0 all-gather.6
  56.7 36.4 all-gather.8
  95.1 82.5 all-gather.4
  179.4 82.5 all-gather.10
  817.6 63.4 reduce-scatter.6
  885.0 95.6 reduce-scatter.8
  984.7 175.4 reduce-scatter.4
  1164.3 175.4 reduce-scatter.10

commit v4 on v3

--- a/solution.py
+++ b/solution.py
@@ -107,40 +107,42 @@
     dv_ref[...] = d_value.astype(jnp.bfloat16)
 
 
-def attention_specs(q_proj, k_proj, seq_len, head_dim):
-    tokens = q_proj.shape[0]
-    kv_heads = k_proj.shape[1] // head_dim
-    q_spec = pl.BlockSpec((seq_len, q_proj.shape[1] // kv_heads), lambda b, h: (b, h))
-    k_spec = pl.BlockSpec((seq_len, head_dim), lambda b, h: (b, h))
+def attention_specs(qkv, heads, kv_heads, seq_len, head_dim):
+    q_spec = pl.BlockSpec((seq_len, heads // kv_heads * head_dim), lambda b, h: (b, h))
+    k_spec = pl.BlockSpec((seq_len, head_dim), lambda b, h: (b, heads + h))
+    v_spec = pl.BlockSpec((seq_len, head_dim), lambda b, h: (b, heads + kv_heads + h))
     t_spec = pl.BlockSpec((seq_len, head_dim), lambda b, h: (b, 0))
     g_spec = pl.BlockSpec((1, head_dim), lambda b, h: (0, 0))
-    return (tokens // seq_len, kv_heads), q_spec, k_spec, [q_spec, k_spec, k_spec, t_spec, t_spec, g_spec, g_spec]
-
-
-def attention_forward(operands, seq_len):
-    q_proj, k_proj, head_dim = operands[0], operands[1], operands[3].shape[1]
-    grid, q_spec, _, in_specs = attention_specs(q_proj, k_proj, seq_len, head_dim)
+    return (qkv.shape[0] // seq_len, kv_heads), q_spec, [q_spec, k_spec, v_spec, t_spec, t_spec, g_spec, g_spec]
+
+
+def attention_forward(qkv, tables, heads, kv_heads, seq_len):
+    head_dim = tables[0].shape[1]
+    grid, q_spec, in_specs = attention_specs(qkv, heads, kv_heads, seq_len, head_dim)
+    width = heads * head_dim
     return pl.pallas_call(
         attention_forward_kernel, grid=grid, in_specs=in_specs, out_specs=q_spec,
-        out_shape=jax.ShapeDtypeStruct(q_proj.shape, jnp.bfloat16),
-        cost_estimate=pl.CostEstimate(flops=4 * q_proj.size * seq_len, bytes_accessed=8 * q_proj.size, transcendentals=0),
+        out_shape=jax.ShapeDtypeStruct((qkv.shape[0], width), jnp.bfloat16),
+        cost_estimate=pl.CostEstimate(flops=2 * qkv.size * seq_len, bytes_accessed=3 * qkv.size, transcendentals=0),
         name="attn_fwd",
-    )(*operands)
-
-
-def attention_backward(d_ctx, operands, seq_len):
-    q_proj, k_proj, head_dim = operands[0], operands[1], operands[3].shape[1]
-    grid, q_spec, k_spec, in_specs = attention_specs(q_proj, k_proj, seq_len, head_dim)
+    )(qkv, qkv, qkv, *tables)
+
+
+def attention_backward(d_ctx, qkv, tables, heads, kv_heads, seq_len):
+    head_dim = tables[0].shape[1]
+    grid, q_spec, in_specs = attention_specs(qkv, heads, kv_heads, seq_len, head_dim)
+    k_spec = pl.BlockSpec((seq_len, head_dim), lambda b, h: (b, h))
+    k_shape = jax.ShapeDtypeStruct((qkv.shape[0], kv_heads * head_dim), jnp.bfloat16)
     gain_spec = pl.BlockSpec((8, head_dim), lambda b, h: (b * grid[1] + h, 0))
     gain_shape = jax.ShapeDtypeStruct((8 * grid[0] * grid[1], head_dim), jnp.float32)
     dq, dk, dv, dqg, dkg = pl.pallas_call(
         attention_backward_kernel, grid=grid, in_specs=[q_spec] + in_specs,
         out_specs=[q_spec, k_spec, k_spec, gain_spec, gain_spec],
-        out_shape=[jax.ShapeDtypeStruct(q_proj.shape, jnp.bfloat16)] + [jax.ShapeDtypeStruct(k_proj.shape, jnp.bfloat16)] * 2 + [gain_shape] * 2,
-        cost_estimate=pl.CostEstimate(flops=10 * q_proj.size * seq_len, bytes_accessed=12 * q_proj.size, transcendentals=0),
+        out_shape=[jax.ShapeDtypeStruct(d_ctx.shape, jnp.bfloat16), k_shape, k_shape, gain_shape, gain_shape],
+        cost_estimate=pl.CostEstimate(flops=5 * qkv.size * seq_len, bytes_accessed=6 * qkv.size, transcendentals=0),
         name="attn_bwd",
-    )(d_ctx, *operands)
-    return dq, dk, dv, jnp.sum(dqg, axis=0), jnp.sum(dkg, axis=0)
+    )(d_ctx, qkv, qkv, qkv, *tables)
+    return jnp.concatenate([dq, dk, dv], axis=1), jnp.sum(dqg, axis=0), jnp.sum(dkg, axis=0)
 
 
 def pick(bit, first, second):
@@ -179,7 +181,7 @@
             first = jnp.concatenate([blk[0], blk[1], blk[4], blk[5]], axis=1)
             second = jnp.concatenate([blk[2], blk[3], blk[6], blk[7]], axis=1)
             keep, send = pick(x_bit, first, second)
-            got = swap(send, XDIR)
+            first = got = swap(send, XDIR)
             row0, row1 = pick(x_bit, keep, got)
             both = jnp.concatenate([row0, row1], axis=0)
             col = [both[:, j * ff_block:(j + 1) * ff_block] for j in range(4)]
@@ -188,25 +190,28 @@
             core0, core1 = pick(c_bit, keep, got)
             four = jnp.concatenate([core0[:rows], core1[:rows], core0[rows:], core1[rows:]], axis=0)
             got = swap(four, YDIR)
-            return jnp.concatenate(pick(y_bit, four, got), axis=0)
-
-        def far_sum(partial_rows):
-            part = partial_rows(1, tokens, 2 * tokens)
+            return jnp.concatenate(pick(y_bit, four, got), axis=0), first
+
+        def far_sum(add_rows):
+            part = add_rows(None, 1, tokens, 2 * tokens)
             part = swap(part, CORE)
-            return partial_rows(1, 0, tokens) + part
-
-        def near_sum(partial_rows):
-            part = partial_rows(0, tokens, 2 * tokens)
+            return add_rows(part, 1, 0, tokens)
+
+        def near_sum(add_rows):
+            part = add_rows(None, 0, tokens, 2 * tokens)
             part = swap(part, CORE)
-            return partial_rows(0, 0, tokens) + part
-
-        def token_product(left, right):
-            return matmul_tn(left[0], right[0]) + matmul_tn(left[1], right[1])
+            return add_rows(part, 0, 0, tokens)
+
+        def plus(base, product):
+            return product if base is None else base + product
+
+        def token_product(left, right, base=None):
+            return plus(plus(base, matmul_tn(left[0], right[0])), matmul_tn(left[1], right[1]))
 
         def scatter_columns(left_send, left_keep, right):
             part = token_product(left_send, right)
             got = swap(part, YDIR)
-            mine = token_product(left_keep, right) + got
+            mine = token_product(left_keep, right, got)
             blk = [mine[j * rows:(j + 1) * rows] for j in range(4)]
             keep, send = pick(c_bit, jnp.concatenate([blk[0], blk[2]], axis=0), jnp.concatenate([blk[1], blk[3]], axis=0))
             got = swap(send, CORE)
@@ -220,14 +225,14 @@
             return jnp.concatenate(parts, axis=1)
 
         gains = lax.all_gather(jnp.stack([norm1_gain, norm2_gain]), axis_name, axis=1, tiled=True)
-        full_q, full_k, full_v, full_o = gather_rows(w_q), gather_rows(w_k), gather_rows(w_v), gather_rows(w_o)
-        gate_own, gains = lax.optimization_barrier((w_gate, gains))
+        full_qkv, full_o = gather_rows(jnp.concatenate([w_q, w_k, w_v], axis=1)), gather_rows(w_o)
+        gate_own, down_own, gains = lax.optimization_barrier((w_gate, w_down, gains))
         gain1, gain2 = gains[0].astype(jnp.float32), gains[1].astype(jnp.float32)
-        up_own, full_k = lax.optimization_barrier((w_up, full_k))
         dy_flat = grad_out.reshape(tokens, width)
-        dy_own, down_own, full_q = lax.optimization_barrier((dy_flat, w_down, full_q))
-        gate_q = quarter_columns(gate_own)
-        up_q = quarter_columns(up_own)
+        dy_own, full_qkv = lax.optimization_barrier((dy_flat, full_qkv))
+        gate_q, gate_first = quarter_columns(gate_own)
+        up_own, _ = lax.optimization_barrier((w_up, gate_first))
+        up_q, _ = quarter_columns(up_own)
         down_q = jnp.concatenate(pick(y_bit, down_own, swap(down_own, YDIR)), axis=0)
         dy_row = row_tokens(dy_own)
 
@@ -235,13 +240,11 @@
         x_scale = rms_scale(x_float)
         x_unit = x_float * x_scale
         normed = (x_unit * gain1).astype(jnp.bfloat16)
-        k_proj = matmul(normed, full_k).astype(jnp.bfloat16)
-        v_proj = matmul(normed, full_v).astype(jnp.bfloat16)
-        q_proj = matmul(normed, full_q).astype(jnp.bfloat16)
+        qkv = matmul(normed, full_qkv).astype(jnp.bfloat16)
         head_dim = q_norm_gain.shape[0]
-        cos_t, sin_t = rope_tables(positions, head_dim)
-        attn_in = (q_proj, k_proj, v_proj, cos_t, sin_t, q_norm_gain.reshape(1, head_dim), k_norm_gain.reshape(1, head_dim))
-        attn_ctx = attention_forward(attn_in, seq_len)
+        heads, kv_heads = w_q.shape[1] // head_dim, w_k.shape[1] // head_dim
+        tables = rope_tables(positions, head_dim) + (q_norm_gain.reshape(1, head_dim), k_norm_gain.reshape(1, head_dim))
+        attn_ctx = attention_forward(qkv, tables, heads, kv_heads, seq_len)
         attn_out = matmul(attn_ctx, full_o).astype(jnp.bfloat16)
         resid_float = (x_float + attn_out.astype(jnp.float32)).astype(jnp.bfloat16).astype(jnp.float32)
         r_scale = rms_scale(resid_float)
@@ -265,11 +268,11 @@
             d_ups.append((d_mlp_act * gate_float * gate_sig).astype(jnp.bfloat16))
             d_gates.append((d_mlp_act * up_float * gate_sig * (1.0 + gate_float * (1.0 - gate_sig))).astype(jnp.bfloat16))
 
-        def out_rows(far, lo, hi):
-            return matmul(acts[far][lo:hi], down_q)
-
-        def in_rows(far, lo, hi):
-            return matmul_nt(d_gates[far][lo:hi], gate_q) + matmul_nt(d_ups[far][lo:hi], up_q)
+        def out_rows(base, far, lo, hi):
+            return plus(base, matmul(acts[far][lo:hi], down_q))
+
+        def in_rows(base, far, lo, hi):
+            return plus(plus(base, matmul_nt(d_gates[far][lo:hi], gate_q)), matmul_nt(d_ups[far][lo:hi], up_q))
 
         half = tokens // 2
         out_side = far_sum(out_rows)
@@ -282,7 +285,7 @@
         in_keep, in_send = zip(*(pick(y_bit, part[:, :width // 2], part[:, width // 2:]) for part in mlp_in))
         grad_gate = scatter_columns(in_send, in_keep, d_gates) * inv_tokens
         grad_up = scatter_columns(in_send, in_keep, d_ups) * inv_tokens
-        grad_down = (token_product(act_keep, dy_row) + down_got) * inv_tokens
+        grad_down = token_product(act_keep, dy_row, down_got) * inv_tokens
         down_total = near_sum(out_rows)
 
         grad_norm2 = jnp.sum(d_mlp_in * r_unit, axis=0)
@@ -295,14 +298,11 @@
         wo_part = matmul_tn(attn_ctx, d_resid_bf) * inv_tokens
         wo_part, d_attn_ctx = lax.optimization_barrier((wo_part, d_attn_ctx))
         grad_wo = lax.psum_scatter(wo_part, axis_name, scatter_dimension=0, tiled=True)
-        d_query, d_key, d_value, grad_qgain, grad_kgain = attention_backward(d_attn_ctx, attn_in, seq_len)
-        wv_part = matmul_tn(normed, d_value) * inv_tokens
-        grad_wv = lax.psum_scatter(wv_part, axis_name, scatter_dimension=0, tiled=True)
-        wk_part = matmul_tn(normed, d_key) * inv_tokens
-        grad_wk = lax.psum_scatter(wk_part, axis_name, scatter_dimension=0, tiled=True)
-        wq_part = matmul_tn(normed, d_query) * inv_tokens
-        grad_wq = lax.psum_scatter(wq_part, axis_name, scatter_dimension=0, tiled=True)
-        d_normed = matmul_nt(d_query, full_q) + matmul_nt(d_key, full_k) + matmul_nt(d_value, full_v)
+        d_qkv, grad_qgain, grad_kgain = attention_backward(d_attn_ctx, qkv, tables, heads, kv_heads, seq_len)
+        qkv_part = matmul_tn(normed, d_qkv) * inv_tokens
+        grad_qkv = lax.psum_scatter(qkv_part, axis_name, scatter_dimension=0, tiled=True)
+        grad_wq, grad_wk, grad_wv = jnp.split(grad_qkv, (w_q.shape[1], w_q.shape[1] + w_k.shape[1]), axis=1)
+        d_normed = matmul_nt(d_qkv, full_qkv)
         grad_norm1 = jnp.sum(d_normed * x_unit, axis=0)
         d_hidden = (d_resid + norm_backward(d_normed * gain1, x_unit, x_scale)).astype(jnp.bfloat16).reshape(hidden.shape)
 

time: 1810 us -> 1710 us (0.945)
  waiting for transfers between devices: 1050 us -> 988 us
  other arithmetic: 128 us -> 101 us
    ppermute x30, waiting for transfers between devices: 1000 us -> 971 us  [swap(): lax.ppermute(value, axis_name, [(j, j ^ mask) for j in range(group_size)])]
    all_gather x4 -> x2, waiting for transfers between devices: 43.3 us -> 15.5 us  [gather_rows(): return lax.all_gather(row_shard, axis_name, axis=0, tiled=True)]
    add x3 -> x1, other arithmetic: 26.3 us -> 6.33 us  [plus(): return product if base is None else base + product]
    dot_general x12 -> x10, matrix products: 124 us -> 117 us  [matmul(): return jnp.dot(left_op, right_op, preferred_element_type=jnp.float32)]
    dot_general x16 -> x14, matrix products: 139 us -> 135 us  [matmul_tn(): lax.dot_general(left_op, right_op, (((0,), (0,)), ((), ())), preferred_el...]
    dot_general x14 -> x12, matrix products: 168 us -> 165 us  [matmul_nt(): lax.dot_general(left_op, right_op, (((1,), (1,)), ((), ())), preferred_el...]
    unnamed x263 -> x241, local copies, waits for them, and re-layouts: 36.1 us -> 38.8 us
  transfers between devices with their start and end apart: 38 -> 34, of which waited for: 16 -> 15; matrix products, arithmetic and copies ran while one was open for 27% -> 26% of each run, Pallas kernels for 2% -> 2%
where the time goes in v4:
time: 1710 us; the launch traced here: 1700 us
  waiting for transfers between devices  988 us (58%)
  matrix products  418 us (24%)
  other arithmetic  101 us (6%)
  Pallas kernels  93 us (5%)
  local copies, waits for them, and re-layouts  62.7 us (4%)
    ppermute x30, waiting for transfers between devices, swap(): lax.ppermute(value, axis_name, [(j, j ^ mask) for j in range(group_size)])  971 us
    dot_general x12, matrix products, matmul_nt(): lax.dot_general(left_op, right_op, (((1,), (1,)), ((), ())), preferred_el...  165 us
    dot_general x14, matrix products, matmul_tn(): lax.dot_general(left_op, right_op, (((0,), (0,)), ((), ())), preferred_el...  135 us
    dot_general x10, matrix products, matmul(): return jnp.dot(left_op, right_op, preferred_element_type=jnp.float32)  117 us
    pallas_call x1, Pallas kernels, attention_backward(): pl.pallas_call(attention_backward_kernel, grid=grid, in_specs=[q_spec] +...  54.9 us
    unnamed x241, local copies, waits for them, and re-layouts  38.8 us
    pallas_call x1, Pallas kernels, attention_forward(): pl.pallas_call(attention_forward_kernel, grid=grid, in_specs=in_specs, ou...  38.1 us
  transfers between devices with their start and end apart: 34, of which 15 were waited for; matrix products, arithmetic and copies ran while one was open for 26% of the time, Pallas kernels for 2%

profile of v4, /device:TPU:0, one launch (start us, length us, event | category | flops | bytes accessed | tf_op | source)
XLA Modules:
  0.0 1704.5 jit_solution(1899781706133757393)
XLA Ops:
  11.2 12.2 all_gather.9
  33.5 59.7 %collective-permute-done.1 = bf16[256,3072]{1,0:T(8,128)(2,1)} collective-permute-done((bf16[256,3072]{1,0:T(8,128)(2,1)}, bf16[256,3072]{1,0:T(8,128)(2,1)}, u32[]{:S(2)}, u32[]{:S(2)}) %collective-permute-start.1) | collective-permute-done | bytes 1572896 | tf_op jit(solution)/shard_map/ppermute | solution.py:161
  99.7 57.4 %collective-permute-done.4 = bf16[256,3072]{1,0:T(8,128)(2,1)S(1)} collective-permute-done((bf16[256,3072]{1,0:T(8,128)(2,1)S(1)}, bf16[256,3072]{1,0:T(8,128)(2,1)S(1)}, u32[]{:S(2)}, u32[]{:S(2)}) %collective-permute-start.4) | collective-permute-done | bytes 1572896 | tf_op jit(solution)/shard_map/ppermute | solution.py:161
  168.3 19.3 %convolution_convert_fusion.4.q_ref.k_ref.v_ref = bf16[768,4096]{1,0:T(8,128)(2,1)} fusion(bf16[768,2048]{1,0:T(8,128)(2,1)} %fusion.37, bf16[2048,4096]{1,0:T(8,128)(2,1)} %all-gather.3.cloned.1.call-done), kind=kOutput, calls=%fused_computation.50 | convolution fusion | flops 12888047616 | bytes 26214400 | tf_op jit(solution)/shard_map/dot_general | solution.py:23
  187.6 38.1 %attn_fwd.1 = bf16[768,2048]{1,0:T(8,128)(2,1)} custom-call(bf16[768,4096]{1,0:T(8,128)(2,1)} %convolution_convert_fusion.4.q_ref.k_ref.v_ref, bf16[768,4096]{1,0:T(8,128)(2,1)} %convolution_convert_fusion.4.q_ref.k_ref.v_ref, bf16[768,4096]{1,0:T(8,128)(2,1)} %convolution_convert_fusion.4.q_ref.k_ref.v_ref, f32[768,128]{1,0:T(8,128)} %get-tuple-element.133.cos_ref, ...), custom_call_target="tpu_custom_call" | custom-call | flops 1610612736 | bytes 9437184 | tf_op jit(solution)/shard_map/attn_fwd/pallas_call | solution.py:123
  225.6 15.5 all-gather.5.cloned.1.call-done
  270.2 64.2 %collective-permute-done.6 = bf16[1024,1536]{1,0:T(8,128)(2,1)} collective-permute-done((bf16[1024,1536]{1,0:T(8,128)(2,1)}, bf16[1024,1536]{1,0:T(8,128)(2,1)}, u32[]{:S(2)}, u32[]{:S(2)}) %collective-permute-start.6) | collective-permute-done | bytes 3145760 | tf_op jit(solution)/shard_map/ppermute | solution.py:161
  355.8 12.0 convolution_convert_fusion.2
  370.9 22.9 %fusion.7 = (bf16[1536,1536]{1,0:T(8,128)(2,1)}, bf16[1536,1536]{1,0:T(8,128)(2,1)}, bf16[1536,1536]{1,0:T(8,128)(2,1)}) fusion(bf16[1536,1536]{1,0:T(8,128)(2,1)} %convolution_convert_fusion.2, bf16[1536,1536]{1,0:T(8,128)(2,1)} %convolution_convert_fusion.3, bf16[1536,2048]{1,0:T(8,128)(2,1)} %copy-done.73, bf16[768,2048]{1,0:T(8,128)(2,1)} %get-tuple-element.82, ...), kind=kOutput, calls=%fused_computation.23 | convolution fusion | flops 9718726656 | bytes 36175872 | tf_op jit(solution)/shard_map/dot_general | solution.py:31
  393.8 14.6 collective-permute-done.16
  437.6 16.6 fusion.8
  468.0 20.3 %fusion.11 = (bf16[1536,1536]{1,0:T(8,128)(2,1)}, bf16[1536,1536]{1,0:T(8,128)(2,1)}) fusion(bf16[1536,1536]{1,0:T(8,128)(2,1)} %get-tuple-element.131, bf16[1536,1536]{1,0:T(8,128)(2,1)} %convolution_convert_fusion.1, bf16[1536,2048]{1,0:T(8,128)(2,1)S(1)} %constant_dynamic-update-slice_fusion.4, bf16[768,2048]{1,0:T(8,128)(2,1)} %get-tuple-element.82, ...), kind=kOutput, calls=%fused_computation.27 | convolution fusion | flops 9711648768 | bytes 31457280 | tf_op jit(solution)/shard_map/dot_general | solution.py:31
  577.4 116.1 %collective-permute-done.19 = f32[768,2048]{1,0:T(8,128)} collective-permute-done((f32[768,2048]{1,0:T(8,128)}, f32[768,2048]{1,0:T(8,128)}, u32[]{:S(2)}, u32[]{:S(2)}) %collective-permute-start.19) | collective-permute-done | bytes 6291488 | tf_op jit(solution)/shard_map/ppermute | solution.py:161
  719.9 12.4 convolution_convert_fusion.5.d_ref
  732.3 54.9 %attn_bwd.1 = (bf16[768,2048]{1,0:T(8,128)(2,1)}, bf16[768,1024]{1,0:T(8,128)(2,1)}, bf16[768,1024]{1,0:T(8,128)(2,1)}, f32[192,128]{1,0:T(8,128)}, f32[192,128]{1,0:T(8,128)}) custom-call(bf16[768,2048]{1,0:T(8,128)(2,1)} %convolution_convert_fusion.5.d_ref, bf16[768,4096]{1,0:T(8,128)(2,1)} %convolution_convert_fusion.4.q_ref.k_ref.v_ref, ...), custom_call_target="tpu_custom_call" | custom-call | flops 4026531840 | bytes 18874368 | tf_op jit(solution)/shard_map/attn_bwd/pallas_call | solution.py:138
  792.8 17.6 %convolution_multiply_fusion = f32[2048,4096]{1,0:T(8,128)} fusion(bf16[768,2048]{1,0:T(8,128)(2,1)S(1)} %copy-done.51, bf16[768,4096]{1,0:T(8,128)(2,1)S(1)} %constant_dynamic-update-slice_fusion.6), kind=kOutput, calls=%fused_computation | convolution fusion | flops 12893290496 | bytes 42991616 | tf_op jit(solution)/shard_map/dot_general | solution.py:27
  826.1 12.0 fusion.78
  909.9 220.8 %collective-permute-done.26 = f32[1024,1536]{1,0:T(8,128)} collective-permute-done((f32[1024,1536]{1,0:T(8,128)S(1)}, f32[1024,1536]{1,0:T(8,128)}, u32[]{:S(2)}, u32[]{:S(2)}) %collective-permute-start.26) | collective-permute-done | bytes 6291488 | tf_op jit(solution)/shard_map/ppermute | solution.py:161
  1147.0 191.7 %collective-permute-done.23 = f32[1024,1536]{1,0:T(8,128)} collective-permute-done((f32[1024,1536]{1,0:T(8,128)}, f32[1024,1536]{1,0:T(8,128)}, u32[]{:S(2)}, u32[]{:S(2)}) %collective-permute-start.23) | collective-permute-done | bytes 6291488 | tf_op jit(solution)/shard_map/ppermute | solution.py:161
  1368.8 104.4 %collective-permute-done.29 = f32[768,2048]{1,0:T(8,128)} collective-permute-done((f32[768,2048]{1,0:T(8,128)}, f32[768,2048]{1,0:T(8,128)}, u32[]{:S(2)}, u32[]{:S(2)}) %collective-permute-start.29) | collective-permute-done | bytes 6291488 | tf_op jit(solution)/shard_map/ppermute | solution.py:161
  1501.4 21.4 %fusion.43 = (f32[2048]{0:T(1024)S(1)}, f32[768]{0:T(1024)S(1)}, f32[768,2048]{1,0:T(8,128)}) fusion(bf16[3,256,2048]{2,1,0:T(8,128)(2,1)} %param.14, f32[768]{0:T(1024)S(1)} %copy-done.88, f32[2048]{0:T(1024)S(1)} %bitcast.81, bf16[768,4096]{1,0:T(8,128)(2,1)} %copy-done.75, bf16[2048,4096]{1,0:T(8,128)(2,1)} %all-gather.3.cloned.1.call-done), kind=kOutput, calls=%fused_computation.81 | convolution fusion | flops 12895908864 | bytes 32528384 | tf_op jit(solution)/shard_map/dot_general | solution.py:31
  1523.0 21.4 %collective-permute-done.13 = f32[384,2048]{1,0:T(8,128)} collective-permute-done((f32[384,2048]{1,0:T(8,128)}, f32[384,2048]{1,0:T(8,128)}, u32[]{:S(2)}, u32[]{:S(2)}) %collective-permute-start.13) | collective-permute-done | bytes 3145760 | tf_op jit(solution)/shard_map/ppermute | solution.py:161
  1563.2 48.7 %collective-permute-done.28 = f32[256,3072]{1,0:T(8,128)} collective-permute-done((f32[256,3072]{1,0:T(8,128)}, f32[256,3072]{1,0:T(8,128)}, u32[]{:S(2)}, u32[]{:S(2)}) %collective-permute-start.28) | collective-permute-done | bytes 3145760 | tf_op jit(solution)/shard_map/ppermute | solution.py:161
  1614.7 63.4 %collective-permute-done.25 = f32[256,3072]{1,0:T(8,128)} collective-permute-done((f32[256,3072]{1,0:T(8,128)}, f32[256,3072]{1,0:T(8,128)}, u32[]{:S(2)}, u32[]{:S(2)}) %collective-permute-start.25) | collective-permute-done | bytes 3145760 | tf_op jit(solution)/shard_map/ppermute | solution.py:161
  (409 shorter events, 451.1 us)
Async XLA Ops:
  7.2 161.1 %all-gather.3.cloned.1.call-start = ((), (), s32[]{:S(2)}) async-start(), calls=%async_computation.2 | async-start | bytes 18874368 | tf_op jit(solution)/shard_map/all_gather | solution.py:164
  10.3 230.7 %all-gather.5.cloned.1.call-start = ((), (), s32[]{:S(2)}) async-start(), calls=%async_computation.3 | async-start | bytes 9437184 | tf_op jit(solution)/shard_map/all_gather | solution.py:164
  11.1 1681.6 %reduce-scatter.3.cloned.1.call-start = ((), (), s32[]{:S(2)}) async-start(), calls=%async_computation.4 | async-start | bytes 37748736 | tf_op jit(solution)/shard_map/reduce_scatter | solution.py:303
  28.8 226.6 %collective-permute-start.7 = (bf16[768,2048]{1,0:T(8,128)(2,1)}, bf16[768,2048]{1,0:T(8,128)(2,1)}, u32[]{:S(2)}, u32[]{:S(2)}) collective-permute-start(bf16[768,2048]{1,0:T(8,128)(2,1)} %param.27), channel_id=1, source_target_pairs={{0,4},{1,5},{2,6},{3,7},{4,0},{5,1},{6,2},{7,3}} | collective-permute-start | bytes 9437192 | tf_op jit(solution)/shard_map/ppermute | solution.py:161
  162.5 105.0 %collective-permute-start.3 = (bf16[1024,1536]{1,0:T(8,128)(2,1)}, bf16[1024,1536]{1,0:T(8,128)(2,1)}, u32[]{:S(2)}, u32[]{:S(2)}) collective-permute-start(bf16[1024,1536]{1,0:T(8,128)(2,1)} %pad_maximum_fusion.8), channel_id=1, source_target_pairs={{0,4},{1,5},{2,6},{3,7},{4,0},{5,1},{6,2},{7,3}} | collective-permute-start | bytes 9437192 | tf_op jit(solution)/shard_map/ppermute | solution.py:161
  167.7 166.7 %collective-permute-start.6 = (bf16[1024,1536]{1,0:T(8,128)(2,1)}, bf16[1024,1536]{1,0:T(8,128)(2,1)}, u32[]{:S(2)}, u32[]{:S(2)}) collective-permute-start(bf16[1024,1536]{1,0:T(8,128)(2,1)} %pad_maximum_fusion.9), channel_id=1, source_target_pairs={{0,4},{1,5},{2,6},{3,7},{4,0},{5,1},{6,2},{7,3}} | collective-permute-start | bytes 9437192 | tf_op jit(solution)/shard_map/ppermute | solution.py:161
  253.9 89.9 %collective-permute-start.9 = (bf16[768,2048]{1,0:T(8,128)(2,1)S(1)}, bf16[768,2048]{1,0:T(8,128)(2,1)}, u32[]{:S(2)}, u32[]{:S(2)}) collective-permute-start(bf16[768,2048]{1,0:T(8,128)(2,1)S(1)} %fusion.24), channel_id=1, source_target_pairs={{0,2},{1,3},{2,0},{3,1},{4,6},{5,7},{6,4},{7,5}} | collective-permute-start | bytes 9437192 | tf_op jit(solution)/shard_map/ppermute | solution.py:161
  255.4 88.4 %collective-permute-start = (bf16[768,2048]{1,0:T(8,128)(2,1)S(1)}, bf16[768,2048]{1,0:T(8,128)(2,1)}, u32[]{:S(2)}, u32[]{:S(2)}) collective-permute-start(bf16[768,2048]{1,0:T(8,128)(2,1)S(1)} %fusion.24), channel_id=1, source_target_pairs={{0,1},{1,0},{2,3},{3,2},{4,5},{5,4},{6,7},{7,6}} | collective-permute-start | bytes 9437192 | tf_op jit(solution)/shard_map/ppermute | solution.py:161
  337.6 70.8 %collective-permute-start.16 = (bf16[768,2048]{1,0:T(8,128)(2,1)}, bf16[768,2048]{1,0:T(8,128)(2,1)}, u32[]{:S(2)}, u32[]{:S(2)}) collective-permute-start(bf16[768,2048]{1,0:T(8,128)(2,1)} %bitcast.2), channel_id=1, source_target_pairs={{0,2},{1,3},{2,0},{3,1},{4,6},{5,7},{6,4},{7,5}} | collective-permute-start | bytes 9437192 | tf_op jit(solution)/shard_map/ppermute | solution.py:161
  343.8 78.3 %collective-permute-start.10 = (bf16[768,2048]{1,0:T(8,128)(2,1)}, bf16[768,2048]{1,0:T(8,128)(2,1)}, u32[]{:S(2)}, u32[]{:S(2)}) collective-permute-start(bf16[768,2048]{1,0:T(8,128)(2,1)} %collective-permute-done.9), channel_id=1, source_target_pairs={{0,1},{1,0},{2,3},{3,2},{4,5},{5,4},{6,7},{7,6}} | collective-permute-start | bytes 9437192 | tf_op jit(solution)/shard_map/ppermute | solution.py:161
  555.2 138.2 %collective-permute-start.19 = (f32[768,2048]{1,0:T(8,128)}, f32[768,2048]{1,0:T(8,128)}, u32[]{:S(2)}, u32[]{:S(2)}) collective-permute-start(f32[768,2048]{1,0:T(8,128)} %add_add_fusion.2), channel_id=1, source_target_pairs={{0,2},{1,3},{2,0},{3,1},{4,6},{5,7},{6,4},{7,5}} | collective-permute-start | bytes 18874376 | tf_op jit(solution)/shard_map/ppermute | solution.py:161
  810.5 887.0 %reduce-scatter.5.cloned.1.call-start = ((), (), s32[]{:S(2)}) async-start(), calls=%async_computation.5 | async-start | bytes 18874368 | tf_op jit(solution)/shard_map/reduce_scatter | solution.py:300
  822.0 731.4 %collective-permute-start.8 = (f32[768,2048]{1,0:T(8,128)}, f32[768,2048]{1,0:T(8,128)}, u32[]{:S(2)}, u32[]{:S(2)}) collective-permute-start(f32[768,2048]{1,0:T(8,128)} %fusion.80), channel_id=1, source_target_pairs={{0,1},{1,0},{2,3},{3,2},{4,5},{5,4},{6,7},{7,6}} | collective-permute-start | bytes 18874376 | tf_op jit(solution)/shard_map/ppermute | solution.py:161
  865.4 265.3 %collective-permute-start.26 = (f32[1024,1536]{1,0:T(8,128)S(1)}, f32[1024,1536]{1,0:T(8,128)}, u32[]{:S(2)}, u32[]{:S(2)}) collective-permute-start(f32[1024,1536]{1,0:T(8,128)S(1)} %convolution_add_fusion), channel_id=1, source_target_pairs={{0,4},{1,5},{2,6},{3,7},{4,0},{5,1},{6,2},{7,3}} | collective-permute-start | bytes 18874376 | tf_op jit(solution)/shard_map/ppermute | solution.py:161
  883.1 455.6 %collective-permute-start.23 = (f32[1024,1536]{1,0:T(8,128)}, f32[1024,1536]{1,0:T(8,128)}, u32[]{:S(2)}, u32[]{:S(2)}) collective-permute-start(f32[1024,1536]{1,0:T(8,128)} %convolution_add_fusion.1), channel_id=1, source_target_pairs={{0,4},{1,5},{2,6},{3,7},{4,0},{5,1},{6,2},{7,3}} | collective-permute-start | bytes 18874376 | tf_op jit(solution)/shard_map/ppermute | solution.py:161
  896.0 577.1 %collective-permute-start.29 = (f32[768,2048]{1,0:T(8,128)}, f32[768,2048]{1,0:T(8,128)}, u32[]{:S(2)}, u32[]{:S(2)}) collective-permute-start(f32[768,2048]{1,0:T(8,128)} %convolution_add_fusion.3), channel_id=1, source_target_pairs={{0,4},{1,5},{2,6},{3,7},{4,0},{5,1},{6,2},{7,3}} | collective-permute-start | bytes 18874376 | tf_op jit(solution)/shard_map/ppermute | solution.py:161
  903.0 454.9 %collective-permute-start.11 = (f32[768,2048]{1,0:T(8,128)}, f32[768,2048]{1,0:T(8,128)}, u32[]{:S(2)}, u32[]{:S(2)}) collective-permute-start(f32[768,2048]{1,0:T(8,128)} %fusion.76), channel_id=1, source_target_pairs={{0,1},{1,0},{2,3},{3,2},{4,5},{5,4},{6,7},{7,6}} | collective-permute-start | bytes 18874376 | tf_op jit(solution)/shard_map/ppermute | solution.py:161
  1147.0 338.8 %collective-permute-start.27 = (f32[512,1536]{1,0:T(8,128)}, f32[512,1536]{1,0:T(8,128)}, u32[]{:S(2)}, u32[]{:S(2)}) collective-permute-start(f32[512,1536]{1,0:T(8,128)} %fusion.54), channel_id=1, source_target_pairs={{0,1},{1,0},{2,3},{3,2},{4,5},{5,4},{6,7},{7,6}} | collective-permute-start | bytes 9437192 | tf_op jit(solution)/shard_map/ppermute | solution.py:161
  1357.9 136.5 %collective-permute-start.24 = (f32[512,1536]{1,0:T(8,128)}, f32[512,1536]{1,0:T(8,128)}, u32[]{:S(2)}, u32[]{:S(2)}) collective-permute-start(f32[512,1536]{1,0:T(8,128)} %fusion.56), channel_id=1, source_target_pairs={{0,1},{1,0},{2,3},{3,2},{4,5},{5,4},{6,7},{7,6}} | collective-permute-start | bytes 9437192 | tf_op jit(solution)/shard_map/ppermute | solution.py:161
  1367.3 155.6 %collective-permute-start.12 = (f32[384,2048]{1,0:T(8,128)}, f32[384,2048]{1,0:T(8,128)}, u32[]{:S(2)}, u32[]{:S(2)}) collective-permute-start(f32[384,2048]{1,0:T(8,128)} %get-tuple-element.80), channel_id=1, source_target_pairs={{0,2},{1,3},{2,0},{3,1},{4,6},{5,7},{6,4},{7,5}} | collective-permute-start | bytes 9437192 | tf_op jit(solution)/shard_map/ppermute | solution.py:161
  1473.2 71.3 %collective-permute-start.13 = (f32[384,2048]{1,0:T(8,128)}, f32[384,2048]{1,0:T(8,128)}, u32[]{:S(2)}, u32[]{:S(2)}) collective-permute-start(f32[384,2048]{1,0:T(8,128)} %get-tuple-element.79), channel_id=1, source_target_pairs={{0,2},{1,3},{2,0},{3,1},{4,6},{5,7},{6,4},{7,5}} | collective-permute-start | bytes 9437192 | tf_op jit(solution)/shard_map/ppermute | solution.py:161
  1493.4 118.4 %collective-permute-start.28 = (f32[256,3072]{1,0:T(8,128)}, f32[256,3072]{1,0:T(8,128)}, u32[]{:S(2)}, u32[]{:S(2)}) collective-permute-start(f32[256,3072]{1,0:T(8,128)} %broadcast_select_fusion.12), channel_id=1, source_target_pairs={{0,2},{1,3},{2,0},{3,1},{4,6},{5,7},{6,4},{7,5}} | collective-permute-start | bytes 9437192 | tf_op jit(solution)/shard_map/ppermute | solution.py:161
  1500.5 177.5 %collective-permute-start.25 = (f32[256,3072]{1,0:T(8,128)}, f32[256,3072]{1,0:T(8,128)}, u32[]{:S(2)}, u32[]{:S(2)}) collective-permute-start(f32[256,3072]{1,0:T(8,128)} %broadcast_select_fusion.16), channel_id=1, source_target_pairs={{0,2},{1,3},{2,0},{3,1},{4,6},{5,7},{6,4},{7,5}} | collective-permute-start | bytes 9437192 | tf_op jit(solution)/shard_map/ppermute | solution.py:161
  1523.0 161.0 %collective-permute-start.20 = (f32[4352]{0:T(1024)S(1)}, f32[4352]{0:T(1024)S(1)}, u32[]{:S(2)}, u32[]{:S(2)}) collective-permute-start(f32[4352]{0:T(1024)S(1)} %maximum_multiply_fusion), channel_id=1, source_target_pairs={{0,1},{1,0},{2,3},{3,2},{4,5},{5,4},{6,7},{7,6}} | collective-permute-start | bytes 52232 | tf_op jit(solution)/shard_map/ppermute | solution.py:161
  (121 other events, 3442.7 us)
Sparse Core Ops, SparseCore 0:
  10.5 146.1 all-gather.2
  158.5 82.5 all-gather.4
  810.6 333.1 reduce-scatter.2
  1147.7 175.4 reduce-scatter.4

commit v5 on v4

--- a/solution.py
+++ b/solution.py
@@ -181,7 +181,7 @@
             first = jnp.concatenate([blk[0], blk[1], blk[4], blk[5]], axis=1)
             second = jnp.concatenate([blk[2], blk[3], blk[6], blk[7]], axis=1)
             keep, send = pick(x_bit, first, second)
-            first = got = swap(send, XDIR)
+            got = swap(send, XDIR)
             row0, row1 = pick(x_bit, keep, got)
             both = jnp.concatenate([row0, row1], axis=0)
             col = [both[:, j * ff_block:(j + 1) * ff_block] for j in range(4)]
@@ -190,7 +190,7 @@
             core0, core1 = pick(c_bit, keep, got)
             four = jnp.concatenate([core0[:rows], core1[:rows], core0[rows:], core1[rows:]], axis=0)
             got = swap(four, YDIR)
-            return jnp.concatenate(pick(y_bit, four, got), axis=0), first
+            return jnp.concatenate(pick(y_bit, four, got), axis=0)
 
         def far_sum(add_rows):
             part = add_rows(None, 1, tokens, 2 * tokens)
@@ -226,13 +226,12 @@
 
         gains = lax.all_gather(jnp.stack([norm1_gain, norm2_gain]), axis_name, axis=1, tiled=True)
         full_qkv, full_o = gather_rows(jnp.concatenate([w_q, w_k, w_v], axis=1)), gather_rows(w_o)
-        gate_own, down_own, gains = lax.optimization_barrier((w_gate, w_down, gains))
+        gate_own, gains = lax.optimization_barrier((w_gate, gains))
         gain1, gain2 = gains[0].astype(jnp.float32), gains[1].astype(jnp.float32)
         dy_flat = grad_out.reshape(tokens, width)
-        dy_own, full_qkv = lax.optimization_barrier((dy_flat, full_qkv))
-        gate_q, gate_first = quarter_columns(gate_own)
-        up_own, _ = lax.optimization_barrier((w_up, gate_first))
-        up_q, _ = quarter_columns(up_own)
+        up_own, down_own, dy_own, full_qkv = lax.optimization_barrier((w_up, w_down, dy_flat, full_qkv))
+        gate_q = quarter_columns(gate_own)
+        up_q = quarter_columns(up_own)
         down_q = jnp.concatenate(pick(y_bit, down_own, swap(down_own, YDIR)), axis=0)
         dy_row = row_tokens(dy_own)
 
@@ -295,11 +294,18 @@
         out_xa, out_xb, _ = lax.optimization_barrier((out_xa, out_xb, d_attn_ctx))
         down_proj = (down_total + jnp.concatenate([out_xa, out_xb], axis=0)).astype(jnp.bfloat16)
         layer_out = (resid_float + down_proj.astype(jnp.float32)).astype(jnp.bfloat16).reshape(hidden.shape)
-        wo_part = matmul_tn(attn_ctx, d_resid_bf) * inv_tokens
-        wo_part, d_attn_ctx = lax.optimization_barrier((wo_part, d_attn_ctx))
-        grad_wo = lax.psum_scatter(wo_part, axis_name, scatter_dimension=0, tiled=True)
         d_qkv, grad_qgain, grad_kgain = attention_backward(d_attn_ctx, qkv, tables, heads, kv_heads, seq_len)
         qkv_part = matmul_tn(normed, d_qkv) * inv_tokens
+        d_resid_late, _ = lax.optimization_barrier((d_resid_bf, qkv_part))
+        blk = [attn_ctx[:, j * rows:(j + 1) * rows] for j in range(8)]
+        keep, send = pick(c_bit, jnp.concatenate(blk[0::2], axis=1), jnp.concatenate(blk[1::2], axis=1))
+        part = matmul_tn(send, d_resid_late)
+        part = swap(part, CORE)
+        part = part + matmul_tn(keep, d_resid_late)
+        keep, send = pick(y_bit, part[:2 * rows], part[2 * rows:])
+        part = keep + swap(send, YDIR)
+        keep, send = pick(x_bit, part[:rows], part[rows:])
+        grad_wo = (keep + swap(send, XDIR)) * inv_tokens
         grad_qkv = lax.psum_scatter(qkv_part, axis_name, scatter_dimension=0, tiled=True)
         grad_wq, grad_wk, grad_wv = jnp.split(grad_qkv, (w_q.shape[1], w_q.shape[1] + w_k.shape[1]), axis=1)
         d_normed = matmul_nt(d_qkv, full_qkv)

time: 1710 us -> 1760 us (1.029)
  other arithmetic: 101 us -> 125 us
    all_gather x2, waiting for transfers between devices: 15.5 us -> 38.7 us  [gather_rows(): return lax.all_gather(row_shard, axis_name, axis=0, tiled=True)]
    ppermute x30 -> x33, waiting for transfers between devices: 971 us -> 958 us  [swap(): lax.ppermute(value, axis_name, [(j, j ^ mask) for j in range(group_size)])]
    dot_general x14 -> x15, matrix products: 135 us -> 142 us  [matmul_tn(): lax.dot_general(left_op, right_op, (((0,), (0,)), ((), ())), preferred_el...]
    unnamed x241 -> x299, local copies, waits for them, and re-layouts: 38.8 us -> 42.5 us
  transfers between devices with their start and end apart: 34 -> 36, of which waited for: 15 -> 14; matrix products, arithmetic and copies ran while one was open for 26% -> 28% of each run, Pallas kernels for 2% -> 2%
where the time goes in v5:
time: 1760 us
  waiting for transfers between devices  997 us (57%)
  matrix products  428 us (24%)
  other arithmetic  125 us (7%)
  Pallas kernels  93 us (5%)
  local copies, waits for them, and re-layouts  63.8 us (4%)
  starting transfers between devices  21 us (1%)
    ppermute x33, waiting for transfers between devices, swap(): lax.ppermute(value, axis_name, [(j, j ^ mask) for j in range(group_size)])  958 us
    dot_general x12, matrix products, matmul_nt(): lax.dot_general(left_op, right_op, (((1,), (1,)), ((), ())), preferred_el...  163 us
    dot_general x15, matrix products, matmul_tn(): lax.dot_general(left_op, right_op, (((0,), (0,)), ((), ())), preferred_el...  142 us
    dot_general x10, matrix products, matmul(): return jnp.dot(left_op, right_op, preferred_element_type=jnp.float32)  124 us
    pallas_call x1, Pallas kernels, attention_backward(): pl.pallas_call(attention_backward_kernel, grid=grid, in_specs=[q_spec] +...  55 us
    unnamed x299, local copies, waits for them, and re-layouts  42.5 us
    all_gather x2, waiting for transfers between devices, gather_rows(): return lax.all_gather(row_shard, axis_name, axis=0, tiled=True)  38.7 us
    pallas_call x1, Pallas kernels, attention_forward(): pl.pallas_call(attention_forward_kernel, grid=grid, in_specs=in_specs, ou...  38.1 us
  transfers between devices with their start and end apart: 36, of which 14 were waited for; matrix products, arithmetic and copies ran while one was open for 28% of the time, Pallas kernels for 2%

profile of v5, /device:TPU:0, one launch (start us, length us, event | category | flops | bytes accessed | tf_op | source)
XLA Modules:
  0.0 1756.6 jit_solution(4020693412303636609)
XLA Ops:
  28.2 63.5 %collective-permute-done.1 = bf16[256,3072]{1,0:T(8,128)(2,1)} collective-permute-done((bf16[256,3072]{1,0:T(8,128)(2,1)}, bf16[256,3072]{1,0:T(8,128)(2,1)}, u32[]{:S(2)}, u32[]{:S(2)}) %collective-permute-start.1) | collective-permute-done | bytes 1572896 | tf_op jit(solution)/shard_map/ppermute | solution.py:161
  108.1 17.2 all-gather.3.cloned.1.call-done
  131.1 19.1 %convolution_convert_fusion.4.q_ref.k_ref.v_ref = bf16[768,4096]{1,0:T(8,128)(2,1)} fusion(bf16[768,2048]{1,0:T(8,128)(2,1)S(1)} %copy-done.62, bf16[2048,4096]{1,0:T(8,128)(2,1)} %all-gather.3.cloned.1.call-done), kind=kOutput, calls=%fused_computation.49 | convolution fusion | flops 12888047616 | bytes 26214400 | tf_op jit(solution)/shard_map/dot_general | solution.py:23
  150.2 38.1 %attn_fwd.1 = bf16[768,2048]{1,0:T(8,128)(2,1)} custom-call(bf16[768,4096]{1,0:T(8,128)(2,1)} %convolution_convert_fusion.4.q_ref.k_ref.v_ref, bf16[768,4096]{1,0:T(8,128)(2,1)} %convolution_convert_fusion.4.q_ref.k_ref.v_ref, bf16[768,4096]{1,0:T(8,128)(2,1)} %convolution_convert_fusion.4.q_ref.k_ref.v_ref, f32[768,128]{1,0:T(8,128)} %get-tuple-element.141.cos_ref, ...), custom_call_target="tpu_custom_call" | custom-call | flops 1610612736 | bytes 9437184 | tf_op jit(solution)/shard_map/attn_fwd/pallas_call | solution.py:123
  188.2 21.5 %all-gather.5.cloned.1.call-done = bf16[2048,2048]{1,0:T(8,128)(2,1)} async-done(((bf16[256,2048]{1,0:T(8,128)(2,1)}), bf16[2048,2048]{1,0:T(8,128)(2,1)}) %all-gather.5.cloned.1.call-update) | async-done | bytes 8388624 | tf_op jit(solution)/shard_map/all_gather | solution.py:164
  241.6 58.4 %collective-permute-done.9 = bf16[768,2048]{1,0:T(8,128)(2,1)} collective-permute-done((bf16[768,2048]{1,0:T(8,128)(2,1)}, bf16[768,2048]{1,0:T(8,128)(2,1)}, u32[]{:S(2)}, u32[]{:S(2)}) %collective-permute-start.9) | collective-permute-done | bytes 3145760 | tf_op jit(solution)/shard_map/ppermute | solution.py:161
  302.4 64.3 %collective-permute-done.16 = bf16[768,2048]{1,0:T(8,128)(2,1)} collective-permute-done((bf16[768,2048]{1,0:T(8,128)(2,1)S(1)}, bf16[768,2048]{1,0:T(8,128)(2,1)}, u32[]{:S(2)}, u32[]{:S(2)}) %collective-permute-start.16) | collective-permute-done | bytes 3145760 | tf_op jit(solution)/shard_map/ppermute | solution.py:161
  371.2 15.5 convolution_convert_fusion.3
  414.1 15.8 convolution_convert_fusion.2
  429.9 22.8 %fusion.7 = (bf16[1536,1536]{1,0:T(8,128)(2,1)}, bf16[1536,1536]{1,0:T(8,128)(2,1)}, bf16[1536,1536]{1,0:T(8,128)(2,1)}) fusion(bf16[1536,1536]{1,0:T(8,128)(2,1)} %convolution_convert_fusion.2, bf16[1536,1536]{1,0:T(8,128)(2,1)} %convolution_convert_fusion.3, bf16[1536,2048]{1,0:T(8,128)(2,1)} %constant_dynamic-update-slice_fusion.2, ...), kind=kOutput, calls=%fused_computation.23 | convolution fusion | flops 9718726656 | bytes 36175872 | tf_op jit(solution)/shard_map/dot_general | solution.py:31
  461.8 17.5 fusion.8
  489.9 20.4 %fusion.11 = (bf16[1536,1536]{1,0:T(8,128)(2,1)}, bf16[1536,1536]{1,0:T(8,128)(2,1)}) fusion(bf16[1536,1536]{1,0:T(8,128)(2,1)} %get-tuple-element.139, bf16[1536,1536]{1,0:T(8,128)(2,1)} %convolution_convert_fusion.1, bf16[1536,2048]{1,0:T(8,128)(2,1)S(1)} %constant_dynamic-update-slice_fusion.4, bf16[768,2048]{1,0:T(8,128)(2,1)} %get-tuple-element.80, ...), kind=kOutput, calls=%fused_computation.27 | convolution fusion | flops 9711648768 | bytes 31457280 | tf_op jit(solution)/shard_map/dot_general | solution.py:31
  599.4 115.8 %collective-permute-done.19 = f32[768,2048]{1,0:T(8,128)} collective-permute-done((f32[768,2048]{1,0:T(8,128)}, f32[768,2048]{1,0:T(8,128)}, u32[]{:S(2)}, u32[]{:S(2)}) %collective-permute-start.19) | collective-permute-done | bytes 6291488 | tf_op jit(solution)/shard_map/ppermute | solution.py:161
  739.4 55.0 %attn_bwd.1 = (bf16[768,2048]{1,0:T(8,128)(2,1)}, bf16[768,1024]{1,0:T(8,128)(2,1)}, bf16[768,1024]{1,0:T(8,128)(2,1)}, f32[192,128]{1,0:T(8,128)}, f32[192,128]{1,0:T(8,128)}) custom-call(bf16[768,2048]{1,0:T(8,128)(2,1)} %convolution_convert_fusion.5.d_ref, bf16[768,4096]{1,0:T(8,128)(2,1)} %convolution_convert_fusion.4.q_ref.k_ref.v_ref, ...), custom_call_target="tpu_custom_call" | custom-call | flops 4026531840 | bytes 18874368 | tf_op jit(solution)/shard_map/attn_bwd/pallas_call | solution.py:138
  800.9 17.5 convolution_multiply_fusion
  929.9 163.4 %collective-permute-done.29 = f32[1024,1536]{1,0:T(8,128)} collective-permute-done((f32[1024,1536]{1,0:T(8,128)S(1)}, f32[1024,1536]{1,0:T(8,128)}, u32[]{:S(2)}, u32[]{:S(2)}) %collective-permute-start.29) | collective-permute-done | bytes 6291488 | tf_op jit(solution)/shard_map/ppermute | solution.py:161
  1105.2 150.9 %collective-permute-done.26 = f32[1024,1536]{1,0:T(8,128)} collective-permute-done((f32[1024,1536]{1,0:T(8,128)}, f32[1024,1536]{1,0:T(8,128)}, u32[]{:S(2)}, u32[]{:S(2)}) %collective-permute-start.26) | collective-permute-done | bytes 6291488 | tf_op jit(solution)/shard_map/ppermute | solution.py:161
  1280.3 108.0 %collective-permute-done.32 = f32[768,2048]{1,0:T(8,128)} collective-permute-done((f32[768,2048]{1,0:T(8,128)}, f32[768,2048]{1,0:T(8,128)}, u32[]{:S(2)}, u32[]{:S(2)}) %collective-permute-start.32) | collective-permute-done | bytes 6291488 | tf_op jit(solution)/shard_map/ppermute | solution.py:161
  1426.7 22.2 %fusion.43 = (f32[2048]{0:T(1024)}, f32[768]{0:T(1024)}, f32[768,2048]{1,0:T(8,128)}) fusion(bf16[3,256,2048]{2,1,0:T(8,128)(2,1)} %param.14, f32[768]{0:T(1024)S(1)} %copy-done.113, f32[2048]{0:T(1024)S(1)} %bitcast.92, bf16[768,4096]{1,0:T(8,128)(2,1)} %copy-done.84, bf16[2048,4096]{1,0:T(8,128)(2,1)} %all-gather.3.cloned.1.call-done), kind=kOutput, calls=%fused_computation.80 | convolution fusion | flops 12895908864 | bytes 32528384 | tf_op jit(solution)/shard_map/dot_general | solution.py:31
  1460.4 19.0 %fusion.42 = (bf16[768,2048]{1,0:T(8,128)(2,1)}, bf16[768,2048]{1,0:T(8,128)(2,1)}) fusion(bf16[3,256,2048]{2,1,0:T(8,128)(2,1)} %param.14, f32[768,2048]{1,0:T(8,128)} %get-tuple-element.140, f32[768]{0:T(1024)S(1)} %broadcast_multiply_fusion.2, f32[2048]{0:T(1024)} %bitcast.91, f32[768]{0:T(1024)} %copy-done.112, f32[768]{0:T(1024)S(1)} %copy-done.111, ...), kind=kLoop, calls=%fused_computation.79 | loop fusion | flops 36175872 | bytes 47214592 | tf_op jit(solution)/shard_map/convert_element_type | solution.py:313
  1479.4 47.7 %collective-permute-done.31 = f32[256,3072]{1,0:T(8,128)} collective-permute-done((f32[256,3072]{1,0:T(8,128)}, f32[256,3072]{1,0:T(8,128)}, u32[]{:S(2)}, u32[]{:S(2)}) %collective-permute-start.31) | collective-permute-done | bytes 3145760 | tf_op jit(solution)/shard_map/ppermute | solution.py:161
  1529.9 61.6 %collective-permute-done.28 = f32[256,3072]{1,0:T(8,128)} collective-permute-done((f32[256,3072]{1,0:T(8,128)}, f32[256,3072]{1,0:T(8,128)}, u32[]{:S(2)}, u32[]{:S(2)}) %collective-permute-start.28) | collective-permute-done | bytes 3145760 | tf_op jit(solution)/shard_map/ppermute | solution.py:161
  1612.8 82.3 %collective-permute-done.24 = f32[512,2048]{1,0:T(8,128)} collective-permute-done((f32[512,2048]{1,0:T(8,128)}, f32[512,2048]{1,0:T(8,128)}, u32[]{:S(2)}, u32[]{:S(2)}) %collective-permute-start.24) | collective-permute-done | bytes 4194336 | tf_op jit(solution)/shard_map/ppermute | solution.py:161
  1707.8 35.2 %collective-permute-done.25 = f32[256,2048]{1,0:T(8,128)S(1)} collective-permute-done((f32[256,2048]{1,0:T(8,128)S(1)}, f32[256,2048]{1,0:T(8,128)S(1)}, u32[]{:S(2)}, u32[]{:S(2)}) %collective-permute-start.25) | collective-permute-done | bytes 2097184 | tf_op jit(solution)/shard_map/ppermute | solution.py:161
  (476 shorter events, 488.1 us)
Async XLA Ops:
  7.2 118.1 %all-gather.3.cloned.1.call-start = ((), (), s32[]{:S(2)}) async-start(), calls=%async_computation.1 | async-start | bytes 18874368 | tf_op jit(solution)/shard_map/all_gather | solution.py:164
  10.5 199.3 %all-gather.5.cloned.1.call-start = ((), (), s32[]{:S(2)}) async-start(), calls=%async_computation.2 | async-start | bytes 9437184 | tf_op jit(solution)/shard_map/all_gather | solution.py:164
  11.3 1733.7 %reduce-scatter.2.cloned.1.call-start = ((), (), s32[]{:S(2)}) async-start(), calls=%async_computation.3 | async-start | bytes 37748736 | tf_op jit(solution)/shard_map/reduce_scatter | solution.py:309
  106.8 123.9 %collective-permute-start.3 = (bf16[1024,1536]{1,0:T(8,128)(2,1)}, bf16[1024,1536]{1,0:T(8,128)(2,1)}, u32[]{:S(2)}, u32[]{:S(2)}) collective-permute-start(bf16[1024,1536]{1,0:T(8,128)(2,1)} %pad_maximum_fusion.8), channel_id=1, source_target_pairs={{0,4},{1,5},{2,6},{3,7},{4,0},{5,1},{6,2},{7,3}} | collective-permute-start | bytes 9437192 | tf_op jit(solution)/shard_map/ppermute | solution.py:161
  230.1 136.5 %collective-permute-start.16 = (bf16[768,2048]{1,0:T(8,128)(2,1)S(1)}, bf16[768,2048]{1,0:T(8,128)(2,1)}, u32[]{:S(2)}, u32[]{:S(2)}) collective-permute-start(bf16[768,2048]{1,0:T(8,128)(2,1)S(1)} %bitcast.71), channel_id=1, source_target_pairs={{0,2},{1,3},{2,0},{3,1},{4,6},{5,7},{6,4},{7,5}} | collective-permute-start | bytes 9437192 | tf_op jit(solution)/shard_map/ppermute | solution.py:161
  230.7 139.9 %collective-permute-start = (bf16[768,2048]{1,0:T(8,128)(2,1)}, bf16[768,2048]{1,0:T(8,128)(2,1)}, u32[]{:S(2)}, u32[]{:S(2)}) collective-permute-start(bf16[768,2048]{1,0:T(8,128)(2,1)} %fusion.24), channel_id=1, source_target_pairs={{0,1},{1,0},{2,3},{3,2},{4,5},{5,4},{6,7},{7,6}} | collective-permute-start | bytes 9437192 | tf_op jit(solution)/shard_map/ppermute | solution.py:161
  236.3 150.4 %collective-permute-start.14 = (bf16[768,2048]{1,0:T(8,128)(2,1)S(1)}, bf16[768,2048]{1,0:T(8,128)(2,1)}, u32[]{:S(2)}, u32[]{:S(2)}) collective-permute-start(bf16[768,2048]{1,0:T(8,128)(2,1)S(1)} %bitcast.72), channel_id=1, source_target_pairs={{0,1},{1,0},{2,3},{3,2},{4,5},{5,4},{6,7},{7,6}} | collective-permute-start | bytes 9437192 | tf_op jit(solution)/shard_map/ppermute | solution.py:161
  238.7 152.0 %collective-permute-start.7 = (bf16[768,2048]{1,0:T(8,128)(2,1)}, bf16[768,2048]{1,0:T(8,128)(2,1)}, u32[]{:S(2)}, u32[]{:S(2)}) collective-permute-start(bf16[768,2048]{1,0:T(8,128)(2,1)} %param.27), channel_id=1, source_target_pairs={{0,4},{1,5},{2,6},{3,7},{4,0},{5,1},{6,2},{7,3}} | collective-permute-start | bytes 9437192 | tf_op jit(solution)/shard_map/ppermute | solution.py:161
  300.0 111.4 %collective-permute-start.6 = (bf16[1024,1536]{1,0:T(8,128)(2,1)S(1)}, bf16[1024,1536]{1,0:T(8,128)(2,1)}, u32[]{:S(2)}, u32[]{:S(2)}) collective-permute-start(bf16[1024,1536]{1,0:T(8,128)(2,1)S(1)} %pad_maximum_fusion.9), channel_id=1, source_target_pairs={{0,4},{1,5},{2,6},{3,7},{4,0},{5,1},{6,2},{7,3}} | collective-permute-start | bytes 9437192 | tf_op jit(solution)/shard_map/ppermute | solution.py:161
  370.7 108.6 %collective-permute-start.17 = (bf16[768,2048]{1,0:T(8,128)(2,1)}, bf16[768,2048]{1,0:T(8,128)(2,1)}, u32[]{:S(2)}, u32[]{:S(2)}) collective-permute-start(bf16[768,2048]{1,0:T(8,128)(2,1)} %collective-permute-done.16), channel_id=1, source_target_pairs={{0,1},{1,0},{2,3},{3,2},{4,5},{5,4},{6,7},{7,6}} | collective-permute-start | bytes 9437192 | tf_op jit(solution)/shard_map/ppermute | solution.py:161
  577.4 137.8 %collective-permute-start.19 = (f32[768,2048]{1,0:T(8,128)}, f32[768,2048]{1,0:T(8,128)}, u32[]{:S(2)}, u32[]{:S(2)}) collective-permute-start(f32[768,2048]{1,0:T(8,128)} %add_add_fusion.2), channel_id=1, source_target_pairs={{0,2},{1,3},{2,0},{3,1},{4,6},{5,7},{6,4},{7,5}} | collective-permute-start | bytes 18874376 | tf_op jit(solution)/shard_map/ppermute | solution.py:161
  847.9 245.4 %collective-permute-start.29 = (f32[1024,1536]{1,0:T(8,128)S(1)}, f32[1024,1536]{1,0:T(8,128)}, u32[]{:S(2)}, u32[]{:S(2)}) collective-permute-start(f32[1024,1536]{1,0:T(8,128)S(1)} %convolution_add_fusion), channel_id=1, source_target_pairs={{0,4},{1,5},{2,6},{3,7},{4,0},{5,1},{6,2},{7,3}} | collective-permute-start | bytes 18874376 | tf_op jit(solution)/shard_map/ppermute | solution.py:161
  883.6 372.5 %collective-permute-start.26 = (f32[1024,1536]{1,0:T(8,128)}, f32[1024,1536]{1,0:T(8,128)}, u32[]{:S(2)}, u32[]{:S(2)}) collective-permute-start(f32[1024,1536]{1,0:T(8,128)} %convolution_add_fusion.1), channel_id=1, source_target_pairs={{0,4},{1,5},{2,6},{3,7},{4,0},{5,1},{6,2},{7,3}} | collective-permute-start | bytes 18874376 | tf_op jit(solution)/shard_map/ppermute | solution.py:161
  883.9 504.5 %collective-permute-start.32 = (f32[768,2048]{1,0:T(8,128)}, f32[768,2048]{1,0:T(8,128)}, u32[]{:S(2)}, u32[]{:S(2)}) collective-permute-start(f32[768,2048]{1,0:T(8,128)} %convolution_add_fusion.4), channel_id=1, source_target_pairs={{0,4},{1,5},{2,6},{3,7},{4,0},{5,1},{6,2},{7,3}} | collective-permute-start | bytes 18874376 | tf_op jit(solution)/shard_map/ppermute | solution.py:161
  885.7 383.9 %collective-permute-start.11 = (f32[768,2048]{1,0:T(8,128)}, f32[768,2048]{1,0:T(8,128)}, u32[]{:S(2)}, u32[]{:S(2)}) collective-permute-start(f32[768,2048]{1,0:T(8,128)} %fusion.76), channel_id=1, source_target_pairs={{0,1},{1,0},{2,3},{3,2},{4,5},{5,4},{6,7},{7,6}} | collective-permute-start | bytes 18874376 | tf_op jit(solution)/shard_map/ppermute | solution.py:161
  929.4 531.0 %collective-permute-start.8 = (f32[768,2048]{1,0:T(8,128)}, f32[768,2048]{1,0:T(8,128)}, u32[]{:S(2)}, u32[]{:S(2)}) collective-permute-start(f32[768,2048]{1,0:T(8,128)} %fusion.80), channel_id=1, source_target_pairs={{0,1},{1,0},{2,3},{3,2},{4,5},{5,4},{6,7},{7,6}} | collective-permute-start | bytes 18874376 | tf_op jit(solution)/shard_map/ppermute | solution.py:161
  1105.2 296.4 %collective-permute-start.30 = (f32[512,1536]{1,0:T(8,128)}, f32[512,1536]{1,0:T(8,128)}, u32[]{:S(2)}, u32[]{:S(2)}) collective-permute-start(f32[512,1536]{1,0:T(8,128)} %fusion.54), channel_id=1, source_target_pairs={{0,1},{1,0},{2,3},{3,2},{4,5},{5,4},{6,7},{7,6}} | collective-permute-start | bytes 9437192 | tf_op jit(solution)/shard_map/ppermute | solution.py:161
  1269.6 140.0 %collective-permute-start.27 = (f32[512,1536]{1,0:T(8,128)}, f32[512,1536]{1,0:T(8,128)}, u32[]{:S(2)}, u32[]{:S(2)}) collective-permute-start(f32[512,1536]{1,0:T(8,128)} %fusion.56), channel_id=1, source_target_pairs={{0,1},{1,0},{2,3},{3,2},{4,5},{5,4},{6,7},{7,6}} | collective-permute-start | bytes 9437192 | tf_op jit(solution)/shard_map/ppermute | solution.py:161
  1279.1 173.4 %collective-permute-start.12 = (f32[384,2048]{1,0:T(8,128)}, f32[384,2048]{1,0:T(8,128)}, u32[]{:S(2)}, u32[]{:S(2)}) collective-permute-start(f32[384,2048]{1,0:T(8,128)} %get-tuple-element.78), channel_id=1, source_target_pairs={{0,2},{1,3},{2,0},{3,1},{4,6},{5,7},{6,4},{7,5}} | collective-permute-start | bytes 9437192 | tf_op jit(solution)/shard_map/ppermute | solution.py:161
  1409.2 117.8 %collective-permute-start.31 = (f32[256,3072]{1,0:T(8,128)}, f32[256,3072]{1,0:T(8,128)}, u32[]{:S(2)}, u32[]{:S(2)}) collective-permute-start(f32[256,3072]{1,0:T(8,128)} %broadcast_select_fusion.12), channel_id=1, source_target_pairs={{0,2},{1,3},{2,0},{3,1},{4,6},{5,7},{6,4},{7,5}} | collective-permute-start | bytes 9437192 | tf_op jit(solution)/shard_map/ppermute | solution.py:161
  1426.6 167.3 %collective-permute-start.23 = (f32[1024,2048]{1,0:T(8,128)}, f32[1024,2048]{1,0:T(8,128)}, u32[]{:S(2)}, u32[]{:S(2)}) collective-permute-start(f32[1024,2048]{1,0:T(8,128)} %fusion.105), channel_id=1, source_target_pairs={{0,1},{1,0},{2,3},{3,2},{4,5},{5,4},{6,7},{7,6}} | collective-permute-start | bytes 25165832 | tf_op jit(solution)/shard_map/ppermute | solution.py:161
  1452.5 139.0 %collective-permute-start.28 = (f32[256,3072]{1,0:T(8,128)}, f32[256,3072]{1,0:T(8,128)}, u32[]{:S(2)}, u32[]{:S(2)}) collective-permute-start(f32[256,3072]{1,0:T(8,128)} %broadcast_select_fusion.16), channel_id=1, source_target_pairs={{0,2},{1,3},{2,0},{3,1},{4,6},{5,7},{6,4},{7,5}} | collective-permute-start | bytes 9437192 | tf_op jit(solution)/shard_map/ppermute | solution.py:161
  1459.6 150.5 %collective-permute-start.20 = (f32[4352]{0:T(1024)S(1)}, f32[4352]{0:T(1024)S(1)}, u32[]{:S(2)}, u32[]{:S(2)}) collective-permute-start(f32[4352]{0:T(1024)S(1)} %maximum_multiply_fusion), channel_id=1, source_target_pairs={{0,1},{1,0},{2,3},{3,2},{4,5},{5,4},{6,7},{7,6}} | collective-permute-start | bytes 52232 | tf_op jit(solution)/shard_map/ppermute | solution.py:161
  1610.2 91.4 %collective-permute-start.21 = (f32[4352]{0:T(1024)S(1)}, f32[4352]{0:T(1024)S(1)}, u32[]{:S(2)}, u32[]{:S(2)}) collective-permute-start(f32[4352]{0:T(1024)S(1)} %fusion.124), channel_id=1, source_target_pairs={{0,2},{1,3},{2,0},{3,1},{4,6},{5,7},{6,4},{7,5}} | collective-permute-start | bytes 52232 | tf_op jit(solution)/shard_map/ppermute | solution.py:161
  (152 other events, 4279.8 us)
Sparse Core Ops, SparseCore 0:
  10.6 114.6 all-gather.2
  127.1 82.6 all-gather.4
  818.5 332.1 reduce-scatter.1
